TPU v7x, 32 devices: a whole 2x2x4 slice. The times are simulated.
32 devices in a mesh: dp: 8 (over y, x, core), tensor: 4 (over z).
Axes of the slice: x: 2, y: 2, z: 4, core: 2. Of those that a mesh axis runs over, the one named last changes fastest.
Arguments:
- hidden_in: bfloat16 [4096, 2048], P(('dp', 'tensor')), may hold values from -6 to 6
- segments: int32 [8, 512], P('dp'), may hold values from 0 to 5, never falling along the last dimension, each value on 1 to 256 neighbouring positions
- routes: int32 [4096, 8], P(('dp', 'tensor')), may hold values from 0 to 31, all different within a row; in each aligned block of 128 rows (0 to 127, 128 to 255, ...) at most 64 rows name the same one
- query_weight: bfloat16 [2048, 4096], P('dp', 'tensor'), may hold values from -0.125 to 0.125
- key_weight: bfloat16 [2048, 512], P('dp', 'tensor'), may hold values from -0.125 to 0.125
- value_weight: bfloat16 [2048, 512], P('dp', 'tensor'), may hold values from -0.125 to 0.125
- output_weight: bfloat16 [4096, 2048], P('tensor', 'dp'), may hold values from -0.5 to 0.5
- gain_attn: float32 [2048], replicated, may hold values from 0.5 to 1.5
- gain_moe: float32 [2048], replicated, may hold values from 0.5 to 1.5
- query_gain: float32 [128], replicated, may hold values from 0.5 to 2.5
- key_gain: float32 [128], replicated, may hold values from 0.5 to 2.5
- router: bfloat16 [2048, 32], replicated, may hold values from -0.0625 to 0.0625
- gate_weight: bfloat16 [32, 2048, 768], P(('dp', 'tensor')), may hold values from -0.125 to 0.125
- up_weight: bfloat16 [32, 2048, 768], P(('dp', 'tensor')), may hold values from -0.125 to 0.125
- down_weight: bfloat16 [32, 768, 2048], P(('dp', 'tensor')), may hold values from -0.625 to 0.625
- cotangent: bfloat16 [4096, 2048], P(('dp', 'tensor')), may hold values from -6 to 6
Outputs:
- output: bfloat16 [4096, 2048], P(('dp', 'tensor'))
- grad_input: float32 [4096, 2048], P(('dp', 'tensor'))
- grad_query_weight: float32 [2048, 4096], P('dp', 'tensor')
- grad_key_weight: float32 [2048, 512], P('dp', 'tensor')
- grad_value_weight: float32 [2048, 512], P('dp', 'tensor')
- grad_output_weight: float32 [4096, 2048], P('tensor', 'dp')
- grad_gain_attn: float32 [2048], replicated
- grad_gain_moe: float32 [2048], replicated
- grad_query_gain: float32 [128], replicated
- grad_key_gain: float32 [128], replicated
- grad_router: float32 [2048, 32], replicated
- grad_gate: float32 [32, 2048, 768], P(('dp', 'tensor'))
- grad_up: float32 [32, 2048, 768], P(('dp', 'tensor'))
- grad_down: float32 [32, 768, 2048], P(('dp', 'tensor'))
Inputs may be any that keep to these rules, and one draw needn't show every extreme that they name: `routes`: in the rows of one device (128 aligned rows) each expert is named by at most 64 rows, a bound that some block reaches; a row names 8 different experts. `segments`: each row numbers its 6 packed sequences in order, never falling; each sequence has 1 to 256 tokens, one exactly 256.
All inputs are finite; a program needn't handle non-finite values.
Results may differ from a plain program's by a relative error of at most 0.019.
Values may be sent and summed in bfloat16 or wider, within the bound.
A program may use at most 256 MiB of HBM per device.

v0:
```python
import math

import jax
import jax.numpy as jnp
from jax import lax
from jax.sharding import PartitionSpec as P

EPSILON = 1e-06
THETA_BASE = 1000000.0
NEG_BIG = -1e30


def mix(form, left, right):
    return jnp.einsum(form, left, right, preferred_element_type=jnp.float32)


def rms_scale(values):
    return lax.rsqrt(jnp.mean(values * values, axis=-1, keepdims=True) + EPSILON)


def rope_tables(seg_ids, head_dim):
    length = seg_ids.shape[0]
    row_index = jnp.arange(length, dtype=jnp.int32)
    starts = jnp.sum((seg_ids[None, :] < seg_ids[:, None]).astype(jnp.int32), axis=1)
    places = (row_index - starts).astype(jnp.float32)
    half_dim = head_dim // 2
    frequency = THETA_BASE ** (-(jnp.arange(half_dim, dtype=jnp.float32) * (2.0 / head_dim)))
    angles = places[:, None] * frequency[None, :]
    return (jnp.cos(angles), jnp.sin(angles))


def rotate(values, cosine, sine_table):
    half_dim = values.shape[-1] // 2
    front_part = values[..., :half_dim]
    back_part = values[..., half_dim:]
    cos_rows = cosine[:, None, :]
    sin_rows = sine_table[:, None, :]
    return jnp.concatenate(
        [
            front_part * cos_rows - back_part * sin_rows,
            back_part * cos_rows + front_part * sin_rows,
        ],
        axis=-1,
    )


def unrotate(values, cosine, sine_table):
    half_dim = values.shape[-1] // 2
    front_part = values[..., :half_dim]
    back_part = values[..., half_dim:]
    cos_rows = cosine[:, None, :]
    sin_rows = sine_table[:, None, :]
    return jnp.concatenate(
        [
            front_part * cos_rows + back_part * sin_rows,
            back_part * cos_rows - front_part * sin_rows,
        ],
        axis=-1,
    )


def head_norm_back(grad_out, normed, factor, gain):
    grad_normed = grad_out * gain
    grad_gain = jnp.sum(grad_out * normed, axis=(0, 1))
    grad_values = factor * (
        grad_normed - normed * jnp.mean(grad_normed * normed, axis=-1, keepdims=True)
    )
    return (grad_values, grad_gain)


def row_norm_back(grad_out, normed, factor, gain):
    grad_normed = grad_out * gain
    grad_gain = jnp.sum(grad_out * normed, axis=0)
    grad_values = factor * (
        grad_normed - normed * jnp.mean(grad_normed * normed, axis=-1, keepdims=True)
    )
    return (grad_values, grad_gain)


def softmax_rows(logits):
    top_value = jnp.max(logits, axis=-1, keepdims=True)
    expo = jnp.exp(logits - top_value)
    return expo / jnp.sum(expo, axis=-1, keepdims=True)


def attn_forward(rows, seg_ids, wq_full, wk_full, wv_full, query_gain, key_gain):
    length = rows.shape[0]
    head_dim = query_gain.shape[0]
    num_heads = wq_full.shape[1] // head_dim
    kv_heads = wk_full.shape[1] // head_dim
    per_group = num_heads // kv_heads
    inv_root = 1.0 / math.sqrt(head_dim)
    block_rows = math.gcd(length, 512)
    cosine, sine_table = rope_tables(seg_ids, head_dim)
    query = jnp.dot(rows, wq_full, preferred_element_type=jnp.float32).reshape(
        length, num_heads, head_dim
    )
    key_proj = jnp.dot(rows, wk_full, preferred_element_type=jnp.float32).reshape(
        length, kv_heads, head_dim
    )
    value_rows = (
        jnp.dot(rows, wv_full, preferred_element_type=jnp.float32)
        .astype(jnp.bfloat16)
        .reshape(length, kv_heads, head_dim)
    )
    query_factor = rms_scale(query)
    query_hat = query * query_factor
    key_factor = rms_scale(key_proj)
    key_hat = key_proj * key_factor
    query_rot = (
        rotate(query_hat * query_gain, cosine, sine_table)
        .astype(jnp.bfloat16)
        .reshape(length, kv_heads, per_group, head_dim)
    )
    key_rot = rotate(key_hat * key_gain, cosine, sine_table).astype(jnp.bfloat16)
    row_index = jnp.arange(length, dtype=jnp.int32)
    scores = mix("qgrd,kgd->grqk", query_rot, key_rot) * inv_root
    visible = (seg_ids[0:block_rows, None] == seg_ids[None, :]) & (
        row_index[None, :] <= row_index[0:block_rows, None]
    )
    scores = jnp.where(visible, scores, NEG_BIG)
    top_value = jnp.max(scores, axis=-1, keepdims=True)
    expo = jnp.exp(scores - top_value)
    totals = jnp.sum(expo, axis=-1, keepdims=True)
    prob_rows = (expo / totals).astype(jnp.bfloat16)
    outputs = mix("grqk,kgd->qgrd", prob_rows, value_rows).astype(jnp.bfloat16)
    lse_parts = top_value[..., 0] + jnp.log(totals[..., 0])
    attn_heads = outputs.reshape(length, num_heads * head_dim)
    return (
        attn_heads,
        lse_parts,
        query_rot,
        key_rot,
        value_rows,
        cosine,
        sine_table,
        query_hat,
        query_factor,
        key_hat,
        key_factor,
    )


def attn_backward(
    grad_attn, rows, seg_ids, wq_full, wk_full, wv_full, wo_full, query_gain, key_gain, saved
):
    (
        attn_heads,
        lse_all,
        query_rot,
        key_rot,
        value_rows,
        cosine,
        sine_table,
        query_hat,
        query_factor,
        key_hat,
        key_factor,
    ) = saved
    length = rows.shape[0]
    head_dim = query_gain.shape[0]
    num_heads = query_hat.shape[1]
    inv_root = 1.0 / math.sqrt(head_dim)
    block_rows = math.gcd(length, 512)
    grad_wo = jnp.dot(attn_heads.T, grad_attn, preferred_element_type=jnp.float32)
    grad_heads = (
        jnp.dot(grad_attn, wo_full.T, preferred_element_type=jnp.float32)
        .astype(jnp.bfloat16)
        .reshape(query_rot.shape)
    )
    heads_view = attn_heads.reshape(query_rot.shape)
    row_delta = jnp.transpose(
        jnp.sum(grad_heads.astype(jnp.float32) * heads_view.astype(jnp.float32), axis=-1), (1, 2, 0)
    )
    row_index = jnp.arange(length, dtype=jnp.int32)
    scores = mix("qgrd,kgd->grqk", query_rot, key_rot) * inv_root
    visible = (seg_ids[0:block_rows, None] == seg_ids[None, :]) & (
        row_index[None, :] <= row_index[0:block_rows, None]
    )
    scores = jnp.where(visible, scores, NEG_BIG)
    prob_f = jnp.where(visible, jnp.exp(scores - lse_all[:, :, 0:block_rows, None]), 0.0)
    prob_rows = prob_f.astype(jnp.bfloat16)
    grad_value = mix("grqk,qgrd->kgd", prob_rows, grad_heads)
    grad_probs = mix("qgrd,kgd->grqk", grad_heads, value_rows)
    grad_scores = (prob_f * (grad_probs - row_delta[:, :, 0:block_rows, None])).astype(jnp.bfloat16)
    pieces = mix("grqk,kgd->qgrd", grad_scores, key_rot) * inv_root
    grad_key_rot = mix("grqk,qgrd->kgd", grad_scores, query_rot) * inv_root
    grad_query_rot = pieces.reshape(length, num_heads, head_dim)
    grad_query, grad_qgain = head_norm_back(
        unrotate(grad_query_rot, cosine, sine_table), query_hat, query_factor, query_gain
    )
    grad_key, grad_kgain = head_norm_back(
        unrotate(grad_key_rot, cosine, sine_table), key_hat, key_factor, key_gain
    )
    query_b = grad_query.astype(jnp.bfloat16).reshape(length, -1)
    key_b = grad_key.astype(jnp.bfloat16).reshape(length, -1)
    value_b = grad_value.astype(jnp.bfloat16).reshape(length, -1)
    grad_rows = (
        jnp.dot(query_b, wq_full.T, preferred_element_type=jnp.float32)
        + jnp.dot(key_b, wk_full.T, preferred_element_type=jnp.float32)
        + jnp.dot(value_b, wv_full.T, preferred_element_type=jnp.float32)
    )
    grad_wq = jnp.dot(rows.T, query_b, preferred_element_type=jnp.float32)
    grad_wk = jnp.dot(rows.T, key_b, preferred_element_type=jnp.float32)
    grad_wv = jnp.dot(rows.T, value_b, preferred_element_type=jnp.float32)
    return (grad_rows, grad_wq, grad_wk, grad_wv, grad_wo, grad_qgain, grad_kgain)


def expert_forward(expert_rows, wgate, wup, wdown):
    gate_pre = jnp.dot(expert_rows, wgate, preferred_element_type=jnp.float32)
    up_pre = jnp.dot(expert_rows, wup, preferred_element_type=jnp.float32)
    hidden_units = (jax.nn.silu(gate_pre) * up_pre).astype(jnp.bfloat16)
    result = jnp.dot(hidden_units, wdown, preferred_element_type=jnp.float32).astype(jnp.bfloat16)
    return (result, gate_pre, up_pre, hidden_units)


def expert_backward(expert_rows, grad_result, wgate, wup, wdown, gate_pre, up_pre, hidden_units):
    grad_hidden = jnp.dot(grad_result, wdown.T, preferred_element_type=jnp.float32)
    sigma = jax.nn.sigmoid(gate_pre)
    grad_gate_pre = (grad_hidden * up_pre * sigma * (1.0 + gate_pre * (1.0 - sigma))).astype(
        jnp.bfloat16
    )
    grad_up_pre = (grad_hidden * gate_pre * sigma).astype(jnp.bfloat16)
    grad_rows = (
        jnp.dot(grad_gate_pre, wgate.T, preferred_element_type=jnp.float32)
        + jnp.dot(grad_up_pre, wup.T, preferred_element_type=jnp.float32)
    ).astype(jnp.bfloat16)
    grad_wd = jnp.dot(hidden_units.T, grad_result, preferred_element_type=jnp.float32)
    grad_wg = jnp.dot(expert_rows.T, grad_gate_pre, preferred_element_type=jnp.float32)
    grad_wu = jnp.dot(expert_rows.T, grad_up_pre, preferred_element_type=jnp.float32)
    return (grad_rows, grad_wg, grad_wu, grad_wd)


def to_experts(buffer):
    return lax.all_to_all(buffer, ("dp", "tensor"), split_axis=0, concat_axis=0, tiled=True)


def to_sources(buffer):
    return lax.all_to_all(buffer, ("dp", "tensor"), split_axis=0, concat_axis=0, tiled=True)


def shards(
    hidden_in,
    segments,
    routes,
    query_weight,
    key_weight,
    value_weight,
    output_weight,
    gain_attn,
    gain_moe,
    query_gain,
    key_gain,
    router,
    gate_weight,
    up_weight,
    down_weight,
    cotangent,
):
    seg_ids = segments[0]
    rows_dev = hidden_in.shape[0]
    width = hidden_in.shape[1]
    top_count = routes.shape[1]
    experts = router.shape[1]
    capacity = 2 * rows_dev * top_count // experts
    full_query, full_key, full_value, full_output = (
        lax.all_gather(query_weight, "dp", axis=0, tiled=True),
        lax.all_gather(key_weight, "dp", axis=0, tiled=True),
        lax.all_gather(value_weight, "dp", axis=0, tiled=True),
        lax.all_gather(output_weight, "dp", axis=1, tiled=True),
    )
    inputs32 = hidden_in.astype(jnp.float32)
    factor_one = rms_scale(inputs32)
    normed_one = inputs32 * factor_one
    rows_one = (normed_one * gain_attn).astype(jnp.bfloat16)
    group_rows = lax.all_gather(rows_one, "tensor", axis=0, tiled=True)
    saved = attn_forward(
        group_rows, seg_ids, full_query, full_key, full_value, query_gain, key_gain
    )
    partial_add = jnp.dot(saved[0], full_output, preferred_element_type=jnp.float32)
    attn_add = lax.psum_scatter(partial_add, "tensor", scatter_dimension=0, tiled=True)
    residual = inputs32 + attn_add
    factor_two = rms_scale(residual)
    normed_two = residual * factor_two
    rows_two = (normed_two * gain_moe).astype(jnp.bfloat16)
    router_probs = softmax_rows(jnp.dot(rows_two, router, preferred_element_type=jnp.float32))
    route_hot = (routes[:, :, None] == jnp.arange(experts, dtype=jnp.int32)[None, None, :]).astype(
        jnp.float32
    )
    picked = jnp.sum(route_hot * router_probs[:, None, :], axis=-1)
    total = jnp.sum(picked, axis=1, keepdims=True)
    gates = picked / total
    flat_routes = routes.reshape(-1)
    onehot = (flat_routes[:, None] == jnp.arange(experts, dtype=jnp.int32)[None, :]).astype(
        jnp.int32
    )
    ranks = jnp.sum(onehot * jnp.cumsum(onehot, axis=0), axis=1) - 1
    slots = flat_routes * capacity + ranks
    send_rows = (
        jnp.zeros((experts * capacity, width), jnp.bfloat16)
        .at[slots]
        .set(jnp.repeat(rows_two, top_count, axis=0))
    )
    received = to_experts(send_rows.reshape(experts, capacity, width)).reshape(-1, width)
    result, gate_pre, up_pre, hidden_units = expert_forward(
        received, gate_weight[0], up_weight[0], down_weight[0]
    )
    returned = to_sources(result.reshape(-1, capacity, width)).reshape(experts * capacity, width)
    pair_out = returned[slots].astype(jnp.float32).reshape(rows_dev, top_count, width)
    moe_sum = jnp.sum(gates[:, :, None] * pair_out, axis=1)
    output = (residual + moe_sum).astype(jnp.bfloat16)
    cot32 = cotangent.astype(jnp.float32)
    grad_gates = jnp.sum(cot32[:, None, :] * pair_out, axis=-1)
    grad_result = (gates[:, :, None] * cot32[:, None, :]).astype(jnp.bfloat16).reshape(-1, width)
    send_grads = jnp.zeros((experts * capacity, width), jnp.bfloat16).at[slots].set(grad_result)
    received_grads = to_experts(send_grads.reshape(experts, capacity, width)).reshape(-1, width)
    grad_expert_rows, grad_wg, grad_wu, grad_wd = expert_backward(
        received,
        received_grads,
        gate_weight[0],
        up_weight[0],
        down_weight[0],
        gate_pre,
        up_pre,
        hidden_units,
    )
    returned_grads = to_sources(grad_expert_rows.reshape(-1, capacity, width)).reshape(
        experts * capacity, width
    )
    grad_pairs = returned_grads[slots].astype(jnp.float32).reshape(rows_dev, top_count, width)
    grad_picked = (grad_gates - jnp.sum(gates * grad_gates, axis=1, keepdims=True)) / total
    grad_probs = jnp.sum(route_hot * grad_picked[:, :, None], axis=1)
    grad_logits = (
        router_probs * (grad_probs - jnp.sum(grad_probs * router_probs, axis=-1, keepdims=True))
    ).astype(jnp.bfloat16)
    grad_router = jnp.dot(rows_two.T, grad_logits, preferred_element_type=jnp.float32)
    grad_rows_two = jnp.sum(grad_pairs, axis=1) + jnp.dot(
        grad_logits, router.T, preferred_element_type=jnp.float32
    )
    grad_res_norm, grad_gain_moe = row_norm_back(grad_rows_two, normed_two, factor_two, gain_moe)
    grad_residual = cot32 + grad_res_norm
    grad_attn = grad_residual.astype(jnp.bfloat16)
    group_grads = lax.all_gather(grad_attn, "tensor", axis=0, tiled=True)
    back_query, back_key, back_value, back_output = (
        lax.all_gather(query_weight, "dp", axis=0, tiled=True),
        lax.all_gather(key_weight, "dp", axis=0, tiled=True),
        lax.all_gather(value_weight, "dp", axis=0, tiled=True),
        lax.all_gather(output_weight, "dp", axis=1, tiled=True),
    )
    grad_group_rows, grad_wq, grad_wk, grad_wv, grad_wo, grad_qgain, grad_kgain = attn_backward(
        group_grads,
        group_rows,
        seg_ids,
        back_query,
        back_key,
        back_value,
        back_output,
        query_gain,
        key_gain,
        saved,
    )
    grad_rows_one = lax.psum_scatter(
        grad_group_rows.astype(jnp.bfloat16), "tensor", scatter_dimension=0, tiled=True
    ).astype(jnp.float32)
    grad_in_norm, grad_gain_attn = row_norm_back(grad_rows_one, normed_one, factor_one, gain_attn)
    grad_input = grad_residual + grad_in_norm
    grad_wq, grad_wk, grad_wv, grad_wo = (
        lax.psum_scatter(
            grad_wq.astype(jnp.bfloat16), "dp", scatter_dimension=0, tiled=True
        ).astype(jnp.float32),
        lax.psum_scatter(
            grad_wk.astype(jnp.bfloat16), "dp", scatter_dimension=0, tiled=True
        ).astype(jnp.float32),
        lax.psum_scatter(
            grad_wv.astype(jnp.bfloat16), "dp", scatter_dimension=0, tiled=True
        ).astype(jnp.float32),
        lax.psum_scatter(
            grad_wo.astype(jnp.bfloat16), "dp", scatter_dimension=1, tiled=True
        ).astype(jnp.float32),
    )
    grad_gain_attn, grad_gain_moe, grad_qgain, grad_kgain, grad_router = lax.psum(
        (grad_gain_attn, grad_gain_moe, grad_qgain, grad_kgain, grad_router), ("dp", "tensor")
    )
    return (
        output,
        grad_input,
        grad_wq,
        grad_wk,
        grad_wv,
        grad_wo,
        grad_gain_attn,
        grad_gain_moe,
        grad_qgain,
        grad_kgain,
        grad_router,
        grad_wg[None],
        grad_wu[None],
        grad_wd[None],
    )


def solution(mesh):
    placed = (
        P(("dp", "tensor"), None),
        P("dp", None),
        P(("dp", "tensor"), None),
        P("dp", "tensor"),
        P("dp", "tensor"),
        P("dp", "tensor"),
        P("tensor", "dp"),
        P(),
        P(),
        P(),
        P(),
        P(),
        P(("dp", "tensor"), None, None),
        P(("dp", "tensor"), None, None),
        P(("dp", "tensor"), None, None),
        P(("dp", "tensor"), None),
    )
    return jax.shard_map(
        shards,
        mesh=mesh,
        in_specs=placed,
        out_specs=(
            P(("dp", "tensor"), None),
            P(("dp", "tensor"), None),
            P("dp", "tensor"),
            P("dp", "tensor"),
            P("dp", "tensor"),
            P("tensor", "dp"),
            P(),
            P(),
            P(),
            P(),
            P(),
            P(("dp", "tensor"), None, None),
            P(("dp", "tensor"), None, None),
            P(("dp", "tensor"), None, None),
        ),
        check_vma=False,
    )
```

profile of v0, /device:TPU:0, one launch (start us, length us, event | category | flops | bytes accessed | tf_op | source)
XLA Modules:
  0.0 1480.8 jit_solution(1355727751144046355)
XLA Ops:
  9.2 2.0 fusion.52
  12.8 13.2 all_gather.24
  26.0 10.8 all_gather.23
  37.2 2.1 multiply_cosine_fusion
  39.3 20.5 %all-gather.5.cloned.1.call-done = bf16[512,2048]{1,0:T(8,128)(2,1)} async-done(((bf16[128,2048]{1,0:T(8,128)(2,1)}), bf16[512,2048]{1,0:T(8,128)(2,1)}) %all-gather.5.cloned.1.call-update) | async-done | bytes 2097168 | tf_op jit(solution)/shard_map/all_gather | solution.py:276
  59.8 2.5 multiply_reduce_fusion.8
  63.7 3.1 fusion.48
  66.8 30.3 %all-gather.7.cloned.1.call-done = bf16[2048,1024]{1,0:T(8,128)(2,1)} async-done(((bf16[256,1024]{1,0:T(8,128)(2,1)}), bf16[2048,1024]{1,0:T(8,128)(2,1)}) %all-gather.7.cloned.1.call-update) | async-done | bytes 4194320 | tf_op jit(solution)/shard_map/all_gather | solution.py:267
  97.1 5.2 fusion.91
  106.5 2.1 fusion.36
  109.4 2.3 fusion.7
  111.8 1.8 fusion.5
  115.6 3.7 fusion.41
  119.3 17.0 %all-gather.9.cloned.1.call-done = bf16[1024,2048]{1,0:T(8,128)(2,1)} async-done(((bf16[1024,256]{1,0:T(8,128)(2,1)}), bf16[1024,2048]{1,0:T(8,128)(2,1)}) %all-gather.9.cloned.1.call-update) | async-done | bytes 4194320 | tf_op jit(solution)/shard_map/all_gather | solution.py:270
  136.4 6.9 fusion.92
  144.2 9.0 reduce-window.6
  154.0 66.3 %reduce-scatter.7.cloned.1.call-done = f32[128,2048]{1,0:T(8,128)} async-done(((f32[512,2048]{1,0:T(8,128)}), f32[128,2048]{1,0:T(8,128)}) %reduce-scatter.7.cloned.1.call-update) | async-done | bytes 1048592 | tf_op jit(solution)/shard_map/reduce_scatter | solution.py:281
  223.8 11.7 scatter_custom_fusion
  235.5 5.7 all-to-all-start
  241.2 2.1 convert_element_type.187
  245.0 12.1 scatter_custom_fusion.1
  257.1 165.5 %all-to-all-done = bf16[32,64,2048]{2,1,0:T(8,128)(2,1)} async-done(((bf16[32,64,2048]{2,1,0:T(8,128)(2,1)}), bf16[32,64,2048]{2,1,0:T(8,128)(2,1)}, u32[]{:S(2)}, u32[]{:S(2)}) %all-to-all-start) | async-done | bytes 8388640 | tf_op jit(solution)/shard_map/all_to_all | solution.py:235
  422.6 8.6 all-to-all-start.2
  431.2 11.8 fusion.25
  443.0 10.7 fusion.29
  453.8 158.8 %all-to-all-done.2 = bf16[32,64,2048]{2,1,0:T(8,128)(2,1)} async-done(((bf16[32,64,2048]{2,1,0:T(8,128)(2,1)}), bf16[32,64,2048]{2,1,0:T(8,128)(2,1)}, u32[]{:S(2)}, u32[]{:S(2)}) %all-to-all-start.2) | async-done | bytes 8388640 | tf_op jit(solution)/shard_map/all_to_all | solution.py:235
  612.6 15.9 %multiply_convert_fusion = (bf16[2048,768]{1,0:T(8,128)(2,1)}, bf16[2048,768]{1,0:T(8,128)(2,1)}, bf16[2048,768]{1,0:T(8,128)(2,1)S(1)}) fusion(f32[2048,768]{1,0:T(8,128)} %fusion.29, f32[2048,768]{1,0:T(8,128)} %fusion.25, bf16[2048,2048]{1,0:T(8,128)(2,1)} %bitcast.27, bf16[1,768,2048]{2,1,0:T(8,128)(2,1)S(1)} %copy-done), kind=kOutput, calls=%fused_computation.22 | convolution fusion | flops 6467616768 | bytes 33554432 | tf_op jit(solution)/shard_map/dot_general | solution.py:218
  628.5 8.9 convolution_convert_fusion
  637.5 8.7 all-to-all-start.1
  646.2 12.4 fusion.27
  658.6 12.4 add_convert_fusion
  671.0 156.6 %all-to-all-done.1 = bf16[32,64,2048]{2,1,0:T(8,128)(2,1)} async-done(((bf16[32,64,2048]{2,1,0:T(8,128)(2,1)}), bf16[32,64,2048]{2,1,0:T(8,128)(2,1)}, u32[]{:S(2)}, u32[]{:S(2)}) %all-to-all-start.1) | async-done | bytes 8388640 | tf_op jit(solution)/shard_map/all_to_all | solution.py:239
  827.6 8.5 all-to-all-start.3
  836.1 13.8 gather_fusion
  849.9 5.8 fusion.1
  855.9 161.5 %all-to-all-done.3 = bf16[32,64,2048]{2,1,0:T(8,128)(2,1)} async-done(((bf16[32,64,2048]{2,1,0:T(8,128)(2,1)}), bf16[32,64,2048]{2,1,0:T(8,128)(2,1)}, u32[]{:S(2)}, u32[]{:S(2)}) %all-to-all-start.3) | async-done | bytes 8388640 | tf_op jit(solution)/shard_map/all_to_all | solution.py:239
  1017.4 13.3 gather_fusion.1
  1030.7 5.2 convert_reduce_fusion
  1039.8 6.0 fusion.8
  1045.7 8.0 copy.184
  1053.8 34.0 %all-gather.11.cloned.1.call-done = bf16[512,2048]{1,0:T(8,128)(2,1)} async-done(((bf16[128,2048]{1,0:T(8,128)(2,1)}), bf16[512,2048]{1,0:T(8,128)(2,1)}) %all-gather.11.cloned.1.call-update) | async-done | bytes 2097168 | tf_op jit(solution)/shard_map/all_gather | solution.py:343
  1087.8 6.2 convolution_convert_fusion.5
  1095.9 6.0 fusion.11
  1101.9 2.2 fusion.46
  1104.2 1.8 multiply_bitcast_fusion
  1109.2 3.0 fusion.59
  1115.4 1.7 multiply_reduce_fusion.6
  1122.0 1.7 mul.564
  1126.6 2.4 fusion.93
  1130.1 2.1 add_convert_fusion.1
  1132.3 5.9 convolution_convert_fusion.1
  1139.4 4.4 convolution_convert_fusion.2
  1145.7 11.0 convolution_bitcast_fusion
  1156.7 11.2 convolution_bitcast_fusion.1
  1167.9 11.1 convolution_bitcast_fusion.2
  1181.5 4.2 reduce-scatter.13.cloned.1.call-done
  1187.2 44.5 %reduce-scatter.9.cloned.1.call-done = bf16[128,2048]{1,0:T(8,128)(2,1)} async-done(((bf16[512,2048]{1,0:T(8,128)(2,1)}), bf16[128,2048]{1,0:T(8,128)(2,1)}) %reduce-scatter.9.cloned.1.call-update) | async-done | bytes 524304 | tf_op jit(solution)/shard_map/reduce_scatter | solution.py:362
  1233.2 4.1 fusion.51
  1237.3 39.8 %all-reduce = (f32[2048]{0:T(1024)}, f32[2048]{0:T(1024)}, f32[128]{0:T(128)}, f32[128]{0:T(128)}) all-reduce(f32[2048]{0:T(1024)S(1)} %get-tuple-element.18, f32[2048]{0:T(1024)S(1)} %copy-done.61, f32[128]{0:T(128)S(1)} %bitcast_reduce_fusion, f32[128]{0:T(128)S(1)} %copy-done.76), channel_id=1, replica_groups=mesh['dp'=8,'tensor'=4] {'dp','tensor'}, use_global_device_ids=true, to_apply=%region_34.35 | all-reduce | flops 4352 | bytes 34816 | tf_op jit(solution)/shard_map/psum | solution.py:381
  1277.1 8.3 reduce-scatter.17.cloned.1.call-done
  1285.4 2.1 convert_element_type.216
  1287.5 52.3 %reduce-scatter.11.cloned.1.call-done = bf16[256,1024]{1,0:T(8,128)(2,1)} async-done(((bf16[2048,1024]{1,0:T(8,128)(2,1)}), bf16[256,1024]{1,0:T(8,128)(2,1)}) %reduce-scatter.11.cloned.1.call-update) | async-done | bytes 524304 | tf_op jit(solution)/shard_map/reduce_scatter | solution.py:368
  1339.8 2.1 convert_element_type.210
  1341.9 130.5 %all-reduce.3.cloned.1.call-done = f32[2048,32]{0,1:T(8,128)} async-done(((f32[2048,32]{0,1:T(8,128)}), f32[2048,32]{0,1:T(8,128)}) %all-reduce.3.cloned.1.call-update) | async-done | bytes 262160 | tf_op jit(solution)/shard_map/psum | solution.py:381
  (270 shorter events, 50.4 us)
Async XLA Ops:
  7.2 605.4 %copy-start = (bf16[1,768,2048]{2,1,0:T(8,128)(2,1)S(1)}, bf16[1,768,2048]{2,1,0:T(8,128)(2,1)}, u32[]{:S(2)}) copy-start(bf16[1,768,2048]{2,1,0:T(8,128)(2,1)} %param.30) | copy-start | bytes 9437188
  7.2 29.6 %copy-start.62 = (s32[1,512]{1,0:T(1,128)S(1)}, s32[1,512]{1,0:T(1,128)}, u32[]{:S(2)}) copy-start(s32[1,512]{1,0:T(1,128)} %param.17) | copy-start | bytes 6148
  7.2 55.8 %copy-start.73 = (f32[128]{0:T(128)S(1)}, f32[128]{0:T(128)}, u32[]{:S(2)}) copy-start(f32[128]{0:T(128)} %param.26) | copy-start | bytes 1540
  7.2 52.6 %all-gather.5.cloned.1.call-start = ((), (), s32[]{:S(2)}) async-start(), calls=%async_computation.10 | async-start | bytes 2621440 | tf_op jit(solution)/shard_map/all_gather | solution.py:276
  11.3 85.8 %all-gather.7.cloned.1.call-start = ((), (), s32[]{:S(2)}) async-start(), calls=%async_computation.11 | async-start | bytes 4718592 | tf_op jit(solution)/shard_map/all_gather | solution.py:267
  12.0 124.4 %all-gather.9.cloned.1.call-start = ((), (), s32[]{:S(2)}) async-start(), calls=%async_computation.12 | async-start | bytes 4718592 | tf_op jit(solution)/shard_map/all_gather | solution.py:270
  12.7 207.5 %reduce-scatter.7.cloned.1.call-start = ((), (), s32[]{:S(2)}) async-start(), calls=%async_computation.13 | async-start | bytes 5242880 | tf_op jit(solution)/shard_map/reduce_scatter | solution.py:281
  12.8 54.0 %copy-start.69 = (f32[64]{0:T(128)}, f32[64]{0:T(128)S(1)}, u32[]{:S(2)}) copy-start(f32[64]{0:T(128)S(1)} %negate_power_fusion) | copy-start | bytes 772
  37.0 65.2 %copy-start.59 = (f32[512]{0:T(512)}, f32[512]{0:T(512)S(1)}, u32[]{:S(2)}) copy-start(f32[512]{0:T(512)S(1)} %subtract_convert_fusion.1) | copy-start | bytes 6148
  37.2 76.3 %copy-start.23 = (pred[512,512]{0,1:T(8,128)(4,1)}, pred[512,512]{0,1:T(8,128)(4,1)S(1)}, u32[]{:S(2)}) copy-start(pred[512,512]{0,1:T(8,128)(4,1)S(1)} %fusion.58) | copy-start | bytes 786436
  63.7 45.7 %copy-start.37 = (bf16[512,64]{0,1:T(8,128)(2,1)}, bf16[512,64]{0,1:T(8,128)(2,1)S(1)}, u32[]{:S(2)}) copy-start(bf16[512,64]{0,1:T(8,128)(2,1)S(1)} %get-tuple-element.45) | copy-start | bytes 196612
  63.7 45.7 %copy-start.39 = (bf16[512,64]{0,1:T(8,128)(2,1)}, bf16[512,64]{0,1:T(8,128)(2,1)S(1)}, u32[]{:S(2)}) copy-start(bf16[512,64]{0,1:T(8,128)(2,1)S(1)} %get-tuple-element.46) | copy-start | bytes 196612
  111.7 3.3 copy-start.2
  111.8 3.8 copy-start.49
  143.3 79.6 %copy-start.46 = (f32[2048]{0:T(1024)S(1)}, f32[2048]{0:T(1024)}, u32[]{:S(2)}) copy-start(f32[2048]{0:T(1024)} %param.24) | copy-start | bytes 24580
  221.9 13.6 copy-start.64
  235.5 7.9 copy-start.41
  235.5 187.1 %all-to-all-start = ((bf16[32,64,2048]{2,1,0:T(8,128)(2,1)}), bf16[32,64,2048]{2,1,0:T(8,128)(2,1)}, u32[]{:S(2)}, u32[]{:S(2)}) async-start(bf16[32,64,2048]{2,1,0:T(8,128)(2,1)} %bitcast.265), calls=%async_computation.1 | async-start | bytes 16777216 | tf_op jit(solution)/shard_map/all_to_all | solution.py:235
  422.6 190.0 %all-to-all-start.2 = ((bf16[32,64,2048]{2,1,0:T(8,128)(2,1)}), bf16[32,64,2048]{2,1,0:T(8,128)(2,1)}, u32[]{:S(2)}, u32[]{:S(2)}) async-start(bf16[32,64,2048]{2,1,0:T(8,128)(2,1)} %bitcast.266), calls=%async_computation.3 | async-start | bytes 16777216 | tf_op jit(solution)/shard_map/all_to_all | solution.py:235
  431.2 11.8 copy-start.78
  628.5 9.0 copy-start.81
  637.5 8.7 copy-start.79
  637.5 190.1 %all-to-all-start.1 = ((bf16[32,64,2048]{2,1,0:T(8,128)(2,1)}), bf16[32,64,2048]{2,1,0:T(8,128)(2,1)}, u32[]{:S(2)}, u32[]{:S(2)}) async-start(bf16[32,64,2048]{2,1,0:T(8,128)(2,1)} %bitcast.270), calls=%async_computation.2 | async-start | bytes 16777216 | tf_op jit(solution)/shard_map/all_to_all | solution.py:239
  646.2 12.4 copy-start.80
  646.2 12.4 copy-start.84
  827.6 189.9 %all-to-all-start.3 = ((bf16[32,64,2048]{2,1,0:T(8,128)(2,1)}), bf16[32,64,2048]{2,1,0:T(8,128)(2,1)}, u32[]{:S(2)}, u32[]{:S(2)}) async-start(bf16[32,64,2048]{2,1,0:T(8,128)(2,1)} %bitcast.269), calls=%async_computation.4 | async-start | bytes 16777216 | tf_op jit(solution)/shard_map/all_to_all | solution.py:239
  836.1 251.8 %all-gather.11.cloned.1.call-start = ((), (), s32[]{:S(2)}) async-start(), calls=%async_computation.14 | async-start | bytes 2621440 | tf_op jit(solution)/shard_map/all_gather | solution.py:343
  836.1 13.8 copy-start.11
  855.9 180.0 %copy-start.52 = (bf16[128,32]{0,1:T(8,128)(2,1)}, bf16[128,32]{0,1:T(8,128)(2,1)S(1)}, u32[]{:S(2)}) copy-start(bf16[128,32]{0,1:T(8,128)(2,1)S(1)} %multiply_convert_fusion.5) | copy-start | bytes 24580
  1030.7 5.2 copy-start.8
  1030.7 5.2 copy-start.47
  1030.7 5.2 copy-start.65
  1030.7 6.3 copy-start.21
  1035.9 3.8 copy-start.45
  1036.0 3.8 copy-start.55
  1036.0 3.8 copy-start.24
  1037.0 8.7 copy-start.12
  1038.2 141.7 %reduce-scatter.15.cloned.1.call-start = ((), (), s32[]{:S(2)}) async-start(), calls=%async_computation.18 | async-start | bytes 589824 | tf_op jit(solution)/shard_map/reduce_scatter | solution.py:374
  1039.8 6.0 copy-start.56
  1053.8 41.7 %copy-start.19 = (bf16[128,8,512]{2,0,1:T(8,128)(2,1)S(1)}, bf16[128,8,512]{2,0,1:T(8,128)(2,1)}, u32[]{:S(2)}) copy-start(bf16[128,8,512]{2,0,1:T(8,128)(2,1)} %fusion.41) | copy-start | bytes 3145732
  1095.9 6.0 copy-start.14
  1095.9 6.0 copy-start.16
  1104.2 3.4 copy-start.29
  1104.2 3.4 copy-start.31
  1115.4 70.3 %reduce-scatter.13.cloned.1.call-start = ((), (), s32[]{:S(2)}) async-start(), calls=%async_computation.17 | async-start | bytes 589824 | tf_op jit(solution)/shard_map/reduce_scatter | solution.py:371
  1120.4 3.4 copy-start.34
  1120.4 4.0 copy-start.63
  1122.0 109.7 %reduce-scatter.9.cloned.1.call-start = ((), (), s32[]{:S(2)}) async-start(), calls=%async_computation.15 | async-start | bytes 2621440 | tf_op jit(solution)/shard_map/reduce_scatter | solution.py:362
  1132.2 153.2 %reduce-scatter.17.cloned.1.call-start = ((), (), s32[]{:S(2)}) async-start(), calls=%async_computation.19 | async-start | bytes 4718592 | tf_op jit(solution)/shard_map/reduce_scatter | solution.py:377
  1138.2 201.6 %reduce-scatter.11.cloned.1.call-start = ((), (), s32[]{:S(2)}) async-start(), calls=%async_computation.16 | async-start | bytes 4718592 | tf_op jit(solution)/shard_map/reduce_scatter | solution.py:368
  1143.8 328.6 %all-reduce.3.cloned.1.call-start = ((), (), s32[]{:S(2)}) async-start(), calls=%async_computation.20 | async-start | bytes 524288 | tf_op jit(solution)/shard_map/psum | solution.py:381
  1145.7 11.0 copy-start.85
  1156.7 11.2 copy-start.83
  1167.8 11.1 copy-start.17
  1167.8 11.1 copy-start.53
  1167.8 63.8 %copy-start.10 = (bf16[128,2048]{1,0:T(8,128)(2,1)S(1)}, bf16[128,2048]{1,0:T(8,128)(2,1)}, u32[]{:S(2)}) copy-start(bf16[128,2048]{1,0:T(8,128)(2,1)} %param.16) | copy-start | bytes 1572868
  1167.9 63.8 %copy-start.51 = (f32[2048]{0:T(1024)S(1)}, f32[2048]{0:T(1024)}, u32[]{:S(2)}) copy-start(f32[2048]{0:T(1024)} %param.23) | copy-start | bytes 24580
  1167.9 63.8 %copy-start.68 = (f32[128]{0:T(128)S(1)}, f32[128]{0:T(128)}, u32[]{:S(2)}) copy-start(f32[128]{0:T(128)} %copy-done.67) | copy-start | bytes 1540
  1167.9 65.3 %copy-start.48 = (f32[2048]{0:T(1024)S(1)}, f32[2048]{0:T(1024)}, u32[]{:S(2)}) copy-start(f32[2048]{0:T(1024)} %param.24) | copy-start | bytes 24580
  1167.9 65.3 %copy-start.66 = (f32[128]{0:T(128)S(1)}, f32[128]{0:T(128)}, u32[]{:S(2)}) copy-start(f32[128]{0:T(128)} %copy-done.64) | copy-start | bytes 1540
  1167.9 65.3 %copy-start.75 = (f32[128]{0:T(128)S(1)}, f32[128]{0:T(128)}, u32[]{:S(2)}) copy-start(f32[128]{0:T(128)} %copy-done.74) | copy-start | bytes 1540
  1179.9 57.4 %copy-start.61 = (f32[2048]{0:T(1024)S(1)}, f32[2048]{0:T(1024)}, u32[]{:S(2)}) copy-start(f32[2048]{0:T(1024)} %get-tuple-element.16) | copy-start | bytes 24580
  1179.9 57.4 %copy-start.76 = (f32[128]{0:T(128)S(1)}, f32[128]{0:T(128)}, u32[]{:S(2)}) copy-start(f32[128]{0:T(128)} %get-tuple-element.20) | copy-start | bytes 1540
  1233.1 241.0 %copy-start.1 = (bf16[1,768,2048]{2,1,0:T(8,128)(2,1)S(1)}, bf16[1,768,2048]{2,1,0:T(8,128)(2,1)}, u32[]{:S(2)}) copy-start(bf16[1,768,2048]{2,1,0:T(8,128)(2,1)} %param.30) | copy-start | bytes 9437188
  (37 other events, 70.3 us)
Sparse Core Ops, SparseCore 0:
  11.4 48.3 all-gather.4
  61.7 35.3 all-gather.6
  99.0 37.3 all-gather.8
  143.4 76.8 reduce-scatter.6
  1038.4 49.4 all-gather.10
  1115.5 32.9 reduce-scatter.14
  1151.5 34.1 reduce-scatter.12
  1188.0 43.6 reduce-scatter.8
  1235.0 50.3 reduce-scatter.16
  1288.6 51.1 reduce-scatter.10
  1345.9 126.5 all-reduce.2
where the time goes:
time: 1480 us
  waiting for transfers between devices  1050 us (71%)
  matrix products  168 us (11%)
  other arithmetic  80.1 us (5%)
  local copies, waits for them, and re-layouts  69.5 us (5%)
  blocking collectives  63.9 us (4%)
  starting transfers between devices  32.4 us (2%)
  between operations  15.2 us (1%)
    all_to_all x2, waiting for transfers between devices, to_experts(): lax.all_to_all(buffer, ('dp', 'tensor'), split_axis=0, concat_axis=0, til...  324 us
    all_to_all x2, waiting for transfers between devices, to_sources(): lax.all_to_all(buffer, ('dp', 'tensor'), split_axis=0, concat_axis=0, til...  318 us
    psum x1, waiting for transfers between devices, shards(): lax.psum((grad_gain_attn, grad_gain_moe, grad_qgain, grad_kgain, grad_rou...  131 us
    reduce_scatter x1, waiting for transfers between devices, shards(): lax.psum_scatter(partial_add, 'tensor', scatter_dimension=0, tiled=True)  66.3 us
    reduce_scatter x1, waiting for transfers between devices, shards(): lax.psum_scatter(grad_wq.astype(jnp.bfloat16), 'dp', scatter_dimension=0,...  52.3 us
    reduce_scatter x1, waiting for transfers between devices, shards(): lax.psum_scatter(grad_group_rows.astype(jnp.bfloat16), 'tensor', scatter_...  44.5 us
    psum x1, blocking collectives, shards(): lax.psum((grad_gain_attn, grad_gain_moe, grad_qgain, grad_kgain, grad_rou...  39.8 us
    all_gather x1, waiting for transfers between devices, shards(): group_grads = lax.all_gather(grad_attn, 'tensor', axis=0, tiled=True)  34 us
  transfers between devices with their start and end apart: 15, of which 14 were waited for; matrix products, arithmetic and copies ran while one was open for 14% of the time, Pallas kernels for 0%

commit v1 on v0

--- a/solution.py
+++ b/solution.py
@@ -3,11 +3,578 @@
 import jax
 import jax.numpy as jnp
 from jax import lax
+from jax.experimental import pallas as pl
+from jax.experimental.pallas import tpu as pltpu
 from jax.sharding import PartitionSpec as P
 
 EPSILON = 1e-06
 THETA_BASE = 1000000.0
 NEG_BIG = -1e30
+
+
+MESH = pl.DeviceIdType.MESH
+
+
+class Place:
+    def __init__(self, length):
+        self.length = length
+        self.dp = lax.axis_index("dp")
+        self.z = lax.axis_index("tensor")
+        core, along_x, along_y = self.dp % 2, (self.dp // 2) % 2, self.dp // 4
+        self.to_core = 1 - 2 * core
+        self.core = self.dp + self.to_core
+        self.x = self.dp + 2 - 4 * along_x
+        self.y = self.dp + 4 - 8 * along_y
+        self.columns = (self.dp, self.x, self.y, self.x + self.y - self.dp)
+        self.has_up = self.z < length - 1
+        self.has_down = self.z > 0
+
+    def device(self, kind):
+        if kind == "x":
+            return (self.x, self.z)
+        if kind == "y":
+            return (self.y, self.z)
+        if kind == "core":
+            return (self.core, self.z)
+        if kind == "up":
+            return (self.dp, self.z + 1)
+        return (self.dp, self.z - 1)
+
+    def condition(self, kind):
+        return {"up": self.has_up, "down": self.has_down}.get(kind)
+
+    def target(self, turn):
+        length, z = self.length, self.z
+
+        def at_least(left, right):
+            return (left - right + 2 * length) // (2 * length)
+
+        high = at_least(z, length // 2)
+        mirrored = z + high * (length - 1 - 2 * z)
+        above = length - 1 - mirrored
+        first = at_least(above - 1, turn)
+        if turn == length - 1:
+            return z
+        found = first * (length - 1 - turn) + (1 - first) * (turn - above)
+        return found + high * (length - 1 - 2 * found)
+
+
+def guarded(condition, action):
+    if condition is None:
+        action()
+    else:
+        pl.when(condition)(action)
+
+
+def meet(place, over_z, over_dp):
+    barrier = pltpu.get_barrier_semaphore()
+    kinds = (("x", "y", "core") if over_dp else ()) + (("up", "down") if over_z else ())
+    for kind in kinds:
+
+        def greet(kind=kind):
+            pl.semaphore_signal(
+                barrier, 1, device_id=place.device(kind), device_id_type=MESH
+            )
+
+        guarded(place.condition(kind), greet)
+    count = 3 if over_dp else 0
+    if over_z:
+        length = place.length
+        count = count + (place.z + length - 1) // length + (2 * length - 2 - place.z) // length
+    pl.semaphore_wait(barrier, count)
+
+
+class Sends:
+    def __init__(self, place):
+        self.place = place
+        self.started = []
+
+    def start(self, kind, views, condition=None):
+        def build():
+            source, target, send_sem, recv_sem = views()
+            return pltpu.make_async_remote_copy(
+                src_ref=source,
+                dst_ref=target,
+                send_sem=send_sem,
+                recv_sem=recv_sem,
+                device_id=self.place.device(kind),
+                device_id_type=MESH,
+            )
+
+        guarded(self.place.condition(kind), lambda: build().start())
+        self.started.append((condition, self.place.condition(kind), build))
+
+    def drain(self):
+        for outer, inner, build in self.started:
+
+            def finish(inner=inner, build=build):
+                guarded(inner, lambda: build().wait_send())
+
+            guarded(outer, finish)
+
+
+class GatherItem:
+    def __init__(self, mode, place, own, slot, recv, send, local):
+        self.mode, self.place = mode, place
+        self.own, self.slot = own, slot
+        self.recv, self.send, self.local = recv, send, local
+        self.over_z = mode != "dp"
+        self.over_dp = mode != "z"
+        self.length = place.length if self.over_z else 1
+        self.z = place.z if self.over_z else 0
+
+    def index(self, column, z):
+        if self.mode == "all":
+            return column * self.length + z
+        return column if self.mode == "dp" else z
+
+    @staticmethod
+    def semaphores(mode, length):
+        blocks = {"all": 8 * length, "dp": 8, "z": length}[mode]
+        turns = 2 * length - 1 if mode != "dp" else 1
+        return [
+            pltpu.SemaphoreType.DMA((blocks, 2)),
+            pltpu.SemaphoreType.DMA((10, turns, 2)),
+            pltpu.SemaphoreType.DMA((2,)),
+        ]
+
+    def turns(self, distance):
+        if distance == 0:
+            return [(0, self.z, None, None)]
+        place = self.place
+        return [
+            (2 * distance - 1, self.z - distance, place.z - distance >= 0, "up"),
+            (2 * distance, self.z + distance, place.z + distance < self.length, "down"),
+        ]
+
+    def pass_on(self, sends, lane, kind, column, z, turn, h, source=None, condition=None):
+
+        def views():
+            view = self.slot(column, z, h)
+            return (
+                view if source is None else source(h),
+                view,
+                self.send.at[lane, turn, h],
+                self.recv.at[self.index(column, z), h],
+            )
+
+        sends.start(kind, views, condition)
+
+    def arrived(self, column, z, h):
+        view = self.slot(column, z, h)
+        pltpu.make_async_copy(view, view, self.recv.at[self.index(column, z), h]).wait()
+
+    def begin(self, sends):
+        place = self.place
+        for h in range(2):
+            own = self.own
+            if self.over_z:
+                self.pass_on(sends, 0, "up", place.dp, self.z, 0, h, own)
+                self.pass_on(sends, 1, "down", place.dp, self.z, 0, h, own)
+            if self.over_dp:
+                self.pass_on(sends, 2, "x", place.dp, self.z, 0, h, own)
+                self.pass_on(sends, 3, "y", place.dp, self.z, 0, h, own)
+                self.pass_on(sends, 4, "core", place.dp, self.z, 0, h, own)
+        for h in range(2):
+            pltpu.make_async_copy(
+                self.own(h), self.slot(place.dp, self.z, h), self.local.at[h]
+            ).start()
+
+    def along_z(self, sends, distance):
+        if not self.over_z or distance >= self.length:
+            return
+        place = self.place
+        for turn, z, condition, onward in self.turns(distance):
+
+            def step(turn=turn, z=z, condition=condition, onward=onward):
+                for h in range(2):
+                    self.arrived(place.dp, z, h)
+                    if distance < self.length - 1:
+                        self.pass_on(
+                            sends, 0 if onward == "up" else 1, onward, place.dp, z, turn, h,
+                            condition=condition,
+                        )
+                    if self.over_dp:
+                        for lane, kind in ((2, "x"), (3, "y"), (4, "core")):
+                            self.pass_on(
+                                sends, lane, kind, place.dp, z, turn, h, condition=condition
+                            )
+
+            guarded(condition, step)
+
+    def across(self, sends, distance):
+        if not self.over_dp or not 0 <= distance < self.length:
+            return
+        _, x, y, _ = self.place.columns
+        for turn, z, condition, _ in self.turns(distance):
+
+            def step(turn=turn, z=z, condition=condition):
+                for h in range(2):
+                    self.arrived(x, z, h)
+                    if h == 0:
+                        self.pass_on(sends, 5, "y", x, z, turn, h, condition=condition)
+                    self.pass_on(sends, 7, "core", x, z, turn, h, condition=condition)
+                    self.arrived(y, z, h)
+                    if h == 1:
+                        self.pass_on(sends, 6, "x", y, z, turn, h, condition=condition)
+                    self.pass_on(sends, 8, "core", y, z, turn, h, condition=condition)
+
+            guarded(condition, step)
+
+    def diagonal(self, sends, distance):
+        if not self.over_dp or not 0 <= distance < self.length:
+            return
+        corner = self.place.columns[3]
+        for turn, z, condition, _ in self.turns(distance):
+
+            def step(turn=turn, z=z, condition=condition):
+                for h in range(2):
+                    self.arrived(corner, z, h)
+                    self.pass_on(sends, 9, "core", corner, z, turn, h, condition=condition)
+
+            guarded(condition, step)
+
+    def finish(self):
+        place = self.place
+        for h in range(2):
+            pltpu.make_async_copy(
+                self.own(h), self.slot(place.dp, self.z, h), self.local.at[h]
+            ).wait()
+        if self.over_dp:
+            for column in place.columns:
+                for z in range(self.length):
+                    for h in range(2):
+                        self.arrived(column + place.to_core, z, h)
+
+
+def run_gather(place, items):
+    meet(place, any(i.over_z for i in items), any(i.over_dp for i in items))
+    sends = Sends(place)
+    for item in items:
+        item.begin(sends)
+    for step in range(place.length + 2):
+        for item in items:
+            item.along_z(sends, step + 1)
+        for item in items:
+            item.across(sends, step)
+        for item in items:
+            item.diagonal(sends, step - 1)
+    for item in items:
+        item.finish()
+    sends.drain()
+
+
+def gather(specs, length, collective_id, name):
+    modes = [mode for _, mode, _ in specs]
+    shapes, sems = [], []
+    for array, mode, by_columns in specs:
+        blocks = {"all": 8 * length, "dp": 8, "z": length}[mode]
+        if by_columns:
+            shape = (array.shape[0], blocks * array.shape[1])
+        else:
+            shape = (blocks,) + array.shape
+        shapes.append(jax.ShapeDtypeStruct(shape, array.dtype))
+        sems += GatherItem.semaphores(mode, length)
+    count = len(specs)
+
+    def kernel(*refs):
+        place = Place(length)
+        items = []
+        for number, (array, mode, by_columns) in enumerate(specs):
+            source, target = refs[number], refs[count + number]
+            recv, send, local = refs[2 * count + 3 * number : 2 * count + 3 * number + 3]
+            half = array.shape[0] // 2
+            width = array.shape[1]
+            item = GatherItem(mode, place, None, None, recv, send, local)
+
+            def own(h, source=source, half=half):
+                return source.at[pl.ds(h * half, half)]
+
+            def slot(column, z, h, target=target, half=half, width=width, item=item, by=by_columns):
+                block = item.index(column, z)
+                if by:
+                    return target.at[
+                        pl.ds(h * half, half), pl.ds(pl.multiple_of(block * width, width), width)
+                    ]
+                return target.at[block, pl.ds(h * half, half)]
+
+            item.own, item.slot = own, slot
+            items.append(item)
+        run_gather(place, items)
+
+    return pl.pallas_call(
+        kernel,
+        name=name,
+        out_shape=shapes,
+        in_specs=[pl.BlockSpec(memory_space=pl.ANY)] * count,
+        out_specs=[pl.BlockSpec(memory_space=pl.ANY)] * count,
+        scratch_shapes=sems,
+        compiler_params=pltpu.CompilerParams(collective_id=collective_id, has_side_effects=True),
+    )(*[array for array, _, _ in specs])
+
+
+class ReduceItem:
+    def __init__(self, mode, place, block, bufs, out):
+        self.mode, self.place, self.block, self.out = mode, place, block, out
+        self.over_z = mode != "dp"
+        self.over_dp = mode != "z"
+        self.length = place.length if self.over_z else 1
+        (self.acc, self.from_core, self.corner, self.from_xy, self.from_z,
+         self.load, self.send, self.recv) = bufs
+
+    @staticmethod
+    def scratch(mode, length, rows, width):
+        t = length if mode != "dp" else 1
+        columns = 4 if mode != "z" else 1
+        dp = mode != "z"
+        half = (rows // 2, width)
+        small = (8, 128)
+        return [
+            pltpu.VMEM((columns, t, 2) + half, jnp.bfloat16),
+            pltpu.VMEM(((columns, t, 2) + half) if dp else small, jnp.bfloat16),
+            pltpu.VMEM(((2, t) + half) if dp else small, jnp.bfloat16),
+            pltpu.VMEM(((2, t, 2) + half) if dp else small, jnp.bfloat16),
+            pltpu.VMEM(((t + 1, 2) + half) if mode != "dp" else small, jnp.bfloat16),
+            pltpu.SemaphoreType.DMA((columns, t, 2)),
+            pltpu.SemaphoreType.DMA((10, t, 2)),
+            pltpu.SemaphoreType.DMA((9, t + 1, 2)),
+        ]
+
+    def z_of(self, turn):
+        return self.place.target(turn) if self.over_z else 0
+
+    def got(self, ref, lane, turn, h):
+        pltpu.make_async_copy(ref, ref, self.recv.at[lane, turn, h]).wait()
+
+    def loaded(self, column, turn, h):
+        ref = self.acc.at[column, turn, h]
+        pltpu.make_async_copy(ref, ref, self.load.at[column, turn, h]).wait()
+
+    def add(self, target, refs, out=None):
+        rows = target.shape[0]
+        step = 16 if rows % 16 == 0 else rows
+        place = target if out is None else out
+
+        def body(i, carry):
+            at = pl.ds(pl.multiple_of(i * step, step), step)
+            total = target[at, :].astype(jnp.float32)
+            for ref in refs:
+                total = total + ref[at, :].astype(jnp.float32)
+            place[at, :] = total.astype(place.dtype)
+            return carry
+
+        lax.fori_loop(0, rows // step, body, 0, unroll=2 if (rows // step) % 2 == 0 else 1)
+
+    def begin(self):
+        place = self.place
+        if self.over_z:
+
+            @pl.when((place.z == 0) | (place.z == self.length - 1))
+            def _():
+                def clear(i, carry):
+                    self.from_z[i // 2, i % 2] = jnp.zeros(self.from_z.shape[2:], jnp.bfloat16)
+                    return carry
+
+                lax.fori_loop(0, 2 * (self.length + 1), clear, 0)
+
+    def start(self, sends):
+        place = self.place
+        order = (3, 1, 2, 0) if self.over_dp else (0,)
+        for column in order:
+            for turn in range(self.length):
+                for h in range(2):
+                    pltpu.make_async_copy(
+                        self.block(place.columns[column], self.z_of(turn), h),
+                        self.acc.at[column, turn, h],
+                        self.load.at[column, turn, h],
+                    ).start()
+                    if self.over_dp:
+                        sends.start(
+                            "core",
+                            lambda column=column, turn=turn, h=h: (
+                                self.block(
+                                    place.columns[column] + place.to_core, self.z_of(turn), h
+                                ),
+                                self.from_core.at[column, turn, h],
+                                self.send.at[column, turn, h],
+                                self.recv.at[column, turn, h],
+                            ),
+                        )
+
+    def settle(self, column, turn, h, extra=(), out=None):
+        self.loaded(column, turn, h)
+        refs = list(extra)
+        if self.over_dp:
+            ref = self.from_core.at[column, turn, h]
+            self.got(ref, column, turn, h)
+            refs.append(ref)
+        if refs or out is not None:
+            self.add(self.acc.at[column, turn, h], refs, out)
+
+    def corners(self, sends, turn):
+        if not self.over_dp or turn >= self.length:
+            return
+        for h, kind in ((0, "y"), (1, "x")):
+            self.settle(3, turn, h)
+            sends.start(
+                kind,
+                lambda h=h: (
+                    self.acc.at[3, turn, h],
+                    self.corner.at[h, turn],
+                    self.send.at[4, turn, h],
+                    self.recv.at[4, turn, h],
+                ),
+            )
+
+    def straight(self, sends, turn, second):
+        if not self.over_dp or turn >= self.length:
+            return
+        for column, kind in ((1, "x"), (2, "y")):
+            h = (column - 1) if second else (2 - column)
+            extra = ()
+            if second:
+                ref = self.corner.at[h, turn]
+                self.got(ref, 4, turn, h)
+                extra = (ref,)
+            self.settle(column, turn, h, extra)
+            sends.start(
+                kind,
+                lambda column=column, h=h: (
+                    self.acc.at[column, turn, h],
+                    self.from_xy.at[column - 1, turn, h],
+                    self.send.at[4 + column, turn, h],
+                    self.recv.at[4 + column, turn, h],
+                ),
+            )
+
+    def home(self, sends, turn):
+        if turn >= self.length:
+            return
+        place = self.place
+        last = turn == self.length - 1
+        z = self.z_of(turn)
+        for h in range(2):
+            extra = []
+            if self.over_dp:
+                for lane in (0, 1):
+                    ref = self.from_xy.at[lane, turn, h]
+                    self.got(ref, 5 + lane, turn, h)
+                    extra.append(ref)
+            if self.over_z:
+                slot = self.from_z.at[z, h]
+
+                def got_slot(h=h):
+                    self.got(self.from_z.at[z, h], 7, z, h)
+
+                def got_other(h=h):
+                    self.got(self.from_z.at[self.length, h], 7, self.length, h)
+
+                if last:
+                    guarded(place.has_down, got_slot)
+                    guarded(place.has_up, got_other)
+                    extra += [slot, self.from_z.at[self.length, h]]
+                else:
+                    guarded((z > place.z) & place.has_down, got_slot)
+                    guarded((z < place.z) & place.has_up, got_slot)
+                    extra.append(slot)
+            self.settle(
+                0, turn, h, extra, self.out(h) if last else None
+            )
+            if self.over_z and not last:
+
+                def going_up(h=h):
+                    return (
+                        self.acc.at[0, turn, h],
+                        self.from_z.at[z, h],
+                        self.send.at[7, turn, h],
+                        self.recv.at[7, z, h],
+                    )
+
+                def going_down(h=h):
+                    arrives = (z - place.z + 1 + self.length) // self.length
+                    goal = z + arrives * (self.length - z)
+                    return (
+                        self.acc.at[0, turn, h],
+                        self.from_z.at[goal, h],
+                        self.send.at[7, turn, h],
+                        self.recv.at[7, goal, h],
+                    )
+
+                above, below = z > place.z, z < place.z
+                pl.when(above)(lambda: sends.start("up", going_up, above))
+                pl.when(below)(lambda: sends.start("down", going_down, below))
+
+
+def run_reduce(place, items):
+    for item in items:
+        item.begin()
+    meet(place, any(i.over_z for i in items), any(i.over_dp for i in items))
+    sends = Sends(place)
+    for item in items:
+        item.start(sends)
+    longest = max(item.length for item in items)
+    for turn in range(longest):
+        for item in items:
+            item.corners(sends, turn)
+    for turn in range(longest):
+        for item in items:
+            item.straight(sends, turn, False)
+    for turn in range(longest):
+        for item in items:
+            item.straight(sends, turn, True)
+    for turn in range(longest):
+        for item in items:
+            item.home(sends, turn)
+    sends.drain()
+
+
+def reduce_scatter(specs, length, collective_id, name):
+    count = len(specs)
+    shapes, scratch, dims = [], [], []
+    for array, mode, by_columns, dtype in specs:
+        blocks = {"all": 8 * length, "dp": 8, "z": length}[mode]
+        if by_columns:
+            rows, width = array.shape[0], array.shape[1] // blocks
+        else:
+            rows, width = array.shape[0] // blocks, array.shape[1]
+        dims.append((rows, width))
+        shapes.append(jax.ShapeDtypeStruct((rows, width), dtype))
+        scratch += ReduceItem.scratch(mode, length, rows, width)
+
+    def kernel(*refs):
+        place = Place(length)
+        items = []
+        for number, (array, mode, by_columns, dtype) in enumerate(specs):
+            rows, width = dims[number]
+            source, target = refs[number], refs[count + number]
+            bufs = refs[2 * count + 8 * number : 2 * count + 8 * number + 8]
+            half = rows // 2
+
+            def block(column, z, h, source=source, half=half, rows=rows, width=width, mode=mode, by=by_columns):
+                index = {"all": column * length + z, "dp": column, "z": z}[mode]
+                if by:
+                    return source.at[
+                        pl.ds(h * half, half), pl.ds(pl.multiple_of(index * width, width), width)
+                    ]
+                return source.at[pl.ds(pl.multiple_of(index * rows + h * half, half), half)]
+
+            def out(h, target=target, half=half):
+                return target.at[pl.ds(h * half, half)]
+
+            items.append(ReduceItem(mode, place, block, bufs, out))
+        run_reduce(place, items)
+
+    return pl.pallas_call(
+        kernel,
+        name=name,
+        out_shape=shapes,
+        in_specs=[pl.BlockSpec(memory_space=pl.ANY)] * count,
+        out_specs=[pl.BlockSpec(memory_space=pltpu.VMEM)] * count,
+        scratch_shapes=scratch,
+        compiler_params=pltpu.CompilerParams(
+            collective_id=collective_id, has_side_effects=True, vmem_limit_bytes=56 << 20
+        ),
+    )(*[array for array, _, _, _ in specs])
 
 
 def mix(form, left, right):
@@ -399,6 +966,256 @@
     )
 
 
+def attn_backward_joint(
+    grad_attn, rows, seg_ids, joint_full, wo_full, query_gain, key_gain, saved
+):
+    (
+        attn_heads,
+        lse_all,
+        query_rot,
+        key_rot,
+        value_rows,
+        cosine,
+        sine_table,
+        query_hat,
+        query_factor,
+        key_hat,
+        key_factor,
+    ) = saved
+    length = rows.shape[0]
+    head_dim = query_gain.shape[0]
+    num_heads = query_hat.shape[1]
+    inv_root = 1.0 / math.sqrt(head_dim)
+    block_rows = math.gcd(length, 512)
+    grad_wo = jnp.dot(attn_heads.T, grad_attn, preferred_element_type=jnp.float32)
+    grad_heads = (
+        jnp.dot(grad_attn, wo_full.T, preferred_element_type=jnp.float32)
+        .astype(jnp.bfloat16)
+        .reshape(query_rot.shape)
+    )
+    heads_view = attn_heads.reshape(query_rot.shape)
+    row_delta = jnp.transpose(
+        jnp.sum(grad_heads.astype(jnp.float32) * heads_view.astype(jnp.float32), axis=-1), (1, 2, 0)
+    )
+    row_index = jnp.arange(length, dtype=jnp.int32)
+    scores = mix("qgrd,kgd->grqk", query_rot, key_rot) * inv_root
+    visible = (seg_ids[0:block_rows, None] == seg_ids[None, :]) & (
+        row_index[None, :] <= row_index[0:block_rows, None]
+    )
+    scores = jnp.where(visible, scores, NEG_BIG)
+    prob_f = jnp.where(visible, jnp.exp(scores - lse_all[:, :, 0:block_rows, None]), 0.0)
+    prob_rows = prob_f.astype(jnp.bfloat16)
+    grad_value = mix("grqk,qgrd->kgd", prob_rows, grad_heads)
+    grad_probs = mix("qgrd,kgd->grqk", grad_heads, value_rows)
+    grad_scores = (prob_f * (grad_probs - row_delta[:, :, 0:block_rows, None])).astype(jnp.bfloat16)
+    pieces = mix("grqk,kgd->qgrd", grad_scores, key_rot) * inv_root
+    grad_key_rot = mix("grqk,qgrd->kgd", grad_scores, query_rot) * inv_root
+    grad_query_rot = pieces.reshape(length, num_heads, head_dim)
+    grad_query, grad_qgain = head_norm_back(
+        unrotate(grad_query_rot, cosine, sine_table), query_hat, query_factor, query_gain
+    )
+    grad_key, grad_kgain = head_norm_back(
+        unrotate(grad_key_rot, cosine, sine_table), key_hat, key_factor, key_gain
+    )
+    query_b = grad_query.astype(jnp.bfloat16).reshape(length, -1)
+    key_b = grad_key.astype(jnp.bfloat16).reshape(length, -1)
+    value_b = grad_value.astype(jnp.bfloat16).reshape(length, -1)
+    joint_b = jnp.concatenate([query_b, key_b, value_b], axis=1)
+    grad_rows = jnp.dot(joint_b, joint_full.T, preferred_element_type=jnp.float32)
+    grad_joint = jnp.dot(rows.T, joint_b, preferred_element_type=jnp.float32)
+    return (grad_rows, grad_joint, grad_wo, grad_qgain, grad_kgain)
+
+
+AXES = ("dp", "tensor")
+
+
+def slots_of(marks, capacity):
+    rows = marks.shape[1]
+    order = jnp.arange(rows, dtype=jnp.int32)
+    upto = (order[:, None] <= order[None, :]).astype(jnp.bfloat16)
+    ranks = jnp.dot(marks.astype(jnp.bfloat16), upto, preferred_element_type=jnp.float32) - 1.0
+    slot = jnp.arange(capacity, dtype=jnp.float32)
+    chosen = (ranks[:, None, :] == slot[None, :, None]) & (marks[:, None, :] > 0.5)
+    return chosen.astype(jnp.bfloat16)
+
+
+def gathered(
+    hidden_in,
+    segments,
+    routes,
+    query_weight,
+    key_weight,
+    value_weight,
+    output_weight,
+    gain_attn,
+    gain_moe,
+    query_gain,
+    key_gain,
+    router,
+    gate_weight,
+    up_weight,
+    down_weight,
+    cotangent,
+):
+    seg_ids = segments[0]
+    rows_dev, width = hidden_in.shape
+    top_count = routes.shape[1]
+    experts = router.shape[1]
+    capacity = 2 * rows_dev * top_count // experts
+    length = lax.axis_size("tensor")
+    devices = lax.axis_size("dp") * length
+    expert = lax.axis_index("dp") * length + lax.axis_index("tensor")
+    query_cols, key_cols = query_weight.shape[1], key_weight.shape[1]
+
+    inputs32 = hidden_in.astype(jnp.float32)
+    factor_one = rms_scale(inputs32)
+    normed_one = inputs32 * factor_one
+    rows_one = (normed_one * gain_attn).astype(jnp.bfloat16)
+    joint_weight = jnp.concatenate([query_weight, key_weight, value_weight], axis=1)
+    group_rows, full_joint, full_output = gather(
+        [
+            (rows_one, "z", False),
+            (joint_weight, "dp", False),
+            (output_weight, "dp", True),
+        ],
+        length,
+        0,
+        "gather_attention",
+    )
+    group_rows = group_rows.reshape(-1, width)
+    full_joint = full_joint.reshape(width, -1)
+    full_query = full_joint[:, :query_cols]
+    full_key = full_joint[:, query_cols : query_cols + key_cols]
+    full_value = full_joint[:, query_cols + key_cols :]
+    saved = attn_forward(
+        group_rows, seg_ids, full_query, full_key, full_value, query_gain, key_gain
+    )
+    partial_add = jnp.dot(saved[0], full_output, preferred_element_type=jnp.float32)
+    (attn_add,) = reduce_scatter(
+        [(partial_add.astype(jnp.bfloat16), "z", False, jnp.float32)], length, 1, "reduce_attention"
+    )
+    residual = inputs32 + attn_add
+    factor_two = rms_scale(residual)
+    normed_two = residual * factor_two
+    rows_two = (normed_two * gain_moe).astype(jnp.bfloat16)
+    router_probs = softmax_rows(jnp.dot(rows_two, router, preferred_element_type=jnp.float32))
+    route_hot = (routes[:, :, None] == jnp.arange(experts, dtype=jnp.int32)[None, None, :]).astype(
+        jnp.float32
+    )
+    picked = jnp.sum(route_hot * router_probs[:, None, :], axis=-1)
+    total = jnp.sum(picked, axis=1, keepdims=True)
+    gates = picked / total
+    named = jnp.sum(route_hot, axis=1)
+    gate_table = jnp.where(named > 0.5, jnp.sum(route_hot * gates[:, :, None], axis=1), -1.0)
+    all_rows, all_cots, all_gates = gather(
+        [
+            (rows_two, "all", False),
+            (cotangent, "all", False),
+            (gate_table.T, "all", False),
+        ],
+        length,
+        2,
+        "gather_rows",
+    )
+    own_gates = lax.dynamic_slice_in_dim(all_gates, expert, 1, axis=1)[:, 0, :]
+    marks = (own_gates >= 0.0).astype(jnp.float32)
+    chosen = slots_of(marks, capacity)
+    slot_gates = jnp.sum(chosen.astype(jnp.float32) * own_gates[:, None, :], axis=-1)
+    received = mix("bst,btd->bsd", chosen, all_rows).astype(jnp.bfloat16).reshape(-1, width)
+    cot_slots = mix("bst,btd->bsd", chosen, all_cots).reshape(-1, width)
+    received_grads = (slot_gates.reshape(-1, 1) * cot_slots).astype(jnp.bfloat16)
+    result, gate_pre, up_pre, hidden_units = expert_forward(
+        received, gate_weight[0], up_weight[0], down_weight[0]
+    )
+    grad_expert_rows, grad_wg, grad_wu, grad_wd = expert_backward(
+        received,
+        received_grads,
+        gate_weight[0],
+        up_weight[0],
+        down_weight[0],
+        gate_pre,
+        up_pre,
+        hidden_units,
+    )
+    result32 = result.astype(jnp.float32)
+    slot_grads = jnp.sum(cot_slots * result32, axis=-1).reshape(devices, capacity)
+    token_grads = jnp.sum(chosen.astype(jnp.float32) * slot_grads[:, :, None], axis=1)
+    back_grads = lax.all_to_all(token_grads, AXES, split_axis=0, concat_axis=0, tiled=True)
+    partial_rows = mix(
+        "bst,bsd->btd", chosen, grad_expert_rows.reshape(devices, capacity, width)
+    ).astype(jnp.bfloat16)
+    (grad_sum,) = reduce_scatter(
+        [(partial_rows.reshape(-1, width), "all", False, jnp.float32)], length, 3, "reduce_grads"
+    )
+    scaled = (slot_gates.reshape(-1, 1) * result32).astype(jnp.bfloat16)
+    partial_out = mix("bst,bsd->btd", chosen, scaled.reshape(devices, capacity, width)).astype(
+        jnp.bfloat16
+    )
+    (moe_sum,) = reduce_scatter(
+        [(partial_out.reshape(-1, width), "all", False, jnp.float32)], length, 4, "reduce_outputs"
+    )
+    output = (residual + moe_sum).astype(jnp.bfloat16)
+    cot32 = cotangent.astype(jnp.float32)
+    grad_gates = jnp.sum(route_hot * back_grads.T[:, None, :], axis=-1)
+    grad_picked = (grad_gates - jnp.sum(gates * grad_gates, axis=1, keepdims=True)) / total
+    grad_probs = jnp.sum(route_hot * grad_picked[:, :, None], axis=1)
+    grad_logits = (
+        router_probs * (grad_probs - jnp.sum(grad_probs * router_probs, axis=-1, keepdims=True))
+    ).astype(jnp.bfloat16)
+    all_logits = lax.all_gather(grad_logits, AXES, axis=0, tiled=True)
+    grad_router = jnp.dot(
+        all_rows.reshape(-1, width).T, all_logits, preferred_element_type=jnp.float32
+    )
+    grad_rows_two = grad_sum + jnp.dot(grad_logits, router.T, preferred_element_type=jnp.float32)
+    grad_res_norm, grad_gain_moe = row_norm_back(grad_rows_two, normed_two, factor_two, gain_moe)
+    grad_residual = cot32 + grad_res_norm
+    grad_attn = grad_residual.astype(jnp.bfloat16)
+    (group_grads,) = gather([(grad_attn, "z", False)], length, 5, "gather_grads")
+    grad_group_rows, grad_joint, grad_wo, grad_qgain, grad_kgain = attn_backward_joint(
+        group_grads.reshape(-1, width),
+        group_rows,
+        seg_ids,
+        full_joint,
+        full_output,
+        query_gain,
+        key_gain,
+        saved,
+    )
+    grad_rows_one, grad_joint, grad_wo = reduce_scatter(
+        [
+            (grad_group_rows.astype(jnp.bfloat16), "z", False, jnp.float32),
+            (grad_joint.astype(jnp.bfloat16), "dp", False, jnp.float32),
+            (grad_wo.astype(jnp.bfloat16), "dp", True, jnp.float32),
+        ],
+        length,
+        6,
+        "reduce_weights",
+    )
+    grad_in_norm, grad_gain_attn = row_norm_back(grad_rows_one, normed_one, factor_one, gain_attn)
+    grad_input = grad_residual + grad_in_norm
+    small = jnp.concatenate([grad_gain_attn, grad_gain_moe, grad_qgain, grad_kgain]).reshape(-1, 128)
+    small = jnp.pad(small, ((0, -small.shape[0] % 16), (0, 0)))
+    (all_small,) = gather([(small, "all", False)], length, 7, "gather_small")
+    sums = jnp.sum(all_small, axis=0).reshape(-1)
+    head_dim = query_gain.shape[0]
+    return (
+        output,
+        grad_input,
+        grad_joint[:, :query_cols],
+        grad_joint[:, query_cols : query_cols + key_cols],
+        grad_joint[:, query_cols + key_cols :],
+        grad_wo,
+        sums[:width],
+        sums[width : 2 * width],
+        sums[2 * width : 2 * width + head_dim],
+        sums[2 * width + head_dim : 2 * width + 2 * head_dim],
+        grad_router,
+        grad_wg[None],
+        grad_wu[None],
+        grad_wd[None],
+    )
+
+
 def solution(mesh):
     placed = (
         P(("dp", "tensor"), None),
@@ -418,8 +1235,9 @@
         P(("dp", "tensor"), None, None),
         P(("dp", "tensor"), None),
     )
+    program = gathered if mesh.shape["dp"] == 8 and mesh.shape["tensor"] <= 4 else shards
     return jax.shard_map(
-        shards,
+        program,
         mesh=mesh,
         in_specs=placed,
         out_specs=(

time: 1480 us -> 959 us (0.65)
  waiting for transfers between devices: 1050 us -> 0.01 us
  Pallas kernels: 0 us -> 568 us
  matrix products: 168 us -> 217 us
  local copies, waits for them, and re-layouts: 69.5 us -> 34.2 us
  starting transfers between devices: 32.4 us -> 4.31 us
  other arithmetic: 80.1 us -> 53.5 us
    all_to_all x4 -> x1, waiting for transfers between devices: 642 us -> 0.01 us  [gathered(): lax.all_to_all(token_grads, AXES, split_axis=0, concat_axis=0, tiled=True)]
    pallas_call x0 -> x8, Pallas kernels: none -> 568 us  [the longest x4 310 us: reduce_scatter(): pl.pallas_call(kernel, name=name, out_shape=shapes, in_specs=[pl.BlockSpe...]
    reduce_scatter x6 -> x0, waiting for transfers between devices: 176 us -> none  [the longest x1 66.3 us: shards(): lax.psum_scatter(partial_add, 'tensor', scatter_dimension=0, tiled=True)]
    psum x1 -> x0, waiting for transfers between devices: 131 us -> none  [shards(): lax.psum((grad_gain_attn, grad_gain_moe, grad_qgain, grad_kgain, grad_rou...]
    all_gather x4 -> x0, waiting for transfers between devices: 102 us -> none  [the longest x1 34 us: shards(): group_grads = lax.all_gather(grad_attn, 'tensor', axis=0, tiled=True)]
    all_gather x2 -> x1, blocking collectives: 24 us -> 74.2 us  [gathered(): all_logits = lax.all_gather(grad_logits, AXES, axis=0, tiled=True)]
    dot_general x6 -> x10, matrix products: 16.8 us -> 65.6 us  [mix(): return jnp.einsum(form, left, right, preferred_element_type=jnp.float32)]
    psum x1 -> x0, blocking collectives: 39.8 us -> none  [shards(): lax.psum((grad_gain_attn, grad_gain_moe, grad_qgain, grad_kgain, grad_rou...]
  transfers between devices with their start and end apart: 15 -> 1, of which waited for: 14 -> 0; matrix products, arithmetic and copies ran while one was open for 14% -> 14% of each run, Pallas kernels for 0% -> 20%
where the time goes in v1:
time: 959 us; the launch traced here: 954 us
  Pallas kernels  568 us (59%)
  matrix products  217 us (23%)
  blocking collectives  74.2 us (8%)
  other arithmetic  53.5 us (6%)
  local copies, waits for them, and re-layouts  34.2 us (4%)
    pallas_call x4, Pallas kernels, reduce_scatter(): pl.pallas_call(kernel, name=name, out_shape=shapes, in_specs=[pl.BlockSpe...  310 us
    pallas_call x4, Pallas kernels, gather(): pl.pallas_call(kernel, name=name, out_shape=shapes, in_specs=[pl.BlockSpe...  258 us
    all_gather x1, blocking collectives, gathered(): all_logits = lax.all_gather(grad_logits, AXES, axis=0, tiled=True)  74.2 us
    dot_general x10, matrix products, mix(): return jnp.einsum(form, left, right, preferred_element_type=jnp.float32)  65.6 us
    convert_element_type x2, other arithmetic, gathered(): (slot_gates.reshape(-1, 1) * cot_slots).astype(jnp.bfloat16)  21.1 us
  transfers between devices with their start and end apart: 1, of which 0 were waited for; matrix products, arithmetic and copies ran while one was open for 14% of the time, Pallas kernels for 20%

profile of v1, /device:TPU:0, one launch (start us, length us, event | category | flops | bytes accessed | tf_op | source)
XLA Modules:
  0.0 954.0 jit_solution(2253902169484594921)
XLA Ops:
  0.7 1.0 convert_reduce_fusion
  1.7 1.7 fusion.46
  3.4 1.2 fusion.43
  5.2 2.0 fusion.37.refs_0_
  7.2 2.0 pad_maximum_fusion.5.refs_1_
  9.2 57.9 %gather_attention.1 = (bf16[4,128,2048]{2,1,0:T(8,128)(2,1)}, bf16[8,256,1280]{2,1,0:T(8,128)(2,1)}, bf16[1024,2048]{1,0:T(8,128)(2,1)}) custom-call(bf16[128,2048]{1,0:T(8,128)(2,1)} %fusion.37.refs_0_, bf16[256,1280]{1,0:T(8,128)(2,1)} %pad_maximum_fusion.5.refs_1_, bf16[1024,256]{1,0:T(8,128)(2,1)} %refs_2_.1), custom_call_target="tpu_custom_call" | custom-call | tf_op jit(solution)/shard_map/gather_attention/pallas_call | solution.py:305
  67.1 3.2 fusion.33
  70.3 2.5 multiply_reduce_fusion.9
  72.8 2.6 slice_bitcast_fusion
  75.5 1.2 multiply_cosine_fusion
  77.4 6.6 copy.70
  84.0 5.2 multiply_reduce_fusion.3
  90.7 1.6 fusion.7
  92.3 1.7 fusion.5
  94.1 1.5 copy-done.2
  95.6 2.7 fusion.27
  98.3 1.0 copy-done.32
  99.3 3.7 convolution_convert_fusion.6.refs_0_
  103.0 40.9 %reduce_attention.1 = f32[128,2048]{1,0:T(8,128)} custom-call(bf16[512,2048]{1,0:T(8,128)(2,1)} %convolution_convert_fusion.6.refs_0_), custom_call_target="tpu_custom_call" | custom-call | tf_op jit(solution)/shard_map/reduce_attention/pallas_call | solution.py:567
  143.9 1.4 multiply_reduce_fusion.6
  148.9 147.5 %gather_rows.1 = (bf16[32,128,2048]{2,1,0:T(8,128)(2,1)}, bf16[32,128,2048]{2,1,0:T(8,128)(2,1)}, f32[32,32,128]{2,1,0:T(8,128)}) custom-call(bf16[128,2048]{1,0:T(8,128)(2,1)} %copy-done.17, bf16[128,2048]{1,0:T(8,128)(2,1)} %refs_1_.1, f32[32,128]{1,0:T(8,128)} %select_bitcast_fusion.refs_2_), custom_call_target="tpu_custom_call" | custom-call | tf_op jit(solution)/shard_map/gather_rows/pallas_call | solution.py:305
  297.6 13.9 %fusion.49 = f32[32,64,2048]{2,1,0:T(8,128)} fusion(bf16[32,128,2048]{2,1,0:T(8,128)(2,1)} %get-tuple-element.28, f32[32,128]{1,0:T(8,128)S(1)} %convolution_add_fusion.1, pred[32,128]{1,0:T(8,128)(4,1)S(1)} %bitcast.256), kind=kOutput, calls=%fused_computation.106 | convolution fusion | flops 1074266112 | bytes 33574912 | tf_op jit(solution)/shard_map/bst,btd->bsd/dot_general | solution.py:581
  311.5 11.5 %convolution_convert_fusion.4 = bf16[32,64,2048]{2,1,0:T(8,128)(2,1)} fusion(bf16[32,128,2048]{2,1,0:T(8,128)(2,1)} %get-tuple-element.27, f32[32,128]{1,0:T(8,128)S(1)} %convolution_add_fusion.1, pred[32,128]{1,0:T(8,128)(4,1)S(1)} %bitcast.257), kind=kOutput, calls=%fused_computation.25 | convolution fusion | flops 1078460416 | bytes 25186304 | tf_op jit(solution)/shard_map/bst,btd->bsd/dot_general | solution.py:581
  323.0 12.1 %fusion.21 = f32[2048,768]{1,0:T(8,128)} fusion(bf16[2048,2048]{1,0:T(8,128)(2,1)} %bitcast.229, bf16[1,2048,768]{2,1,0:T(8,128)(2,1)S(1)} %copy-done.77), kind=kOutput, calls=%fused_computation.45 | convolution fusion | flops 6442450944 | bytes 17825792 | tf_op jit(solution)/shard_map/dot_general | solution.py:777
  335.1 10.9 %multiply_convert_fusion.3 = (bf16[2048,768]{1,0:T(8,128)(2,1)S(1)}, f32[2048,768]{1,0:T(8,128)}) fusion(f32[2048,768]{1,0:T(8,128)} %fusion.21, bf16[2048,2048]{1,0:T(8,128)(2,1)S(1)} %bitcast.230, bf16[1,2048,768]{2,1,0:T(8,128)(2,1)S(1)} %copy-done.79), kind=kOutput, calls=%fused_computation.23 | convolution fusion | flops 6451888128 | bytes 27262976 | tf_op jit(solution)/shard_map/dot_general | solution.py:778
  346.0 13.4 %fusion.1 = (f32[2048]{0:T(1024)S(1)}, bf16[2048,2048]{1,0:T(8,128)(2,1)}) fusion(f32[32,64,2048]{2,1,0:T(8,128)} %fusion.49, bf16[2048,768]{1,0:T(8,128)(2,1)S(1)} %get-tuple-element.79, bf16[1,768,2048]{2,1,0:T(8,128)(2,1)S(1)} %copy-done), kind=kOutput, calls=%fused_computation.3 | convolution fusion | flops 6459226112 | bytes 31465472 | tf_op jit(solution)/shard_map/dot_general | solution.py:780
  359.5 1.1 fusion.36
  360.6 4.3 all-to-all-start
  365.0 9.1 multiply_convert_fusion
  374.2 15.1 %multiply_convert_fusion.1 = (bf16[2048,768]{1,0:T(8,128)(2,1)}, bf16[2048,768]{1,0:T(8,128)(2,1)S(1)}) fusion(f32[2048,768]{1,0:T(8,128)} %fusion.21, f32[2048,768]{1,0:T(8,128)} %get-tuple-element.80, bf16[2048,2048]{1,0:T(8,128)(2,1)} %bitcast.236, bf16[1,768,2048]{2,1,0:T(8,128)(2,1)S(1)} %copy-done), kind=kOutput, calls=%fused_computation.21 | convolution fusion | flops 6462898176 | bytes 30408704 | tf_op jit(solution)/shard_map/dot_general | solution.py:785
  389.3 1.7 copy-done.84
  391.0 9.0 convolution_bitcast_fusion.2
  400.0 12.3 %fusion.19 = f32[2048,2048]{1,0:T(8,128)} fusion(bf16[2048,768]{1,0:T(8,128)(2,1)} %copy-done.84, bf16[1,2048,768]{2,1,0:T(8,128)(2,1)S(1)} %copy-done.78), kind=kOutput, calls=%fused_computation.43 | convolution fusion | flops 6442450944 | bytes 23068672 | tf_op jit(solution)/shard_map/dot_general | solution.py:792
  412.3 11.9 %fusion.2 = (bf16[2048,2048]{1,0:T(8,128)(2,1)}, bf16[2048,2048]{1,0:T(8,128)(2,1)}) fusion(f32[32,64,2048]{2,1,0:T(8,128)S(1)} %bitcast.223, f32[2048]{0:T(1024)S(1)} %mul.510, bf16[2048,2048]{1,0:T(8,128)(2,1)} %get-tuple-element.82), kind=kLoop, calls=%fused_computation.5 | loop fusion | flops 20971520 | bytes 41951232 | tf_op jit(solution)/shard_map/convert_element_type | solution.py:1126
  424.3 11.2 %convolution_bitcast_fusion = f32[1,768,2048]{2,1,0:T(8,128)} fusion(bf16[2048,768]{1,0:T(8,128)(2,1)S(1)} %copy-done.83, bf16[2048,2048]{1,0:T(8,128)(2,1)} %get-tuple-element.67), kind=kOutput, calls=%fused_computation.33 | convolution fusion | flops 6442450944 | bytes 17825792 | tf_op jit(solution)/shard_map/dot_general | solution.py:795
  435.5 9.0 convolution_bitcast_fusion.1
  444.5 13.8 %convolution_convert_fusion.1 = bf16[32,128,2048]{2,1,0:T(8,128)(2,1)} fusion(bf16[32,64,2048]{2,1,0:T(8,128)(2,1)} %bitcast.227, f32[32,128]{1,0:T(8,128)S(1)} %convolution_add_fusion.1, pred[32,128]{1,0:T(8,128)(4,1)S(1)} %bitcast.259), kind=kOutput, calls=%fused_computation.9 | convolution fusion | flops 1082654720 | bytes 25186304 | tf_op jit(solution)/shard_map/bst,bsd->btd/dot_general | solution.py:581
  458.3 13.7 %add_convert_fusion = bf16[2048,2048]{1,0:T(8,128)(2,1)} fusion(f32[2048,2048]{1,0:T(8,128)} %fusion.19, bf16[2048,768]{1,0:T(8,128)(2,1)} %get-tuple-element.49, bf16[1,2048,768]{2,1,0:T(8,128)(2,1)S(1)} %copy-done.80), kind=kOutput, calls=%fused_computation.6 | convolution fusion | flops 6450839552 | bytes 31457280 | tf_op jit(solution)/shard_map/dot_general | solution.py:793
  472.0 13.7 %convolution_convert_fusion = bf16[32,128,2048]{2,1,0:T(8,128)(2,1)} fusion(bf16[32,64,2048]{2,1,0:T(8,128)(2,1)} %bitcast.228, f32[32,128]{1,0:T(8,128)S(1)} %convolution_add_fusion.1, pred[32,128]{1,0:T(8,128)(4,1)S(1)} %bitcast.260), kind=kOutput, calls=%fused_computation.8 | convolution fusion | flops 1082654720 | bytes 25186304 | tf_op jit(solution)/shard_map/bst,bsd->btd/dot_general | solution.py:581
  485.8 5.8 fusion.8
  491.5 8.1 copy.80
  499.6 97.9 %reduce_outputs.1 = f32[128,2048]{1,0:T(8,128)} custom-call(bf16[4096,2048]{1,0:T(8,128)(2,1)} %bitcast.225), custom_call_target="tpu_custom_call" | custom-call | tf_op jit(solution)/shard_map/reduce_outputs/pallas_call | solution.py:567
  597.7 97.3 %reduce_grads.1 = f32[128,2048]{1,0:T(8,128)} custom-call(bf16[4096,2048]{1,0:T(8,128)(2,1)} %bitcast.226), custom_call_target="tpu_custom_call" | custom-call | tf_op jit(solution)/shard_map/reduce_grads/pallas_call | solution.py:567
  695.2 74.2 %all_gather.3 = bf16[4096,32]{0,1:T(8,128)(2,1)} all-gather(bf16[128,32]{0,1:T(8,128)(2,1)S(1)} %multiply_convert_fusion.7), channel_id=1, replica_groups=mesh['dp'=8,'tensor'=4] {'dp','tensor'}, dimensions={0}, use_global_device_ids=true | all-gather | bytes 270336 | tf_op jit(solution)/shard_map/all_gather | solution.py:1165
  769.5 1.7 multiply_reduce_fusion.4
  771.3 1.2 fusion.96.refs_0_
  772.5 33.4 %gather_grads.1 = bf16[4,128,2048]{2,1,0:T(8,128)(2,1)} custom-call(bf16[128,2048]{1,0:T(8,128)(2,1)} %fusion.96.refs_0_), custom_call_target="tpu_custom_call" | custom-call | tf_op jit(solution)/shard_map/gather_grads/pallas_call | solution.py:305
  805.8 5.3 convolution_convert_fusion.8
  811.2 4.3 convolution_convert_fusion.5.refs_2_
  816.3 1.6 multiply_reduce_fusion.2
  817.9 5.4 fusion.9
  823.3 1.4 fusion.31
  828.7 1.0 copy-done.9
  830.6 4.2 convolution_convert_fusion.7.refs_0_
  834.7 4.7 convolution_convert_fusion.2.refs_1_
  839.5 74.0 %reduce_weights.1 = (f32[128,2048]{1,0:T(8,128)}, f32[256,1280]{1,0:T(8,128)}, f32[1024,256]{1,0:T(8,128)}) custom-call(bf16[512,2048]{1,0:T(8,128)(2,1)} %convolution_convert_fusion.7.refs_0_, bf16[2048,1280]{1,0:T(8,128)(2,1)} %convolution_convert_fusion.2.refs_1_, bf16[1024,2048]{1,0:T(8,128)(2,1)} %convolution_convert_fusion.5.refs_2_), custom_call_target="tpu_custom_call" | custom-call | tf_op jit(solution)/shard_map/reduce_weights/pallas_call | solution.py:567
  913.4 1.7 fusion.97
  915.2 2.3 slice.77
  917.5 1.6 fusion.42
  919.7 19.3 %gather_small.1 = f32[32,48,128]{2,1,0:T(8,128)} custom-call(f32[48,128]{1,0:T(8,128)} %pad.4.refs_0_), custom_call_target="tpu_custom_call" | custom-call | tf_op jit(solution)/shard_map/gather_small/pallas_call | solution.py:305
  939.1 1.2 reduce_sum.282
  941.5 9.6 %fusion.99 = f32[2048,32]{0,1:T(8,128)} fusion(bf16[4096,32]{0,1:T(8,128)(2,1)S(1)} %copy-done.27, bf16[4096,2048]{1,0:T(8,128)(2,1)} %bitcast.224), kind=kOutput, calls=%fused_computation.200 | convolution fusion | flops 536870912 | bytes 17301504 | tf_op jit(solution)/shard_map/dot_general | solution.py:1166
  951.1 1.7 fusion.41
  952.8 1.0 copy.99
  (236 shorter events, 14.9 us)
Async XLA Ops:
  0.6 345.4 %copy-start = (bf16[1,768,2048]{2,1,0:T(8,128)(2,1)S(1)}, bf16[1,768,2048]{2,1,0:T(8,128)(2,1)}, u32[]{:S(2)}) copy-start(bf16[1,768,2048]{2,1,0:T(8,128)(2,1)} %param.30) | copy-start | bytes 9437188
  0.7 76.1 %copy-start.70 = (f32[64]{0:T(128)}, f32[64]{0:T(128)S(1)}, u32[]{:S(2)}) copy-start(f32[64]{0:T(128)S(1)} %negate_power_fusion) | copy-start | bytes 772
  67.1 5.7 copy-start.18
  72.8 3.9 copy-start.21
  72.8 3.8 copy-start.72
  76.7 13.1 %copy-start.28 = (f32[512,64]{0,1:T(8,128)}, f32[512,64]{0,1:T(8,128)S(1)}, u32[]{:S(2)}) copy-start(f32[512,64]{0,1:T(8,128)S(1)} %get-tuple-element.69) | copy-start | bytes 393220
  77.4 13.3 %copy-start.45 = (bf16[512,64]{0,1:T(8,128)(2,1)}, bf16[512,64]{0,1:T(8,128)(2,1)S(1)}, u32[]{:S(2)}) copy-start(bf16[512,64]{0,1:T(8,128)(2,1)S(1)} %get-tuple-element.61) | copy-start | bytes 196612
  77.4 13.3 %copy-start.47 = (bf16[512,64]{0,1:T(8,128)(2,1)}, bf16[512,64]{0,1:T(8,128)(2,1)S(1)}, u32[]{:S(2)}) copy-start(bf16[512,64]{0,1:T(8,128)(2,1)S(1)} %get-tuple-element.62) | copy-start | bytes 196612
  84.0 5.3 copy-start.74
  92.3 3.3 copy-start.2
  92.3 3.3 copy-start.81
  95.6 3.7 copy-start.76
  99.3 44.6 %copy-start.10 = (bf16[128,2048]{1,0:T(8,128)(2,1)S(1)}, bf16[128,2048]{1,0:T(8,128)(2,1)}, u32[]{:S(2)}) copy-start(bf16[128,2048]{1,0:T(8,128)(2,1)} %param.16) | copy-start | bytes 1572868
  103.0 43.4 %copy-start.49 = (f32[2048]{0:T(1024)S(1)}, f32[2048]{0:T(1024)}, u32[]{:S(2)}) copy-start(f32[2048]{0:T(1024)} %param.24) | copy-start | bytes 24580
  103.0 44.3 %copy-start.35 = (bf16[2048,32]{0,1:T(8,128)(2,1)S(1)}, bf16[2048,32]{0,1:T(8,128)(2,1)}, u32[]{:S(2)}) copy-start(bf16[2048,32]{0,1:T(8,128)(2,1)} %param.27) | copy-start | bytes 393220
  103.0 45.2 %copy-start.52 = (s32[128,8]{0,1:T(8,128)S(1)}, s32[128,8]{0,1:T(8,128)}, u32[]{:S(2)}) copy-start(s32[128,8]{0,1:T(8,128)} %param.18) | copy-start | bytes 12292
  148.2 163.3 %copy-start.64 = (f32[128]{0:T(128)}, f32[128]{0:T(128)S(1)}, u32[]{:S(2)}) copy-start(f32[128]{0:T(128)S(1)} %fusion.86) | copy-start | bytes 1540
  148.3 163.2 %copy-start.54 = (f32[128,8]{0,1:T(8,128)}, f32[128,8]{0,1:T(8,128)S(1)}, u32[]{:S(2)}) copy-start(f32[128,8]{0,1:T(8,128)S(1)} %get-tuple-element.43) | copy-start | bytes 12292
  148.3 163.2 %copy-start.66 = (f32[128]{0:T(128)}, f32[128]{0:T(128)S(1)}, u32[]{:S(2)}) copy-start(f32[128]{0:T(128)S(1)} %get-tuple-element.42) | copy-start | bytes 1540
  311.5 11.5 %copy-start.77 = (bf16[1,2048,768]{2,1,0:T(8,128)(2,1)S(1)}, bf16[1,2048,768]{2,1,0:T(8,128)(2,1)}, u32[]{:S(2)}) copy-start(bf16[1,2048,768]{2,1,0:T(8,128)(2,1)} %param.28) | copy-start | bytes 9437188
  323.0 12.1 %copy-start.6 = (bf16[32,64,2048]{2,1,0:T(8,128)(2,1)S(1)}, bf16[32,64,2048]{2,1,0:T(8,128)(2,1)}, u32[]{:S(2)}) copy-start(bf16[32,64,2048]{2,1,0:T(8,128)(2,1)} %convolution_convert_fusion.4) | copy-start | bytes 25165828
  323.0 12.1 %copy-start.79 = (bf16[1,2048,768]{2,1,0:T(8,128)(2,1)S(1)}, bf16[1,2048,768]{2,1,0:T(8,128)(2,1)}, u32[]{:S(2)}) copy-start(bf16[1,2048,768]{2,1,0:T(8,128)(2,1)} %param.29) | copy-start | bytes 9437188
  346.0 13.5 %copy-start.82 = (bf16[2048,768]{1,0:T(8,128)(2,1)}, bf16[2048,768]{1,0:T(8,128)(2,1)S(1)}, u32[]{:S(2)}) copy-start(bf16[2048,768]{1,0:T(8,128)(2,1)S(1)} %get-tuple-element.79) | copy-start | bytes 9437188
  360.6 334.4 %all-to-all-start = ((f32[32,1,128]{2,1,0:T(1,128)}), f32[32,1,128]{2,1,0:T(1,128)S(1)}, u32[]{:S(2)}, u32[]{:S(2)}) async-start(f32[32,1,128]{2,1,0:T(1,128)} %bitcast.30), calls=%async_computation | async-start | bytes 32768 | tf_op jit(solution)/shard_map/all_to_all | solution.py:1143
  365.0 25.9 %slice-start.4 = ((s8[8388608]{0:T(1024)(128)(4,1)}), s8[4194304]{0:T(1024)(128)(4,1)S(1)}, s32[]{:S(2)}) async-start(s8[8388608]{0:T(1024)(128)(4,1)} %bitcast.231), calls=%async_computation.5 | async-start | bytes 8388608
  374.2 16.8 %slice-start.5 = ((s8[8388608]{0:T(1024)(128)(4,1)}), s8[4194304]{0:T(1024)(128)(4,1)S(1)}, s32[]{:S(2)}) async-start(s8[8388608]{0:T(1024)(128)(4,1)} %bitcast.231), calls=%async_computation.6 | async-start | bytes 8388608
  391.0 9.0 copy-start.78
  391.0 21.3 %slice-start = ((s8[16777216]{0:T(1024)(128)(4,1)}), s8[4194304]{0:T(1024)(128)(4,1)S(1)}, s32[]{:S(2)}) async-start(s8[16777216]{0:T(1024)(128)(4,1)} %bitcast.222), calls=%async_computation.1 | async-start | bytes 8388608
  391.0 21.3 %slice-start.1 = ((s8[16777216]{0:T(1024)(128)(4,1)}), s8[4194304]{0:T(1024)(128)(4,1)S(1)}, s32[]{:S(2)}) async-start(s8[16777216]{0:T(1024)(128)(4,1)} %bitcast.222), calls=%async_computation.2 | async-start | bytes 8388608
  400.0 12.4 %slice-start.2 = ((s8[16777216]{0:T(1024)(128)(4,1)}), s8[4194304]{0:T(1024)(128)(4,1)S(1)}, s32[]{:S(2)}) async-start(s8[16777216]{0:T(1024)(128)(4,1)} %bitcast.222), calls=%async_computation.3 | async-start | bytes 8388608
  400.0 12.4 %slice-start.3 = ((s8[16777216]{0:T(1024)(128)(4,1)}), s8[4194304]{0:T(1024)(128)(4,1)S(1)}, s32[]{:S(2)}) async-start(s8[16777216]{0:T(1024)(128)(4,1)} %bitcast.222), calls=%async_computation.4 | async-start | bytes 8388608
  412.3 11.9 %copy-start.83 = (bf16[2048,768]{1,0:T(8,128)(2,1)S(1)}, bf16[2048,768]{1,0:T(8,128)(2,1)}, u32[]{:S(2)}) copy-start(bf16[2048,768]{1,0:T(8,128)(2,1)} %copy-done.82) | copy-start | bytes 9437188
  424.3 11.2 %copy-start.85 = (bf16[2048,768]{1,0:T(8,128)(2,1)S(1)}, bf16[2048,768]{1,0:T(8,128)(2,1)}, u32[]{:S(2)}) copy-start(bf16[2048,768]{1,0:T(8,128)(2,1)} %get-tuple-element.49) | copy-start | bytes 9437188
  444.5 13.8 %copy-start.80 = (bf16[1,2048,768]{2,1,0:T(8,128)(2,1)S(1)}, bf16[1,2048,768]{2,1,0:T(8,128)(2,1)}, u32[]{:S(2)}) copy-start(bf16[1,2048,768]{2,1,0:T(8,128)(2,1)} %param.29) | copy-start | bytes 9437188
  472.0 13.7 %copy-start.24 = (pred[512,512]{0,1:T(8,128)(4,1)S(1)}, pred[512,512]{0,1:T(8,128)(4,1)}, u32[]{:S(2)}) copy-start(pred[512,512]{0,1:T(8,128)(4,1)} %fusion.46) | copy-start | bytes 786436
  597.5 97.5 %copy-start.53 = (s32[128,8]{0,1:T(8,128)S(1)}, s32[128,8]{0,1:T(8,128)}, u32[]{:S(2)}) copy-start(s32[128,8]{0,1:T(8,128)} %param.18) | copy-start | bytes 12292
  597.6 97.5 %copy-start.55 = (f32[128,8]{0,1:T(8,128)S(1)}, f32[128,8]{0,1:T(8,128)}, u32[]{:S(2)}) copy-start(f32[128,8]{0,1:T(8,128)} %copy-done.54) | copy-start | bytes 12292
  597.6 97.5 %copy-start.67 = (f32[128]{0:T(128)S(1)}, f32[128]{0:T(128)}, u32[]{:S(2)}) copy-start(f32[128]{0:T(128)} %copy-done.66) | copy-start | bytes 1540
  597.6 97.6 %copy-start.42 = (f32[128,32]{0,1:T(8,128)S(1)}, f32[128,32]{0,1:T(8,128)}, u32[]{:S(2)}) copy-start(f32[128,32]{0,1:T(8,128)} %copy-done.41) | copy-start | bytes 49156
  597.6 97.6 %copy-start.61 = (f32[128]{0:T(128)S(1)}, f32[128]{0:T(128)}, u32[]{:S(2)}) copy-start(f32[128]{0:T(128)} %copy-done.60) | copy-start | bytes 1540
  597.6 97.6 %copy-start.65 = (f32[128]{0:T(128)S(1)}, f32[128]{0:T(128)}, u32[]{:S(2)}) copy-start(f32[128]{0:T(128)} %copy-done.64) | copy-start | bytes 1540
  597.6 171.9 %copy-start.4 = (f32[128,2048]{1,0:T(8,128)S(1)}, f32[128,2048]{1,0:T(8,128)}, u32[]{:S(2)}) copy-start(f32[128,2048]{1,0:T(8,128)} %copy-done.3) | copy-start | bytes 3145732
  597.6 171.9 %copy-start.36 = (bf16[2048,32]{0,1:T(8,128)(2,1)S(1)}, bf16[2048,32]{0,1:T(8,128)(2,1)}, u32[]{:S(2)}) copy-start(bf16[2048,32]{0,1:T(8,128)(2,1)} %param.27) | copy-start | bytes 393220
  597.6 171.8 %copy-start.50 = (f32[2048]{0:T(1024)S(1)}, f32[2048]{0:T(1024)}, u32[]{:S(2)}) copy-start(f32[2048]{0:T(1024)} %param.24) | copy-start | bytes 24580
  597.6 171.8 %copy-start.63 = (f32[128]{0:T(128)S(1)}, f32[128]{0:T(128)}, u32[]{:S(2)}) copy-start(f32[128]{0:T(128)} %copy-done.62) | copy-start | bytes 1540
  597.7 173.6 %copy-start.15 = (bf16[128,2048]{1,0:T(8,128)(2,1)S(1)}, bf16[128,2048]{1,0:T(8,128)(2,1)}, u32[]{:S(2)}) copy-start(bf16[128,2048]{1,0:T(8,128)(2,1)} %refs_1_.1) | copy-start | bytes 1572868
  771.2 39.9 %copy-start.13 = (f32[128,2048]{1,0:T(8,128)}, f32[128,2048]{1,0:T(8,128)S(1)}, u32[]{:S(2)}) copy-start(f32[128,2048]{1,0:T(8,128)S(1)} %get-tuple-element.83) | copy-start | bytes 3145732
  805.8 5.4 copy-start.25
  805.8 5.4 copy-start.33
  817.9 5.4 copy-start.38
  817.9 5.4 copy-start.40
  825.6 4.9 slice-start.6
  830.5 4.2 copy-start.26
  839.5 78.0 %copy-start.11 = (bf16[128,2048]{1,0:T(8,128)(2,1)S(1)}, bf16[128,2048]{1,0:T(8,128)(2,1)}, u32[]{:S(2)}) copy-start(bf16[128,2048]{1,0:T(8,128)(2,1)} %param.16) | copy-start | bytes 1572868
  839.5 78.0 %copy-start.51 = (f32[2048]{0:T(1024)S(1)}, f32[2048]{0:T(1024)}, u32[]{:S(2)}) copy-start(f32[2048]{0:T(1024)} %param.23) | copy-start | bytes 24580
  839.5 78.0 %copy-start.69 = (f32[128]{0:T(128)S(1)}, f32[128]{0:T(128)}, u32[]{:S(2)}) copy-start(f32[128]{0:T(128)} %copy-done.68) | copy-start | bytes 1540
  913.4 28.0 %copy-start.27 = (bf16[4096,32]{0,1:T(8,128)(2,1)S(1)}, bf16[4096,32]{0,1:T(8,128)(2,1)}, u32[]{:S(2)}) copy-start(bf16[4096,32]{0,1:T(8,128)(2,1)} %all_gather.3) | copy-start | bytes 786436
  941.4 9.7 %copy-start.5 = (f32[128,2048]{1,0:T(8,128)S(1)}, f32[128,2048]{1,0:T(8,128)}, u32[]{:S(2)}) copy-start(f32[128,2048]{1,0:T(8,128)} %copy-done.3) | copy-start | bytes 3145732
  941.4 9.7 %copy-start.12 = (bf16[128,2048]{1,0:T(8,128)(2,1)S(1)}, bf16[128,2048]{1,0:T(8,128)(2,1)}, u32[]{:S(2)}) copy-start(bf16[128,2048]{1,0:T(8,128)(2,1)} %param.16) | copy-start | bytes 1572868
  941.4 9.7 %copy-start.14 = (f32[128,2048]{1,0:T(8,128)S(1)}, f32[128,2048]{1,0:T(8,128)}, u32[]{:S(2)}) copy-start(f32[128,2048]{1,0:T(8,128)} %copy-done.13) | copy-start | bytes 3145732
  941.4 9.7 %copy-start.16 = (bf16[128,2048]{1,0:T(8,128)(2,1)S(1)}, bf16[128,2048]{1,0:T(8,128)(2,1)}, u32[]{:S(2)}) copy-start(bf16[128,2048]{1,0:T(8,128)(2,1)} %refs_1_.1) | copy-start | bytes 1572868
  941.4 9.7 %copy-start.19 = (f32[128,2048]{1,0:T(8,128)S(1)}, f32[128,2048]{1,0:T(8,128)}, u32[]{:S(2)}) copy-start(f32[128,2048]{1,0:T(8,128)} %reduce_outputs.1) | copy-start | bytes 3145732
  941.4 9.7 %copy-start.20 = (f32[128,2048]{1,0:T(8,128)S(1)}, f32[128,2048]{1,0:T(8,128)}, u32[]{:S(2)}) copy-start(f32[128,2048]{1,0:T(8,128)} %get-tuple-element.29) | copy-start | bytes 3145732
  941.4 12.3 %copy-start.1 = (bf16[1,768,2048]{2,1,0:T(8,128)(2,1)S(1)}, bf16[1,768,2048]{2,1,0:T(8,128)(2,1)}, u32[]{:S(2)}) copy-start(bf16[1,768,2048]{2,1,0:T(8,128)(2,1)} %param.30) | copy-start | bytes 9437188
  (31 other events, 42.7 us)

commit v2 on v1

--- a/solution.py
+++ b/solution.py
@@ -26,8 +26,6 @@
         self.x = self.dp + 2 - 4 * along_x
         self.y = self.dp + 4 - 8 * along_y
         self.columns = (self.dp, self.x, self.y, self.x + self.y - self.dp)
-        self.has_up = self.z < length - 1
-        self.has_down = self.z > 0
 
     def device(self, kind):
         if kind == "x":
@@ -40,8 +38,33 @@
             return (self.dp, self.z + 1)
         return (self.dp, self.z - 1)
 
+    @property
+    def has_up(self):
+        return self.z < self.length - 1
+
+    @property
+    def has_down(self):
+        return self.z > 0
+
     def condition(self, kind):
-        return {"up": self.has_up, "down": self.has_down}.get(kind)
+        if kind == "up":
+            return self.has_up
+        return self.has_down if kind == "down" else None
+
+    def nearest(self, turn):
+        length = self.length
+
+        def equal(left, right):
+            far = 2 * length
+            return (left - right + far) // far - (left - right - 1 + far) // far
+
+        found = 0
+        for mine in range(length):
+            order = sorted(range(length), key=lambda other: (abs(other - mine), other))
+            for step, other in enumerate(order):
+                if other:
+                    found = found + equal(self.z, mine) * equal(turn, step) * other
+        return found
 
     def target(self, turn):
         length, z = self.length, self.z
@@ -89,7 +112,7 @@
         self.place = place
         self.started = []
 
-    def start(self, kind, views, condition=None):
+    def start(self, kind, views, condition=lambda: None):
         def build():
             source, target, send_sem, recv_sem = views()
             return pltpu.make_async_remote_copy(
@@ -102,15 +125,15 @@
             )
 
         guarded(self.place.condition(kind), lambda: build().start())
-        self.started.append((condition, self.place.condition(kind), build))
+        self.started.append((condition, kind, build))
 
     def drain(self):
-        for outer, inner, build in self.started:
-
-            def finish(inner=inner, build=build):
-                guarded(inner, lambda: build().wait_send())
-
-            guarded(outer, finish)
+        for condition, kind, build in self.started:
+
+            def finish(kind=kind, build=build):
+                guarded(self.place.condition(kind), lambda: build().wait_send())
+
+            guarded(condition(), finish)
 
 
 class GatherItem:
@@ -140,16 +163,16 @@
 
     def turns(self, distance):
         if distance == 0:
-            return [(0, self.z, None, None)]
-        place = self.place
+            return [(0, 0, lambda: None, None)]
+        place, length = self.place, self.length
         return [
-            (2 * distance - 1, self.z - distance, place.z - distance >= 0, "up"),
-            (2 * distance, self.z + distance, place.z + distance < self.length, "down"),
+            (2 * distance - 1, -distance, lambda: place.z >= distance, "up"),
+            (2 * distance, distance, lambda: place.z < length - distance, "down"),
         ]
 
-    def pass_on(self, sends, lane, kind, column, z, turn, h, source=None, condition=None):
-
+    def pass_on(self, sends, lane, kind, column, offset, turn, h, source=None, condition=lambda: None):
         def views():
+            z = self.z + offset
             view = self.slot(column, z, h)
             return (
                 view if source is None else source(h),
@@ -169,12 +192,12 @@
         for h in range(2):
             own = self.own
             if self.over_z:
-                self.pass_on(sends, 0, "up", place.dp, self.z, 0, h, own)
-                self.pass_on(sends, 1, "down", place.dp, self.z, 0, h, own)
+                self.pass_on(sends, 0, "up", place.dp, 0, 0, h, own)
+                self.pass_on(sends, 1, "down", place.dp, 0, 0, h, own)
             if self.over_dp:
-                self.pass_on(sends, 2, "x", place.dp, self.z, 0, h, own)
-                self.pass_on(sends, 3, "y", place.dp, self.z, 0, h, own)
-                self.pass_on(sends, 4, "core", place.dp, self.z, 0, h, own)
+                self.pass_on(sends, 2, "x", place.dp, 0, 0, h, own)
+                self.pass_on(sends, 3, "y", place.dp, 0, 0, h, own)
+                self.pass_on(sends, 4, "core", place.dp, 0, 0, h, own)
         for h in range(2):
             pltpu.make_async_copy(
                 self.own(h), self.slot(place.dp, self.z, h), self.local.at[h]
@@ -184,67 +207,72 @@
         if not self.over_z or distance >= self.length:
             return
         place = self.place
-        for turn, z, condition, onward in self.turns(distance):
-
-            def step(turn=turn, z=z, condition=condition, onward=onward):
+        for turn, offset, condition, onward in self.turns(distance):
+
+            def step(turn=turn, offset=offset, condition=condition, onward=onward):
                 for h in range(2):
-                    self.arrived(place.dp, z, h)
+                    self.arrived(place.dp, self.z + offset, h)
                     if distance < self.length - 1:
                         self.pass_on(
-                            sends, 0 if onward == "up" else 1, onward, place.dp, z, turn, h,
+                            sends, 0 if onward == "up" else 1, onward, place.dp, offset, turn, h,
                             condition=condition,
                         )
                     if self.over_dp:
                         for lane, kind in ((2, "x"), (3, "y"), (4, "core")):
                             self.pass_on(
-                                sends, lane, kind, place.dp, z, turn, h, condition=condition
+                                sends, lane, kind, place.dp, offset, turn, h, condition=condition
                             )
 
-            guarded(condition, step)
+            guarded(condition(), step)
 
     def across(self, sends, distance):
         if not self.over_dp or not 0 <= distance < self.length:
             return
         _, x, y, _ = self.place.columns
-        for turn, z, condition, _ in self.turns(distance):
-
-            def step(turn=turn, z=z, condition=condition):
+        for turn, offset, condition, _ in self.turns(distance):
+
+            def step(turn=turn, offset=offset, condition=condition):
                 for h in range(2):
-                    self.arrived(x, z, h)
+                    self.arrived(x, self.z + offset, h)
                     if h == 0:
-                        self.pass_on(sends, 5, "y", x, z, turn, h, condition=condition)
-                    self.pass_on(sends, 7, "core", x, z, turn, h, condition=condition)
-                    self.arrived(y, z, h)
+                        self.pass_on(sends, 5, "y", x, offset, turn, h, condition=condition)
+                    self.pass_on(sends, 7, "core", x, offset, turn, h, condition=condition)
+                    self.arrived(y, self.z + offset, h)
                     if h == 1:
-                        self.pass_on(sends, 6, "x", y, z, turn, h, condition=condition)
-                    self.pass_on(sends, 8, "core", y, z, turn, h, condition=condition)
-
-            guarded(condition, step)
+                        self.pass_on(sends, 6, "x", y, offset, turn, h, condition=condition)
+                    self.pass_on(sends, 8, "core", y, offset, turn, h, condition=condition)
+
+            guarded(condition(), step)
 
     def diagonal(self, sends, distance):
         if not self.over_dp or not 0 <= distance < self.length:
             return
         corner = self.place.columns[3]
-        for turn, z, condition, _ in self.turns(distance):
-
-            def step(turn=turn, z=z, condition=condition):
+        for turn, offset, condition, _ in self.turns(distance):
+
+            def step(turn=turn, offset=offset, condition=condition):
                 for h in range(2):
-                    self.arrived(corner, z, h)
-                    self.pass_on(sends, 9, "core", corner, z, turn, h, condition=condition)
-
-            guarded(condition, step)
-
-    def finish(self):
-        place = self.place
+                    self.arrived(corner, self.z + offset, h)
+                    self.pass_on(sends, 9, "core", corner, offset, turn, h, condition=condition)
+
+            guarded(condition(), step)
+
+    def settled(self):
         for h in range(2):
             pltpu.make_async_copy(
-                self.own(h), self.slot(place.dp, self.z, h), self.local.at[h]
+                self.own(h), self.slot(self.place.dp, self.z, h), self.local.at[h]
             ).wait()
+
+    def from_core(self, z):
+        for column in self.place.columns:
+            for h in range(2):
+                self.arrived(column + self.place.to_core, z, h)
+
+    def finish(self):
+        self.settled()
         if self.over_dp:
-            for column in place.columns:
-                for z in range(self.length):
-                    for h in range(2):
-                        self.arrived(column + place.to_core, z, h)
+            for z in range(self.length):
+                self.from_core(z)
 
 
 def run_gather(place, items):
@@ -377,29 +405,32 @@
 
                 lax.fori_loop(0, 2 * (self.length + 1), clear, 0)
 
-    def start(self, sends):
+    def load_all(self):
         place = self.place
-        order = (3, 1, 2, 0) if self.over_dp else (0,)
-        for column in order:
-            for turn in range(self.length):
+        for turn in range(self.length):
+            for column in (3, 1, 2, 0) if self.over_dp else (0,):
                 for h in range(2):
                     pltpu.make_async_copy(
                         self.block(place.columns[column], self.z_of(turn), h),
                         self.acc.at[column, turn, h],
                         self.load.at[column, turn, h],
                     ).start()
-                    if self.over_dp:
-                        sends.start(
-                            "core",
-                            lambda column=column, turn=turn, h=h: (
-                                self.block(
-                                    place.columns[column] + place.to_core, self.z_of(turn), h
-                                ),
-                                self.from_core.at[column, turn, h],
-                                self.send.at[column, turn, h],
-                                self.recv.at[column, turn, h],
-                            ),
-                        )
+
+    def hand_over(self, sends, turn):
+        if not self.over_dp or turn >= self.length:
+            return
+        place = self.place
+        for column in (3, 1, 2, 0):
+            for h in range(2):
+                sends.start(
+                    "core",
+                    lambda column=column, h=h: (
+                        self.block(place.columns[column] + place.to_core, self.z_of(turn), h),
+                        self.from_core.at[column, turn, h],
+                        self.send.at[column, turn, h],
+                        self.recv.at[column, turn, h],
+                    ),
+                )
 
     def settle(self, column, turn, h, extra=(), out=None):
         self.loaded(column, turn, h)
@@ -412,7 +443,7 @@
             self.add(self.acc.at[column, turn, h], refs, out)
 
     def corners(self, sends, turn):
-        if not self.over_dp or turn >= self.length:
+        if not self.over_dp or not 0 <= turn < self.length:
             return
         for h, kind in ((0, "y"), (1, "x")):
             self.settle(3, turn, h)
@@ -427,7 +458,7 @@
             )
 
     def straight(self, sends, turn, second):
-        if not self.over_dp or turn >= self.length:
+        if not self.over_dp or not 0 <= turn < self.length:
             return
         for column, kind in ((1, "x"), (2, "y")):
             h = (column - 1) if second else (2 - column)
@@ -448,7 +479,7 @@
             )
 
     def home(self, sends, turn):
-        if turn >= self.length:
+        if not 0 <= turn < self.length:
             return
         place = self.place
         last = turn == self.length - 1
@@ -501,8 +532,8 @@
                     )
 
                 above, below = z > place.z, z < place.z
-                pl.when(above)(lambda: sends.start("up", going_up, above))
-                pl.when(below)(lambda: sends.start("down", going_down, below))
+                pl.when(above)(lambda: sends.start("up", going_up, lambda: above))
+                pl.when(below)(lambda: sends.start("down", going_down, lambda: below))
 
 
 def run_reduce(place, items):
@@ -511,20 +542,22 @@
     meet(place, any(i.over_z for i in items), any(i.over_dp for i in items))
     sends = Sends(place)
     for item in items:
-        item.start(sends)
+        item.load_all()
+    for turn in range(2):
+        for item in items:
+            item.hand_over(sends, turn)
     longest = max(item.length for item in items)
-    for turn in range(longest):
+    for step in range(longest + 2):
         for item in items:
-            item.corners(sends, turn)
-    for turn in range(longest):
+            item.corners(sends, step)
         for item in items:
-            item.straight(sends, turn, False)
-    for turn in range(longest):
+            item.straight(sends, step, False)
         for item in items:
-            item.straight(sends, turn, True)
-    for turn in range(longest):
+            item.hand_over(sends, step + 2)
         for item in items:
-            item.home(sends, turn)
+            item.straight(sends, step - 1, True)
+        for item in items:
+            item.home(sends, step - 2 if item.over_dp else step)
     sends.drain()
 
 
@@ -575,6 +608,261 @@
             collective_id=collective_id, has_side_effects=True, vmem_limit_bytes=56 << 20
         ),
     )(*[array for array, _, _, _ in specs])
+
+
+def dot(left, right, left_dim=1, right_dim=0):
+    return lax.dot_general(
+        left, right, (((left_dim,), (right_dim,)), ((), ())), preferred_element_type=jnp.float32
+    )
+
+
+def experts(rows_own, cots_own, gates_own, wgate, wup, wdown, length, capacity, collective_id):
+    rows, width = rows_own.shape
+    hidden = wgate.shape[1]
+    devices = 8 * length
+    count = 4 * capacity
+    tile = 512 if width % 512 == 0 else width
+    narrow = 256 if hidden % 256 == 0 else hidden
+    f32, bf16 = jnp.float32, jnp.bfloat16
+
+    def kernel(
+        rows_ref, cots_ref, gates_ref, wg, wu, wd,
+        all_rows, all_cots, part_out, part_grad, token_out, out_wg, out_wu, out_wd,
+        table, row_buf, cot_buf, picked, cotan, gated, hid, dgate, dup, scaled, back,
+        chosen, slot_gate, slot_sum, acc_g, acc_u, acc_d, stage_out, stage_grad,
+        recv_r, send_r, local_r, recv_c, send_c, local_c, recv_t, send_t, local_t,
+        load_sem, store_sem, final_sem,
+    ):
+        place = Place(length)
+        expert = place.dp * length + place.z
+
+        def item_of(source, target, sems, half):
+            item = GatherItem("all", place, None, None, *sems)
+            item.own = lambda h: source.at[pl.ds(h * half, half)]
+            item.slot = lambda column, z, h: target.at[
+                column * length + z, pl.ds(h * half, half)
+            ]
+            return item
+
+        big = [
+            item_of(rows_ref, all_rows, (recv_r, send_r, local_r), rows // 2),
+            item_of(cots_ref, all_cots, (recv_c, send_c, local_c), rows // 2),
+        ]
+        items = [item_of(gates_ref, table, (recv_t, send_t, local_t), gates_ref.shape[0] // 2)] + big
+        meet(place, True, True)
+        sends = Sends(place)
+        for item in items:
+            item.begin(sends)
+
+        def along(distance):
+            for item in items:
+                item.along_z(sends, distance)
+
+        def across(distance):
+            for item in items:
+                item.across(sends, distance)
+
+        def corner(distance):
+            for item in items:
+                item.diagonal(sends, distance)
+
+        def clear(i, carry):
+            at = pl.ds(pl.multiple_of(i * 64, 64), 64)
+            acc_g[at, :] = jnp.zeros((64, hidden), f32)
+            acc_u[at, :] = jnp.zeros((64, hidden), f32)
+            return carry
+
+        def clear_down(i, carry):
+            at = pl.ds(pl.multiple_of(i * 64, 64), 64)
+            acc_d[at, :] = jnp.zeros((64, width), f32)
+            return carry
+
+        lax.fori_loop(0, width // 64, clear, 0)
+        lax.fori_loop(0, hidden // 64, clear_down, 0)
+        along(1)
+        across(0)
+        for item in items:
+            item.settled()
+
+        def block_of(j, side, z):
+            return (place.columns[j] + side * place.to_core) * length + z
+
+        def load(j, side, z, slot):
+            block = block_of(j, side, z)
+            return [
+                pltpu.make_async_copy(all_rows.at[block], row_buf.at[slot, j], load_sem.at[slot, 0, j]),
+                pltpu.make_async_copy(all_cots.at[block], cot_buf.at[slot, j], load_sem.at[slot, 1, j]),
+            ]
+
+        def store(j, side, z, slot):
+            block = block_of(j, side, z)
+            return [
+                pltpu.make_async_copy(stage_out.at[slot, j], part_out.at[block], store_sem.at[slot, 0, j]),
+                pltpu.make_async_copy(stage_grad.at[slot, j], part_grad.at[block], store_sem.at[slot, 1, j]),
+            ]
+
+        order = lax.broadcasted_iota(jnp.int32, (rows, rows), 0)
+        upto = (order <= lax.broadcasted_iota(jnp.int32, (rows, rows), 1)).astype(f32).astype(bf16)
+        slots = lax.broadcasted_iota(jnp.int32, (capacity, rows), 0).astype(f32)
+
+        def unit(i, carry):
+            turn, side = i // 2, i % 2
+            z = place.nearest(turn)
+
+            for step in range(length):
+
+                @pl.when(i == 2 * step)
+                def _(step=step):
+                    along(step + 2)
+                    corner(step)
+                    across(step + 1)
+                    for item in items:
+                        item.from_core(place.nearest(step))
+                    for other in range(2):
+                        for j in range(4):
+                            for copy in load(j, other, place.nearest(step), other):
+                                copy.start()
+
+            @pl.when(i >= 2)
+            def _():
+                for j in range(4):
+                    for copy in store(j, side, z, side):
+                        copy.wait()
+
+            for j in range(4):
+                for copy in load(j, side, z, side):
+                    copy.wait()
+                block = block_of(j, side, z)
+                line = table[block, pl.ds(expert, 1), :]
+                named = line >= 0.0
+                ranks = dot(named.astype(f32).astype(bf16), upto) - 1.0
+                pick = jnp.where(named & (ranks == slots), 1.0, 0.0)
+                gate = jnp.sum(pick * line, axis=1, keepdims=True)
+                chosen[j] = pick.astype(bf16)
+                at = pl.ds(j * capacity, capacity)
+                slot_gate[at, :] = jnp.broadcast_to(gate, (capacity, 128))
+
+                def select(n, carry, j=j, at=at):
+                    lanes = pl.ds(pl.multiple_of(n * tile, tile), tile)
+                    picked[at, lanes] = dot(chosen[j], row_buf[side, j, :, lanes]).astype(bf16)
+                    cot = dot(chosen[j], cot_buf[side, j, :, lanes])
+                    cotan[at, lanes] = cot.astype(bf16)
+                    gated[at, lanes] = (slot_gate[at, 0:1] * cot).astype(bf16)
+                    return carry
+
+                lax.fori_loop(0, width // tile, select, 0)
+
+            def middle(n, carry):
+                lanes = pl.ds(pl.multiple_of(n * narrow, narrow), narrow)
+                gate = dot(picked[...], wg[:, lanes])
+                up = dot(picked[...], wu[:, lanes])
+                grad = dot(gated[...], wd[lanes, :], 1, 1)
+                sigma = jax.nn.sigmoid(gate)
+                hid[:, lanes] = (gate * sigma * up).astype(bf16)
+                dgate[:, lanes] = (grad * up * sigma * (1.0 + gate * (1.0 - sigma))).astype(bf16)
+                dup[:, lanes] = (grad * gate * sigma).astype(bf16)
+                return carry
+
+            lax.fori_loop(0, hidden // narrow, middle, 0)
+            slot_sum[...] = jnp.zeros(slot_sum.shape, f32)
+
+            def outward(n, carry):
+                lanes = pl.ds(pl.multiple_of(n * tile, tile), tile)
+                result = dot(hid[...], wd[:, lanes]).astype(bf16).astype(f32)
+                products = cotan[:, lanes].astype(f32) * result
+                total = products[:, 0:128]
+                for k in range(1, tile // 128):
+                    total = total + products[:, 128 * k : 128 * (k + 1)]
+                slot_sum[...] += total
+                scaled[:, lanes] = (slot_gate[:, 0:1] * result).astype(bf16)
+                back[:, lanes] = (
+                    dot(dgate[...], wg[lanes, :], 1, 1) + dot(dup[...], wu[lanes, :], 1, 1)
+                ).astype(bf16)
+                for j in range(4):
+                    at = pl.ds(j * capacity, capacity)
+                    stage_out[side, j, :, lanes] = dot(chosen[j], scaled[at, lanes], 0, 0).astype(bf16)
+                    stage_grad[side, j, :, lanes] = dot(chosen[j], back[at, lanes], 0, 0).astype(bf16)
+                return carry
+
+            lax.fori_loop(0, width // tile, outward, 0)
+            for j in range(4):
+                for copy in store(j, side, z, side):
+                    copy.start()
+                at = pl.ds(j * capacity, capacity)
+                total = jnp.sum(slot_sum[at, :], axis=1, keepdims=True)
+                token_out[pl.ds(block_of(j, side, z), 1), :] = jnp.sum(
+                    chosen[j].astype(f32) * total, axis=0, keepdims=True
+                )
+
+            def weights(n, carry):
+                lanes = pl.ds(pl.multiple_of(n * tile, tile), tile)
+                acc_g[lanes, :] += dot(picked[:, lanes], dgate[...], 0, 0)
+                acc_u[lanes, :] += dot(picked[:, lanes], dup[...], 0, 0)
+                acc_d[:, lanes] += dot(hid[...], gated[:, lanes], 0, 0)
+                return carry
+
+            lax.fori_loop(0, width // tile, weights, 0)
+            return carry
+
+        lax.fori_loop(0, 2 * length, unit, 0)
+        finals = [
+            pltpu.make_async_copy(source, target, final_sem.at[n])
+            for n, (source, target) in enumerate(
+                ((acc_g, out_wg), (acc_u, out_wu), (acc_d, out_wd))
+            )
+        ]
+        for copy in finals:
+            copy.start()
+        for side in range(2):
+            for j in range(4):
+                for copy in store(j, side, 0, side):
+                    copy.wait()
+        for copy in finals:
+            copy.wait()
+        sends.drain()
+
+    any_spec = pl.BlockSpec(memory_space=pl.ANY)
+    vmem = pl.BlockSpec(memory_space=pltpu.VMEM)
+    big = (devices, rows, width)
+    shape = jax.ShapeDtypeStruct
+    sems = pltpu.SemaphoreType.DMA
+    return pl.pallas_call(
+        kernel,
+        name="experts",
+        out_shape=[
+            shape(big, bf16), shape(big, bf16), shape(big, bf16), shape(big, bf16),
+            shape((devices, rows), f32),
+            shape((width, hidden), f32), shape((width, hidden), f32), shape((hidden, width), f32),
+        ],
+        in_specs=[any_spec] * 3 + [vmem] * 3,
+        out_specs=[any_spec] * 4 + [vmem] + [any_spec] * 3,
+        scratch_shapes=[
+            pltpu.VMEM((devices,) + gates_own.shape, f32),
+            pltpu.VMEM((2, 4, rows, width), bf16),
+            pltpu.VMEM((2, 4, rows, width), bf16),
+            pltpu.VMEM((count, width), bf16),
+            pltpu.VMEM((count, width), bf16),
+            pltpu.VMEM((count, width), bf16),
+            pltpu.VMEM((count, hidden), bf16),
+            pltpu.VMEM((count, hidden), bf16),
+            pltpu.VMEM((count, hidden), bf16),
+            pltpu.VMEM((count, width), bf16),
+            pltpu.VMEM((count, width), bf16),
+            pltpu.VMEM((4, capacity, rows), bf16),
+            pltpu.VMEM((count, 128), f32),
+            pltpu.VMEM((count, 128), f32),
+            pltpu.VMEM((width, hidden), f32),
+            pltpu.VMEM((width, hidden), f32),
+            pltpu.VMEM((hidden, width), f32),
+            pltpu.VMEM((2, 4, rows, width), bf16),
+            pltpu.VMEM((2, 4, rows, width), bf16),
+        ]
+        + GatherItem.semaphores("all", length) * 3
+        + [sems((2, 2, 4)), sems((2, 2, 4)), sems((3,))],
+        compiler_params=pltpu.CompilerParams(
+            collective_id=collective_id, has_side_effects=True, vmem_limit_bytes=63 << 20
+        ),
+    )(rows_own, cots_own, gates_own, wgate, wup, wdown)
 
 
 def mix(form, left, right):
@@ -1029,16 +1317,6 @@
 AXES = ("dp", "tensor")
 
 
-def slots_of(marks, capacity):
-    rows = marks.shape[1]
-    order = jnp.arange(rows, dtype=jnp.int32)
-    upto = (order[:, None] <= order[None, :]).astype(jnp.bfloat16)
-    ranks = jnp.dot(marks.astype(jnp.bfloat16), upto, preferred_element_type=jnp.float32) - 1.0
-    slot = jnp.arange(capacity, dtype=jnp.float32)
-    chosen = (ranks[:, None, :] == slot[None, :, None]) & (marks[:, None, :] > 0.5)
-    return chosen.astype(jnp.bfloat16)
-
-
 def gathered(
     hidden_in,
     segments,
@@ -1060,11 +1338,9 @@
     seg_ids = segments[0]
     rows_dev, width = hidden_in.shape
     top_count = routes.shape[1]
-    experts = router.shape[1]
-    capacity = 2 * rows_dev * top_count // experts
+    expert_count = router.shape[1]
+    capacity = 2 * rows_dev * top_count // expert_count
     length = lax.axis_size("tensor")
-    devices = lax.axis_size("dp") * length
-    expert = lax.axis_index("dp") * length + lax.axis_index("tensor")
     query_cols, key_cols = query_weight.shape[1], key_weight.shape[1]
 
     inputs32 = hidden_in.astype(jnp.float32)
@@ -1099,7 +1375,7 @@
     normed_two = residual * factor_two
     rows_two = (normed_two * gain_moe).astype(jnp.bfloat16)
     router_probs = softmax_rows(jnp.dot(rows_two, router, preferred_element_type=jnp.float32))
-    route_hot = (routes[:, :, None] == jnp.arange(experts, dtype=jnp.int32)[None, None, :]).astype(
+    route_hot = (routes[:, :, None] == jnp.arange(expert_count, dtype=jnp.int32)[None, None, :]).astype(
         jnp.float32
     )
     picked = jnp.sum(route_hot * router_probs[:, None, :], axis=-1)
@@ -1107,49 +1383,20 @@
     gates = picked / total
     named = jnp.sum(route_hot, axis=1)
     gate_table = jnp.where(named > 0.5, jnp.sum(route_hot * gates[:, :, None], axis=1), -1.0)
-    all_rows, all_cots, all_gates = gather(
-        [
-            (rows_two, "all", False),
-            (cotangent, "all", False),
-            (gate_table.T, "all", False),
-        ],
-        length,
-        2,
-        "gather_rows",
-    )
-    own_gates = lax.dynamic_slice_in_dim(all_gates, expert, 1, axis=1)[:, 0, :]
-    marks = (own_gates >= 0.0).astype(jnp.float32)
-    chosen = slots_of(marks, capacity)
-    slot_gates = jnp.sum(chosen.astype(jnp.float32) * own_gates[:, None, :], axis=-1)
-    received = mix("bst,btd->bsd", chosen, all_rows).astype(jnp.bfloat16).reshape(-1, width)
-    cot_slots = mix("bst,btd->bsd", chosen, all_cots).reshape(-1, width)
-    received_grads = (slot_gates.reshape(-1, 1) * cot_slots).astype(jnp.bfloat16)
-    result, gate_pre, up_pre, hidden_units = expert_forward(
-        received, gate_weight[0], up_weight[0], down_weight[0]
-    )
-    grad_expert_rows, grad_wg, grad_wu, grad_wd = expert_backward(
-        received,
-        received_grads,
+    all_rows, _, partial_out, partial_rows, token_grads, grad_wg, grad_wu, grad_wd = experts(
+        rows_two,
+        cotangent,
+        gate_table.T,
         gate_weight[0],
         up_weight[0],
         down_weight[0],
-        gate_pre,
-        up_pre,
-        hidden_units,
-    )
-    result32 = result.astype(jnp.float32)
-    slot_grads = jnp.sum(cot_slots * result32, axis=-1).reshape(devices, capacity)
-    token_grads = jnp.sum(chosen.astype(jnp.float32) * slot_grads[:, :, None], axis=1)
+        length,
+        capacity,
+        2,
+    )
     back_grads = lax.all_to_all(token_grads, AXES, split_axis=0, concat_axis=0, tiled=True)
-    partial_rows = mix(
-        "bst,bsd->btd", chosen, grad_expert_rows.reshape(devices, capacity, width)
-    ).astype(jnp.bfloat16)
     (grad_sum,) = reduce_scatter(
         [(partial_rows.reshape(-1, width), "all", False, jnp.float32)], length, 3, "reduce_grads"
-    )
-    scaled = (slot_gates.reshape(-1, 1) * result32).astype(jnp.bfloat16)
-    partial_out = mix("bst,bsd->btd", chosen, scaled.reshape(devices, capacity, width)).astype(
-        jnp.bfloat16
     )
     (moe_sum,) = reduce_scatter(
         [(partial_out.reshape(-1, width), "all", False, jnp.float32)], length, 4, "reduce_outputs"
@@ -1162,15 +1409,14 @@
     grad_logits = (
         router_probs * (grad_probs - jnp.sum(grad_probs * router_probs, axis=-1, keepdims=True))
     ).astype(jnp.bfloat16)
-    all_logits = lax.all_gather(grad_logits, AXES, axis=0, tiled=True)
-    grad_router = jnp.dot(
-        all_rows.reshape(-1, width).T, all_logits, preferred_element_type=jnp.float32
-    )
     grad_rows_two = grad_sum + jnp.dot(grad_logits, router.T, preferred_element_type=jnp.float32)
     grad_res_norm, grad_gain_moe = row_norm_back(grad_rows_two, normed_two, factor_two, gain_moe)
     grad_residual = cot32 + grad_res_norm
     grad_attn = grad_residual.astype(jnp.bfloat16)
-    (group_grads,) = gather([(grad_attn, "z", False)], length, 5, "gather_grads")
+    group_grads, all_logits = gather(
+        [(grad_attn, "z", False), (grad_logits.T, "all", False)], length, 5, "gather_grads"
+    )
+    grad_router = mix("btd,bet->de", all_rows, all_logits)
     grad_group_rows, grad_joint, grad_wo, grad_qgain, grad_kgain = attn_backward_joint(
         group_grads.reshape(-1, width),
         group_rows,

time: 959 us -> 766 us (0.80)
  matrix products: 217 us -> 53.7 us
  blocking collectives: 74.2 us -> 0 us
  Pallas kernels: 568 us -> 602 us
  starting transfers between devices: 4.31 us -> 27.8 us
  other arithmetic: 53.5 us -> 31.5 us
  local copies, waits for them, and re-layouts: 34.2 us -> 45.9 us
    pallas_call x0 -> x1, Pallas kernels: none -> 215 us  [experts(): pl.pallas_call(kernel, name='experts', out_shape=[shape(big, bf16), shape...]
    pallas_call x4 -> x3, Pallas kernels: 258 us -> 126 us  [gather(): pl.pallas_call(kernel, name=name, out_shape=shapes, in_specs=[pl.BlockSpe...]
    dot_general x11 -> x0, matrix products: 117 us -> none  [the longest x1 15.1 us: expert_backward(): jnp.dot(grad_result, wdown.T, preferred_element_type=jnp.float32)]
    all_gather x1 -> x0, blocking collectives: 74.2 us -> none  [gathered(): all_logits = lax.all_gather(grad_logits, AXES, axis=0, tiled=True)]
    pallas_call x4, Pallas kernels: 310 us -> 260 us  [reduce_scatter(): pl.pallas_call(kernel, name=name, out_shape=shapes, in_specs=[pl.BlockSpe...]
    dot_general x10 -> x7, matrix products: 65.6 us -> 21.2 us  [mix(): return jnp.einsum(form, left, right, preferred_element_type=jnp.float32)]
    all_to_all x1, starting transfers between devices: 4.31 us -> 27.8 us  [gathered(): lax.all_to_all(token_grads, AXES, split_axis=0, concat_axis=0, tiled=True)]
    convert_element_type x2 -> x0, other arithmetic: 21.1 us -> none  [gathered(): (slot_gates.reshape(-1, 1) * cot_slots).astype(jnp.bfloat16)]
  transfers between devices with their start and end apart: 1 -> 1, of which waited for: 0 -> 0; matrix products, arithmetic and copies ran while one was open for 14% -> 2% of each run, Pallas kernels for 20% -> 22%
where the time goes in v2:
time: 766 us; the launch traced here: 763 us
  Pallas kernels  602 us (79%)
  matrix products  53.7 us (7%)
  local copies, waits for them, and re-layouts  45.9 us (6%)
  other arithmetic  31.5 us (4%)
  starting transfers between devices  27.8 us (4%)
    pallas_call x4, Pallas kernels, reduce_scatter(): pl.pallas_call(kernel, name=name, out_shape=shapes, in_specs=[pl.BlockSpe...  260 us
    pallas_call x1, Pallas kernels, experts(): pl.pallas_call(kernel, name='experts', out_shape=[shape(big, bf16), shape...  215 us
    pallas_call x3, Pallas kernels, gather(): pl.pallas_call(kernel, name=name, out_shape=shapes, in_specs=[pl.BlockSpe...  126 us
    all_to_all x1, starting transfers between devices, gathered(): lax.all_to_all(token_grads, AXES, split_axis=0, concat_axis=0, tiled=True)  27.8 us
    dot_general x7, matrix products, mix(): return jnp.einsum(form, left, right, preferred_element_type=jnp.float32)  21.2 us
    unnamed x147, local copies, waits for them, and re-layouts  17.5 us
  transfers between devices with their start and end apart: 1, of which 0 were waited for; matrix products, arithmetic and copies ran while one was open for 2% of the time, Pallas kernels for 22%

profile of v2, /device:TPU:0, one launch (start us, length us, event | category | flops | bytes accessed | tf_op | source)
XLA Modules:
  0.0 762.6 jit_solution(2452369608753769989)
XLA Ops:
  0.7 0.9 convert_reduce_fusion
  1.6 1.0 fusion.31
  2.6 1.3 fusion.28
  3.9 2.0 fusion.22.refs_0_
  6.0 2.0 pad_maximum_fusion.5.refs_1_
  8.0 57.9 %gather_attention.1 = (bf16[4,128,2048]{2,1,0:T(8,128)(2,1)}, bf16[8,256,1280]{2,1,0:T(8,128)(2,1)}, bf16[1024,2048]{1,0:T(8,128)(2,1)}) custom-call(bf16[128,2048]{1,0:T(8,128)(2,1)} %fusion.22.refs_0_, bf16[256,1280]{1,0:T(8,128)(2,1)} %pad_maximum_fusion.5.refs_1_, bf16[1024,256]{1,0:T(8,128)(2,1)} %refs_2_.1), custom_call_target="tpu_custom_call" | custom-call | tf_op jit(solution)/shard_map/gather_attention/pallas_call | solution.py:333
  65.9 4.8 slice_bitcast_fusion
  70.6 1.9 multiply_reduce_fusion.9
  72.5 1.7 fusion.20
  74.3 7.0 copy.59
  81.3 4.6 multiply_reduce_fusion.3
  85.9 0.5 multiply_cosine_fusion
  86.6 0.6 fusion.53
  88.1 1.6 fusion.4
  89.8 1.8 fusion.2
  91.5 1.4 copy-done.2
  93.0 2.7 fusion.14
  95.7 3.7 convolution_convert_fusion.2.refs_0_
  99.4 41.1 %reduce_attention.1 = f32[128,2048]{1,0:T(8,128)} custom-call(bf16[512,2048]{1,0:T(8,128)(2,1)} %convolution_convert_fusion.2.refs_0_), custom_call_target="tpu_custom_call" | custom-call | tf_op jit(solution)/shard_map/reduce_attention/pallas_call | solution.py:600
  140.6 1.4 multiply_reduce_fusion.6
  142.0 0.9 copy-done.3
  143.2 0.8 copy-done.10
  145.4 0.6 select_bitcast_fusion.gates_ref
  146.0 215.1 %experts.1 = (bf16[32,128,2048]{2,1,0:T(8,128)(2,1)}, bf16[32,128,2048]{2,1,0:T(8,128)(2,1)}, bf16[32,128,2048]{2,1,0:T(8,128)(2,1)}, bf16[32,128,2048]{2,1,0:T(...) custom-call(bf16[128,2048]{1,0:T(8,128)(2,1)} %copy-done.10, ...), custom_call_target="tpu_custom_call" | custom-call | tf_op jit(solution)/shard_map/experts/pallas_call | solution.py:829
  361.2 27.8 %all-to-all-start = ((f32[32,1,128]{2,1,0:T(1,128)}), f32[32,1,128]{2,1,0:T(1,128)S(1)}, u32[]{:S(2)}, u32[]{:S(2)}) async-start(f32[32,1,128]{2,1,0:T(1,128)} %bitcast.211), calls=%async_computation | async-start | bytes 32768 | tf_op jit(solution)/shard_map/all_to_all | solution.py:1397
  388.9 0.7 log_add_fusion
  389.7 5.8 fusion.5
  395.5 85.1 %reduce_grads.1 = f32[128,2048]{1,0:T(8,128)} custom-call(bf16[4096,2048]{1,0:T(8,128)(2,1)} %bitcast.175), custom_call_target="tpu_custom_call" | custom-call | tf_op jit(solution)/shard_map/reduce_grads/pallas_call | solution.py:600
  480.6 8.0 %copy.69 = bf16[8,512,512]{2,0,1:T(8,128)(2,1)} copy(bf16[8,512,512]{1,2,0:T(8,128)(2,1)} %fusion.5) | data formatting | bytes 8388608 | tf_op jit(solution)/shard_map/reshape.42
  488.6 83.7 %reduce_outputs.1 = f32[128,2048]{1,0:T(8,128)} custom-call(bf16[4096,2048]{1,0:T(8,128)(2,1)} %bitcast.174), custom_call_target="tpu_custom_call" | custom-call | tf_op jit(solution)/shard_map/reduce_outputs/pallas_call | solution.py:600
  572.5 1.7 multiply_reduce_fusion.4
  574.3 2.2 fusion.63.refs_0_
  576.5 49.2 %gather_grads.1 = (bf16[4,128,2048]{2,1,0:T(8,128)(2,1)}, bf16[32,32,128]{2,1,0:T(8,128)(2,1)}) custom-call(bf16[128,2048]{1,0:T(8,128)(2,1)} %fusion.63.refs_0_, bf16[32,128]{1,0:T(8,128)(2,1)} %bitcast.206), custom_call_target="tpu_custom_call" | custom-call | tf_op jit(solution)/shard_map/gather_grads/pallas_call | solution.py:333
  625.7 6.4 convolution_convert_fusion.1.refs_2_
  632.1 3.3 convolution_convert_fusion.4
  635.5 3.0 copy.66
  638.4 2.2 multiply_reduce_fusion.2
  640.7 5.8 fusion.6
  646.5 0.8 multiply_bitcast_fusion
  647.7 1.4 fusion.18
  649.6 0.7 multiply_reduce_fusion
  650.3 0.6 multiply_convert_fusion
  651.0 0.6 fusion.49
  652.1 0.7 copy-done.7
  652.8 0.8 fusion.21
  653.7 4.7 convolution_convert_fusion.refs_1_
  658.4 4.1 convolution_convert_fusion.3.refs_0_
  662.5 50.3 %reduce_weights.1 = (f32[128,2048]{1,0:T(8,128)}, f32[256,1280]{1,0:T(8,128)}, f32[1024,256]{1,0:T(8,128)}) custom-call(bf16[512,2048]{1,0:T(8,128)(2,1)} %convolution_convert_fusion.3.refs_0_, bf16[2048,1280]{1,0:T(8,128)(2,1)} %convolution_convert_fusion.refs_1_, bf16[1024,2048]{1,0:T(8,128)(2,1)} %convolution_convert_fusion.1.refs_2_), custom_call_target="tpu_custom_call" | custom-call | tf_op jit(solution)/shard_map/reduce_weights/pallas_call | solution.py:600
  712.9 1.6 fusion.27
  714.6 0.6 pad.4.refs_0_
  715.2 19.3 %gather_small.1 = f32[32,48,128]{2,1,0:T(8,128)} custom-call(f32[48,128]{1,0:T(8,128)} %pad.4.refs_0_), custom_call_target="tpu_custom_call" | custom-call | tf_op jit(solution)/shard_map/gather_small/pallas_call | solution.py:333
  734.5 1.2 reduce_sum.252
  735.7 0.6 slice_bitcast_fusion.1
  736.3 0.5 slice_bitcast_fusion.3
  736.8 2.3 slice.77
  739.1 1.7 fusion.64
  740.9 8.2 %convolution_bitcast_fusion = f32[2048,32]{0,1:T(8,128)} fusion(bf16[32,32,128]{2,1,0:T(8,128)(2,1)S(1)} %copy-done.28, bf16[32,128,2048]{2,1,0:T(8,128)(2,1)} %get-tuple-element.39), kind=kOutput, calls=%fused_computation.21 | convolution fusion | flops 536870912 | bytes 17301504 | tf_op jit(solution)/shard_map/btd,bet->de/dot_general | solution.py:869
  749.1 1.7 fusion.26
  750.8 1.0 copy.88
  751.8 3.2 copy.89
  755.0 3.2 copy.90
  758.2 0.9 slice-done
  759.0 0.7 slice-done.1
  759.7 2.7 copy.91
  (172 shorter events, 4.3 us)
Async XLA Ops:
  0.6 143.3 %copy-start = (bf16[2048,32]{0,1:T(8,128)(2,1)S(1)}, bf16[2048,32]{0,1:T(8,128)(2,1)}, u32[]{:S(2)}) copy-start(bf16[2048,32]{0,1:T(8,128)(2,1)} %param.27) | copy-start | bytes 393220
  0.7 85.9 %copy-start.52 = (f32[64]{0:T(128)}, f32[64]{0:T(128)S(1)}, u32[]{:S(2)}) copy-start(f32[64]{0:T(128)S(1)} %negate_power_fusion) | copy-start | bytes 772
  2.6 88.9 %copy-start.14 = (pred[512,512]{0,1:T(8,128)(4,1)}, pred[512,512]{0,1:T(8,128)(4,1)S(1)}, u32[]{:S(2)}) copy-start(pred[512,512]{0,1:T(8,128)(4,1)S(1)} %fusion.31) | copy-start | bytes 786436
  3.9 61.9 %copy-start.50 = (f32[128]{0:T(128)}, f32[128]{0:T(128)S(1)}, u32[]{:S(2)}) copy-start(f32[128]{0:T(128)S(1)} %add_rsqrt_fusion.3) | copy-start | bytes 1540
  65.8 4.8 copy-start.16
  74.3 17.2 %copy-start.61 = (bf16[512,128,1]{1,0,2:T(8,128)(2,1)}, bf16[512,128,1]{1,0,2:T(8,128)(2,1)S(1)}, u32[]{:S(2)}) copy-start(bf16[512,128,1]{1,0,2:T(8,128)(2,1)S(1)} %fusion.20) | copy-start | bytes 393220
  81.3 5.2 copy-start.54
  81.3 5.9 copy-start.56
  85.8 2.2 copy-start.5
  85.9 2.2 copy-start.40
  85.9 2.2 copy-start.38
  86.5 1.6 copy-start.18
  86.5 1.6 copy-start.20
  87.2 2.6 copy-start.29
  87.2 2.6 copy-start.31
  88.1 1.6 copy-start.24
  88.1 1.6 copy-start.26
  89.8 3.2 copy-start.2
  93.0 2.7 copy-start.36
  93.0 2.7 copy-start.58
  95.7 3.7 copy-start.22
  95.7 44.8 %copy-start.8 = (bf16[128,2048]{1,0:T(8,128)(2,1)S(1)}, bf16[128,2048]{1,0:T(8,128)(2,1)}, u32[]{:S(2)}) copy-start(bf16[128,2048]{1,0:T(8,128)(2,1)} %param.16) | copy-start | bytes 1572868
  99.4 43.6 %copy-start.33 = (f32[2048]{0:T(1024)S(1)}, f32[2048]{0:T(1024)}, u32[]{:S(2)}) copy-start(f32[2048]{0:T(1024)} %param.24) | copy-start | bytes 24580
  99.4 45.9 %copy-start.37 = (s32[128,8]{0,1:T(8,128)S(1)}, s32[128,8]{0,1:T(8,128)}, u32[]{:S(2)}) copy-start(s32[128,8]{0,1:T(8,128)} %param.18) | copy-start | bytes 12292
  361.2 211.2 %all-to-all-start = ((f32[32,1,128]{2,1,0:T(1,128)}), f32[32,1,128]{2,1,0:T(1,128)S(1)}, u32[]{:S(2)}, u32[]{:S(2)}) async-start(f32[32,1,128]{2,1,0:T(1,128)} %bitcast.211), calls=%async_computation | async-start | bytes 32768 | tf_op jit(solution)/shard_map/all_to_all | solution.py:1397
  488.6 83.8 %copy-start.49 = (f32[128]{0:T(128)S(1)}, f32[128]{0:T(128)}, u32[]{:S(2)}) copy-start(f32[128]{0:T(128)} %copy-done.48) | copy-start | bytes 1540
  488.6 83.8 %copy-start.43 = (f32[128]{0:T(128)S(1)}, f32[128]{0:T(128)}, u32[]{:S(2)}) copy-start(f32[128]{0:T(128)} %copy-done.42) | copy-start | bytes 1540
  488.6 83.9 %copy-start.47 = (f32[128]{0:T(128)S(1)}, f32[128]{0:T(128)}, u32[]{:S(2)}) copy-start(f32[128]{0:T(128)} %copy-done.46) | copy-start | bytes 1540
  488.6 83.9 %copy-start.4 = (f32[128,2048]{1,0:T(8,128)S(1)}, f32[128,2048]{1,0:T(8,128)}, u32[]{:S(2)}) copy-start(f32[128,2048]{1,0:T(8,128)} %copy-done.3) | copy-start | bytes 3145732
  488.6 83.9 %copy-start.45 = (f32[128]{0:T(128)S(1)}, f32[128]{0:T(128)}, u32[]{:S(2)}) copy-start(f32[128]{0:T(128)} %copy-done.44) | copy-start | bytes 1540
  572.5 3.9 copy-start.35
  625.7 6.4 copy-start.59
  625.7 6.4 copy-start.60
  635.5 5.2 copy-start.15
  635.5 5.2 copy-start.62
  640.7 5.8 copy-start.30
  640.7 5.8 copy-start.32
  647.7 1.5 copy-start.19
  647.7 1.5 copy-start.21
  647.7 1.8 copy-start.6
  647.7 1.8 copy-start.57
  649.5 1.5 copy-start.41
  649.5 1.5 copy-start.53
  649.5 2.0 copy-start.39
  649.5 2.0 copy-start.55
  650.3 1.5 copy-start.12
  650.3 2.5 copy-start.7
  651.7 2.0 copy-start.17
  652.8 5.6 slice-start.6
  653.7 4.7 slice-start.7
  662.5 50.4 %copy-start.34 = (f32[2048]{0:T(1024)S(1)}, f32[2048]{0:T(1024)}, u32[]{:S(2)}) copy-start(f32[2048]{0:T(1024)} %param.23) | copy-start | bytes 24580
  662.5 50.4 %copy-start.51 = (f32[128]{0:T(128)S(1)}, f32[128]{0:T(128)}, u32[]{:S(2)}) copy-start(f32[128]{0:T(128)} %copy-done.50) | copy-start | bytes 1540
  712.9 27.9 %copy-start.28 = (bf16[32,32,128]{2,1,0:T(8,128)(2,1)S(1)}, bf16[32,32,128]{2,1,0:T(8,128)(2,1)}, u32[]{:S(2)}) copy-start(bf16[32,32,128]{2,1,0:T(8,128)(2,1)} %get-tuple-element.40) | copy-start | bytes 786436
  740.8 10.9 %slice-start.4 = ((s8[6291456]{0:T(1024)(128)(4,1)}), s8[4194304]{0:T(1024)(128)(4,1)S(1)}, s32[]{:S(2)}) async-start(s8[6291456]{0:T(1024)(128)(4,1)} %bitcast.183), calls=%async_computation.5 | async-start | bytes 8388608
  740.8 8.2 %copy-start.9 = (bf16[128,2048]{1,0:T(8,128)(2,1)S(1)}, bf16[128,2048]{1,0:T(8,128)(2,1)}, u32[]{:S(2)}) copy-start(bf16[128,2048]{1,0:T(8,128)(2,1)} %cots_ref.1) | copy-start | bytes 1572868
  740.8 8.2 %copy-start.11 = (f32[128,2048]{1,0:T(8,128)S(1)}, f32[128,2048]{1,0:T(8,128)}, u32[]{:S(2)}) copy-start(f32[128,2048]{1,0:T(8,128)} %reduce_outputs.1) | copy-start | bytes 3145732
  740.8 8.2 %copy-start.13 = (f32[128,2048]{1,0:T(8,128)S(1)}, f32[128,2048]{1,0:T(8,128)}, u32[]{:S(2)}) copy-start(f32[128,2048]{1,0:T(8,128)} %get-tuple-element.36) | copy-start | bytes 3145732
  740.8 10.9 %slice-start.5 = ((s8[6291456]{0:T(1024)(128)(4,1)}), s8[2097152]{0:T(1024)(128)(4,1)S(1)}, s32[]{:S(2)}) async-start(s8[6291456]{0:T(1024)(128)(4,1)} %bitcast.183), calls=%async_computation.6 | async-start | bytes 4194304
  749.0 1.7 copy-start.23
  749.0 5.9 slice-start.2
  751.8 3.2 slice-start.3
  751.8 7.3 slice-start
  755.0 4.7 slice-start.1
  755.0 7.5 copy-start.1
  (8 other events, 6.6 us)

commit v3 on v2

--- a/solution.py
+++ b/solution.py
@@ -105,6 +105,24 @@
         length = place.length
         count = count + (place.z + length - 1) // length + (2 * length - 2 - place.z) // length
     pl.semaphore_wait(barrier, count)
+
+
+def other_device(place, distance):
+    there = lax.rem(place.dp * place.length + place.z + distance, 8 * place.length)
+    return (there // place.length, lax.rem(there, place.length)), there
+
+
+def meet_all(place):
+    barrier = pltpu.get_barrier_semaphore()
+    others = 8 * place.length - 1
+
+    def greet(n, carry):
+        device, _ = other_device(place, n + 1)
+        pl.semaphore_signal(barrier, 1, device_id=device, device_id_type=MESH)
+        return carry
+
+    lax.fori_loop(0, others, greet, 0)
+    pl.semaphore_wait(barrier, others)
 
 
 class Sends:
@@ -351,14 +369,14 @@
          self.load, self.send, self.recv) = bufs
 
     @staticmethod
-    def scratch(mode, length, rows, width):
+    def scratch(mode, length, rows, width, in_place=False):
         t = length if mode != "dp" else 1
         columns = 4 if mode != "z" else 1
         dp = mode != "z"
         half = (rows // 2, width)
         small = (8, 128)
         return [
-            pltpu.VMEM((columns, t, 2) + half, jnp.bfloat16),
+            pltpu.VMEM(small if in_place else (columns, t, 2) + half, jnp.bfloat16),
             pltpu.VMEM(((columns, t, 2) + half) if dp else small, jnp.bfloat16),
             pltpu.VMEM(((2, t) + half) if dp else small, jnp.bfloat16),
             pltpu.VMEM(((2, t, 2) + half) if dp else small, jnp.bfloat16),
@@ -374,7 +392,17 @@
     def got(self, ref, lane, turn, h):
         pltpu.make_async_copy(ref, ref, self.recv.at[lane, turn, h]).wait()
 
+    computed = False
+    in_place = False
+
+    def partial(self, column, turn, h):
+        if self.in_place:
+            return self.block(self.place.columns[column], self.z_of(turn), h)
+        return self.acc.at[column, turn, h]
+
     def loaded(self, column, turn, h):
+        if self.computed or self.in_place:
+            return
         ref = self.acc.at[column, turn, h]
         pltpu.make_async_copy(ref, ref, self.load.at[column, turn, h]).wait()
 
@@ -440,7 +468,7 @@
             self.got(ref, column, turn, h)
             refs.append(ref)
         if refs or out is not None:
-            self.add(self.acc.at[column, turn, h], refs, out)
+            self.add(self.partial(column, turn, h), refs, out)
 
     def corners(self, sends, turn):
         if not self.over_dp or not 0 <= turn < self.length:
@@ -450,7 +478,7 @@
             sends.start(
                 kind,
                 lambda h=h: (
-                    self.acc.at[3, turn, h],
+                    self.partial(3, turn, h),
                     self.corner.at[h, turn],
                     self.send.at[4, turn, h],
                     self.recv.at[4, turn, h],
@@ -471,7 +499,7 @@
             sends.start(
                 kind,
                 lambda column=column, h=h: (
-                    self.acc.at[column, turn, h],
+                    self.partial(column, turn, h),
                     self.from_xy.at[column - 1, turn, h],
                     self.send.at[4 + column, turn, h],
                     self.recv.at[4 + column, turn, h],
@@ -515,7 +543,7 @@
 
                 def going_up(h=h):
                     return (
-                        self.acc.at[0, turn, h],
+                        self.partial(0, turn, h),
                         self.from_z.at[z, h],
                         self.send.at[7, turn, h],
                         self.recv.at[7, z, h],
@@ -525,7 +553,7 @@
                     arrives = (z - place.z + 1 + self.length) // self.length
                     goal = z + arrives * (self.length - z)
                     return (
-                        self.acc.at[0, turn, h],
+                        self.partial(0, turn, h),
                         self.from_z.at[goal, h],
                         self.send.at[7, turn, h],
                         self.recv.at[7, goal, h],
@@ -536,11 +564,21 @@
                 pl.when(below)(lambda: sends.start("down", going_down, lambda: below))
 
 
-def run_reduce(place, items):
+def advance(item, sends, step):
+    item.corners(sends, step)
+    item.straight(sends, step, False)
+    item.hand_over(sends, step + 2)
+    item.straight(sends, step - 1, True)
+    item.home(sends, step - 2 if item.over_dp else step)
+
+
+def run_reduce(place, items, gathers=()):
     for item in items:
         item.begin()
     meet(place, any(i.over_z for i in items), any(i.over_dp for i in items))
     sends = Sends(place)
+    for item in gathers:
+        item.begin(sends)
     for item in items:
         item.load_all()
     for turn in range(2):
@@ -558,56 +596,49 @@
             item.straight(sends, step - 1, True)
         for item in items:
             item.home(sends, step - 2 if item.over_dp else step)
+        for item in gathers:
+            item.along_z(sends, step + 1)
+            item.across(sends, step)
+            item.diagonal(sends, step - 1)
+    for item in gathers:
+        item.finish()
     sends.drain()
 
 
-def reduce_scatter(specs, length, collective_id, name):
-    count = len(specs)
-    shapes, scratch, dims = [], [], []
-    for array, mode, by_columns, dtype in specs:
-        blocks = {"all": 8 * length, "dp": 8, "z": length}[mode]
-        if by_columns:
-            rows, width = array.shape[0], array.shape[1] // blocks
-        else:
-            rows, width = array.shape[0] // blocks, array.shape[1]
-        dims.append((rows, width))
-        shapes.append(jax.ShapeDtypeStruct((rows, width), dtype))
-        scratch += ReduceItem.scratch(mode, length, rows, width)
-
-    def kernel(*refs):
+def reduce_rows(partials, small, length, collective_id):
+    devices, rows, width = partials.shape
+    half, low = rows // 2, small.shape[0] // 2
+
+    def kernel(source, small_ref, target, small_all, *rest):
         place = Place(length)
-        items = []
-        for number, (array, mode, by_columns, dtype) in enumerate(specs):
-            rows, width = dims[number]
-            source, target = refs[number], refs[count + number]
-            bufs = refs[2 * count + 8 * number : 2 * count + 8 * number + 8]
-            half = rows // 2
-
-            def block(column, z, h, source=source, half=half, rows=rows, width=width, mode=mode, by=by_columns):
-                index = {"all": column * length + z, "dp": column, "z": z}[mode]
-                if by:
-                    return source.at[
-                        pl.ds(h * half, half), pl.ds(pl.multiple_of(index * width, width), width)
-                    ]
-                return source.at[pl.ds(pl.multiple_of(index * rows + h * half, half), half)]
-
-            def out(h, target=target, half=half):
-                return target.at[pl.ds(h * half, half)]
-
-            items.append(ReduceItem(mode, place, block, bufs, out))
-        run_reduce(place, items)
-
+        item = ReduceItem(
+            "all",
+            place,
+            lambda c, z, h: source.at[c * length + z, pl.ds(h * half, half)],
+            rest[:8],
+            lambda h: target.at[pl.ds(h * half, half)],
+        )
+        beside = GatherItem("all", place, None, None, *rest[8:])
+        beside.own = lambda h: small_ref.at[pl.ds(h * low, low)]
+        beside.slot = lambda c, z, h: small_all.at[c * length + z, pl.ds(h * low, low)]
+        run_reduce(place, [item], [beside])
+
+    any_spec = pl.BlockSpec(memory_space=pl.ANY)
     return pl.pallas_call(
         kernel,
-        name=name,
-        out_shape=shapes,
-        in_specs=[pl.BlockSpec(memory_space=pl.ANY)] * count,
-        out_specs=[pl.BlockSpec(memory_space=pltpu.VMEM)] * count,
-        scratch_shapes=scratch,
+        name="reduce_rows",
+        out_shape=[
+            jax.ShapeDtypeStruct((rows, width), jnp.float32),
+            jax.ShapeDtypeStruct((devices,) + small.shape, small.dtype),
+        ],
+        in_specs=[any_spec, any_spec],
+        out_specs=[pl.BlockSpec(memory_space=pltpu.VMEM), any_spec],
+        scratch_shapes=ReduceItem.scratch("all", length, rows, width)
+        + GatherItem.semaphores("all", length),
         compiler_params=pltpu.CompilerParams(
             collective_id=collective_id, has_side_effects=True, vmem_limit_bytes=56 << 20
         ),
-    )(*[array for array, _, _, _ in specs])
+    )(partials, small)
 
 
 def dot(left, right, left_dim=1, right_dim=0):
@@ -616,7 +647,7 @@
     )
 
 
-def experts(rows_own, cots_own, gates_own, wgate, wup, wdown, length, capacity, collective_id):
+def experts(rows_own, all_cots, gates_own, wgate, wup, wdown, length, capacity, collective_id):
     rows, width = rows_own.shape
     hidden = wgate.shape[1]
     devices = 8 * length
@@ -626,12 +657,12 @@
     f32, bf16 = jnp.float32, jnp.bfloat16
 
     def kernel(
-        rows_ref, cots_ref, gates_ref, wg, wu, wd,
-        all_rows, all_cots, part_out, part_grad, token_out, out_wg, out_wu, out_wd,
+        rows_ref, all_cots, gates_ref, wg, wu, wd,
+        all_rows, part_out, part_grad, token_in, out_wg, out_wu, out_wd,
         table, row_buf, cot_buf, picked, cotan, gated, hid, dgate, dup, scaled, back,
-        chosen, slot_gate, slot_sum, acc_g, acc_u, acc_d, stage_out, stage_grad,
-        recv_r, send_r, local_r, recv_c, send_c, local_c, recv_t, send_t, local_t,
-        load_sem, store_sem, final_sem,
+        chosen, slot_gate, slot_sum, acc_g, acc_u, acc_d, stage_out, stage_grad, token_out,
+        recv_r, send_r, local_r, recv_t, send_t, local_t,
+        load_sem, store_sem, final_sem, token_sem,
     ):
         place = Place(length)
         expert = place.dp * length + place.z
@@ -646,10 +677,9 @@
 
         big = [
             item_of(rows_ref, all_rows, (recv_r, send_r, local_r), rows // 2),
-            item_of(cots_ref, all_cots, (recv_c, send_c, local_c), rows // 2),
         ]
         items = [item_of(gates_ref, table, (recv_t, send_t, local_t), gates_ref.shape[0] // 2)] + big
-        meet(place, True, True)
+        meet_all(place)
         sends = Sends(place)
         for item in items:
             item.begin(sends)
@@ -790,9 +820,8 @@
                     copy.start()
                 at = pl.ds(j * capacity, capacity)
                 total = jnp.sum(slot_sum[at, :], axis=1, keepdims=True)
-                token_out[pl.ds(block_of(j, side, z), 1), :] = jnp.sum(
-                    chosen[j].astype(f32) * total, axis=0, keepdims=True
-                )
+                sums = jnp.sum(chosen[j].astype(f32) * total, axis=0, keepdims=True)
+                token_out[block_of(j, side, z)] = jnp.broadcast_to(sums, (8, rows))
 
             def weights(n, carry):
                 lanes = pl.ds(pl.multiple_of(n * tile, tile), tile)
@@ -813,6 +842,24 @@
         ]
         for copy in finals:
             copy.start()
+
+        def token_send(n):
+            device, there = other_device(place, n + 1)
+            return pltpu.make_async_remote_copy(
+                src_ref=token_out.at[there],
+                dst_ref=token_in.at[expert],
+                send_sem=token_sem.at[0],
+                recv_sem=token_sem.at[1],
+                device_id=device,
+                device_id_type=MESH,
+            )
+
+        def send(n, carry):
+            token_send(n).start()
+            return carry
+
+        lax.fori_loop(0, devices - 1, send, 0)
+        pltpu.make_async_copy(token_out.at[expert], token_in.at[expert], token_sem.at[1]).start()
         for side in range(2):
             for j in range(4):
                 for copy in store(j, side, 0, side):
@@ -820,6 +867,9 @@
         for copy in finals:
             copy.wait()
         sends.drain()
+        pltpu.make_async_copy(token_out, token_in, token_sem.at[1]).wait()
+        sent = token_out.at[pl.ds(0, devices - 1)]
+        pltpu.make_async_copy(sent, sent, token_sem.at[0]).wait()
 
     any_spec = pl.BlockSpec(memory_space=pl.ANY)
     vmem = pl.BlockSpec(memory_space=pltpu.VMEM)
@@ -830,12 +880,12 @@
         kernel,
         name="experts",
         out_shape=[
-            shape(big, bf16), shape(big, bf16), shape(big, bf16), shape(big, bf16),
-            shape((devices, rows), f32),
+            shape(big, bf16), shape(big, bf16), shape(big, bf16),
+            shape((devices, 8, rows), f32),
             shape((width, hidden), f32), shape((width, hidden), f32), shape((hidden, width), f32),
         ],
         in_specs=[any_spec] * 3 + [vmem] * 3,
-        out_specs=[any_spec] * 4 + [vmem] + [any_spec] * 3,
+        out_specs=[any_spec] * 3 + [vmem] + [any_spec] * 3,
         scratch_shapes=[
             pltpu.VMEM((devices,) + gates_own.shape, f32),
             pltpu.VMEM((2, 4, rows, width), bf16),
@@ -856,13 +906,448 @@
             pltpu.VMEM((hidden, width), f32),
             pltpu.VMEM((2, 4, rows, width), bf16),
             pltpu.VMEM((2, 4, rows, width), bf16),
+            pltpu.VMEM((devices, 8, rows), f32),
         ]
-        + GatherItem.semaphores("all", length) * 3
-        + [sems((2, 2, 4)), sems((2, 2, 4)), sems((3,))],
+        + GatherItem.semaphores("all", length) * 2
+        + [sems((2, 2, 4)), sems((2, 2, 4)), sems((3,)), sems((2,))],
         compiler_params=pltpu.CompilerParams(
             collective_id=collective_id, has_side_effects=True, vmem_limit_bytes=63 << 20
         ),
-    )(rows_own, cots_own, gates_own, wgate, wup, wdown)
+    )(rows_own, all_cots, gates_own, wgate, wup, wdown)
+
+
+def rope(values, cosine, sine):
+    return values * cosine + pltpu.roll(values, values.shape[-1] // 2, 1) * sine
+
+
+def unrope(values, cosine, sine):
+    return values * cosine - pltpu.roll(values, values.shape[-1] // 2, 1) * sine
+
+
+def row_factor(values):
+    return lax.rsqrt(jnp.mean(values * values, axis=-1, keepdims=True) + EPSILON)
+
+
+def visible_pairs(seg_col, seg_row, start, stop, reach):
+    shape = (stop - start, reach)
+    query = lax.broadcasted_iota(jnp.int32, shape, 0) + start
+    key = lax.broadcasted_iota(jnp.int32, shape, 1)
+    return (seg_col[start:stop, :] == seg_row[:, 0:reach]) & (key <= query)
+
+
+def attend(rows_own, joint_own, output_own, cots_own, seg_col, seg_row, cosine, sine, query_gain, key_gain, length, collective_id):
+    rows, width = rows_own.shape
+    depth, joint = joint_own.shape
+    head_width, part = output_own.shape
+    head = query_gain.shape[-1]
+    heads = head_width // head
+    tokens = rows * length
+    block = tokens // 2
+    tile = 512
+    scale = 1.0 / math.sqrt(head)
+    f32, bf16 = jnp.float32, jnp.bfloat16
+
+    def kernel(
+        rows_ref, joint_ref, output_ref, cots_ref, segc, segr, cos_ref, sin_ref, qgain, kgain,
+        out_add, out_rows, out_joint, out_weight, out_cots, out_qkv, out_heads,
+        rows_v, joint_v, weight_v, qkv, att, key_v, value_v,
+        r0, r1, r2, r3, r4, r5, r6, r7,
+        g0, g1, g2, j0, j1, j2, w0, w1, w2, c0, c1, c2, save_sem,
+    ):
+        place = Place(length)
+
+        def item_of(mode, source, half, slot, sems):
+            item = GatherItem(mode, place, None, None, *sems)
+            item.own = lambda h: source.at[pl.ds(h * half, half)]
+            item.slot = slot
+            return item
+
+        half, deep, tall = rows // 2, depth // 2, head_width // 2
+        own_rows = item_of(
+            "z", rows_ref, half, lambda c, z, h: rows_v.at[z, pl.ds(h * half, half)], (g0, g1, g2)
+        )
+        own_joint = item_of(
+            "dp", joint_ref, deep, lambda c, z, h: joint_v.at[c, pl.ds(h * deep, deep)], (j0, j1, j2)
+        )
+        own_weight = item_of(
+            "dp",
+            output_ref,
+            tall,
+            lambda c, z, h: weight_v.at[
+                pl.ds(h * tall, tall), pl.ds(pl.multiple_of(c * part, part), part)
+            ],
+            (w0, w1, w2),
+        )
+        cots = item_of(
+            "all",
+            cots_ref,
+            half,
+            lambda c, z, h: out_cots.at[c * length + z, pl.ds(h * half, half)],
+            (c0, c1, c2),
+        )
+        total = ReduceItem(
+            "z", place, None, (r0, r1, r2, r3, r4, r5, r6, r7),
+            lambda h: out_add.at[pl.ds(h * half, half)],
+        )
+        total.computed = True
+        total.begin()
+        meet(place, True, True)
+        sends = Sends(place)
+        own_joint.begin(sends)
+        own_rows.begin(sends)
+        own_weight.begin(sends)
+        own_joint.across(sends, 0)
+        own_rows.along_z(sends, 1)
+        own_weight.across(sends, 0)
+        own_joint.diagonal(sends, 0)
+        own_rows.along_z(sends, 2)
+        own_weight.diagonal(sends, 0)
+        for distance in range(3, length):
+            own_rows.along_z(sends, distance)
+        cots.begin(sends)
+        own_joint.finish()
+        own_rows.finish()
+
+        def projection(n, carry):
+            lanes = pl.ds(pl.multiple_of(n * 256, 256), 256)
+            left = rows_v[...].reshape(tokens, width)
+            right = joint_v[:, :, lanes].reshape(width, 256)
+            qkv[:, lanes] = dot(left, right)
+            return carry
+
+        lax.fori_loop(0, joint // 256, projection, 0)
+        saves = [
+            pltpu.make_async_copy(source, target, save_sem.at[n])
+            for n, (source, target) in enumerate(
+                ((rows_v, out_rows), (joint_v, out_joint), (qkv, out_qkv), (weight_v, out_weight), (att, out_heads))
+            )
+        ]
+        for copy in saves[:3]:
+            copy.start()
+        key = qkv[:, head_width : head_width + head]
+        key_v[...] = rope(key * row_factor(key) * kgain[...], cos_ref[...], sin_ref[...]).astype(bf16)
+        value_v[...] = qkv[:, head_width + head : head_width + 2 * head].astype(bf16)
+
+        def one_head(n, carry):
+            lanes = pl.ds(pl.multiple_of(n * head, head), head)
+            for start in range(0, tokens, block):
+                stop = start + block
+                query = qkv[start:stop, lanes]
+                turned = rope(
+                    query * row_factor(query) * qgain[...], cos_ref[start:stop, :], sin_ref[start:stop, :]
+                ).astype(bf16)
+                scores = dot(turned, key_v[0:stop, :], 1, 1) * scale
+                seen = visible_pairs(segc, segr, start, stop, stop)
+                scores = jnp.where(seen, scores, NEG_BIG)
+                top = jnp.max(scores, axis=-1, keepdims=True)
+                powers = jnp.exp(scores - top)
+                probs = (powers / jnp.sum(powers, axis=-1, keepdims=True)).astype(bf16)
+                att[start:stop, lanes] = dot(probs, value_v[0:stop, :]).astype(bf16)
+            return carry
+
+        lax.fori_loop(0, heads // 2, one_head, 0)
+        cots.along_z(sends, 1)
+        cots.across(sends, 0)
+        lax.fori_loop(heads // 2, heads, one_head, 0)
+        saves[4].start()
+        own_weight.finish()
+        saves[3].start()
+
+        def outward(turn):
+            z = total.z_of(turn)
+
+            def body(n, carry):
+                lanes = pl.ds(pl.multiple_of(n * tile, tile), tile)
+                left = att[pl.ds(pl.multiple_of(z * rows, rows), rows), :]
+                found = dot(left, weight_v[:, lanes]).astype(bf16)
+                for h in range(2):
+                    total.acc[0, turn, h, :, lanes] = found[h * half : (h + 1) * half, :]
+                return carry
+
+            lax.fori_loop(0, width // tile, body, 0)
+
+        for turn in range(length):
+            outward(turn)
+            total.home(sends, turn)
+            cots.along_z(sends, turn + 2)
+            cots.diagonal(sends, turn)
+            cots.across(sends, turn + 1)
+        cots.finish()
+        for copy in saves:
+            copy.wait()
+        sends.drain()
+
+    any_spec = pl.BlockSpec(memory_space=pl.ANY)
+    vmem = pl.BlockSpec(memory_space=pltpu.VMEM)
+    shape = jax.ShapeDtypeStruct
+    return pl.pallas_call(
+        kernel,
+        name="attend",
+        out_shape=[
+            shape((rows, width), f32),
+            shape((length, rows, width), bf16),
+            shape((8, depth, joint), bf16),
+            shape((head_width, 8 * part), bf16),
+            shape((8 * length, rows, width), bf16),
+            shape((tokens, joint), f32),
+            shape((tokens, head_width), bf16),
+        ],
+        in_specs=[any_spec] * 4 + [vmem] * 6,
+        out_specs=[vmem] + [any_spec] * 6,
+        scratch_shapes=[
+            pltpu.VMEM((length, rows, width), bf16),
+            pltpu.VMEM((8, depth, joint), bf16),
+            pltpu.VMEM((head_width, 8 * part), bf16),
+            pltpu.VMEM((tokens, joint), f32),
+            pltpu.VMEM((tokens, head_width), bf16),
+            pltpu.VMEM((tokens, head), bf16),
+            pltpu.VMEM((tokens, head), bf16),
+        ]
+        + ReduceItem.scratch("z", length, rows, width)
+        + GatherItem.semaphores("z", length)
+        + GatherItem.semaphores("dp", length) * 2
+        + GatherItem.semaphores("all", length)
+        + [pltpu.SemaphoreType.DMA((5,))],
+        compiler_params=pltpu.CompilerParams(
+            collective_id=collective_id, has_side_effects=True, vmem_limit_bytes=56 << 20
+        ),
+    )(rows_own, joint_own, output_own, cots_own, seg_col, seg_row, cosine, sine, query_gain, key_gain)
+
+
+def attend_back(grad_own, rows_all, joint_all, output_all, qkv_all, heads_all, part_out, seg_col, seg_row, cosine, sine, query_gain, key_gain, length, collective_id):
+    rows, width = grad_own.shape
+    _, depth, joint = joint_all.shape
+    head_width = output_all.shape[0]
+    part = width // 8
+    head = query_gain.shape[-1]
+    heads = head_width // head
+    tokens = rows * length
+    block = tokens // 2
+    scale = 1.0 / math.sqrt(head)
+    f32, bf16 = jnp.float32, jnp.bfloat16
+    half, deep, tall = rows // 2, depth // 2, head_width // 2
+
+    def kernel(
+        grad_ref, rows_ref, joint_ref, output_ref, qkv_ref, heads_ref, part_ref,
+        segc, segr, cos_ref, sin_ref, qgain, kgain,
+        out_rows, out_joint, out_weight, out_moe, out_qgain, out_kgain,
+        grads, joint_v, weight_v, qkv, att, gatt, joint_b, part_w, key_v, value_v, dkey, dvalue,
+        *rest,
+    ):
+        place = Place(length)
+        o_bufs, z_bufs, j_bufs, w_bufs = (rest[8 * n : 8 * n + 8] for n in range(4))
+        gather_sems, load_sem = rest[32:35], rest[35]
+
+        outs = ReduceItem(
+            "all",
+            place,
+            lambda c, z, h: part_ref.at[c * length + z, pl.ds(h * half, half)],
+            o_bufs,
+            lambda h: out_moe.at[pl.ds(h * half, half)],
+        )
+        back = ReduceItem(
+            "z",
+            place,
+            lambda c, z, h: grads.at[z, pl.ds(h * half, half)],
+            z_bufs,
+            lambda h: out_rows.at[pl.ds(h * half, half)],
+        )
+        joints = ReduceItem(
+            "dp",
+            place,
+            lambda c, z, h: joint_v.at[c, pl.ds(h * deep, deep)],
+            j_bufs,
+            lambda h: out_joint.at[pl.ds(h * deep, deep)],
+        )
+        weights = ReduceItem(
+            "dp",
+            place,
+            lambda c, z, h: part_w.at[
+                pl.ds(h * tall, tall), pl.ds(pl.multiple_of(c * part, part), part)
+            ],
+            w_bufs,
+            lambda h: out_weight.at[pl.ds(h * tall, tall)],
+        )
+        for item in (back, joints, weights):
+            item.in_place = True
+        gathers = GatherItem("z", place, None, None, *gather_sems)
+        gathers.own = lambda h: grad_ref.at[pl.ds(h * half, half)]
+        gathers.slot = lambda c, z, h: grads.at[z, pl.ds(h * half, half)]
+
+        outs.begin()
+        back.begin()
+        meet(place, True, True)
+        first, sends = Sends(place), Sends(place)
+        gathers.begin(first)
+        outs.load_all()
+        outs.hand_over(sends, 0)
+        outs.hand_over(sends, 1)
+        loads = [
+            pltpu.make_async_copy(source, target, load_sem.at[n])
+            for n, (source, target) in enumerate(
+                ((output_ref, weight_v), (heads_ref, att), (qkv_ref, qkv), (joint_ref, joint_v))
+            )
+        ]
+        for copy in loads:
+            copy.start()
+        advance(outs, sends, 0)
+        for distance in range(1, length):
+            gathers.along_z(first, distance)
+            if distance < length - 1:
+                advance(outs, sends, distance)
+        gathers.finish()
+        first.drain()
+        for copy in loads[:3]:
+            copy.wait()
+
+        def to_heads(n, carry):
+            lanes = pl.ds(pl.multiple_of(n * 256, 256), 256)
+            left = grads[...].reshape(tokens, width)
+            gatt[:, lanes] = dot(left, weight_v[lanes, :], 1, 1).astype(bf16)
+            return carry
+
+        def to_weight(n, carry):
+            lanes = pl.ds(pl.multiple_of(n * 256, 256), 256)
+            right = grads[:, :, lanes].reshape(tokens, 256)
+            part_w[:, lanes] = dot(att[...], right, 0, 0).astype(bf16)
+            return carry
+
+        lax.fori_loop(0, width // 256, to_weight, 0)
+        weights.hand_over(sends, 0)
+        lax.fori_loop(0, head_width // 256, to_heads, 0)
+        rows_v = weight_v.at[pl.ds(0, tokens)]
+        rows_loads = [
+            pltpu.make_async_copy(
+                rows_ref.at[z], weight_v.at[pl.ds(z * rows, rows)], load_sem.at[4 + z]
+            )
+            for z in range(length)
+        ]
+        for copy in rows_loads:
+            copy.start()
+        advance(weights, sends, 0)
+        key = qkv[:, head_width : head_width + head]
+        key_v[...] = rope(key * row_factor(key) * kgain[...], cos_ref[...], sin_ref[...]).astype(bf16)
+        value_v[...] = qkv[:, head_width + head : head_width + 2 * head].astype(bf16)
+        dkey[...] = jnp.zeros((tokens, head), f32)
+        dvalue[...] = jnp.zeros((tokens, head), f32)
+        out_qgain[...] = jnp.zeros(out_qgain.shape, f32)
+
+        def normed_back(grad, raw, gain, start, stop):
+            factor = row_factor(raw)
+            hat = raw * factor
+            turned = unrope(grad, cos_ref[start:stop, :], sin_ref[start:stop, :])
+            scaled = turned * gain
+            found = factor * (scaled - hat * jnp.mean(scaled * hat, axis=-1, keepdims=True))
+            return found, jnp.sum(turned * hat, axis=0, keepdims=True)
+
+        def one_head(n, carry):
+            lanes = pl.ds(pl.multiple_of(n * head, head), head)
+            for start in range(0, tokens, block):
+                stop = start + block
+                raw = qkv[start:stop, lanes]
+                turned = rope(
+                    raw * row_factor(raw) * qgain[...], cos_ref[start:stop, :], sin_ref[start:stop, :]
+                ).astype(bf16)
+                grad = gatt[start:stop, lanes]
+                delta = jnp.sum(
+                    grad.astype(f32) * att[start:stop, lanes].astype(f32), axis=-1, keepdims=True
+                )
+                scores = dot(turned, key_v[0:stop, :], 1, 1) * scale
+                seen = visible_pairs(segc, segr, start, stop, stop)
+                scores = jnp.where(seen, scores, NEG_BIG)
+                powers = jnp.exp(scores - jnp.max(scores, axis=-1, keepdims=True))
+                probs = powers / jnp.sum(powers, axis=-1, keepdims=True)
+                dprobs = dot(grad, value_v[0:stop, :], 1, 1)
+                dscores = (probs * (dprobs - delta)).astype(bf16)
+                dvalue[0:stop, :] += dot(probs.astype(bf16), grad, 0, 0)
+                dkey[0:stop, :] += dot(dscores, turned, 0, 0) * scale
+                dquery = dot(dscores, key_v[0:stop, :]) * scale
+                found, gain_part = normed_back(dquery, raw, qgain[...], start, stop)
+                joint_b[start:stop, lanes] = found.astype(bf16)
+                out_qgain[...] += gain_part
+            return carry
+
+        lax.fori_loop(0, heads // 2, one_head, 0)
+        advance(outs, sends, length - 1)
+        advance(weights, sends, 1)
+        lax.fori_loop(heads // 2, heads, one_head, 0)
+        found, gain_part = normed_back(
+            dkey[...], qkv[:, head_width : head_width + head], kgain[...], 0, tokens
+        )
+        out_kgain[...] = gain_part
+        joint_b[:, head_width : head_width + head] = found.astype(bf16)
+        joint_b[:, head_width + head : head_width + 2 * head] = dvalue[...].astype(bf16)
+        advance(outs, sends, length)
+        advance(weights, sends, 2)
+        loads[3].wait()
+
+        def to_rows(n, carry):
+            lanes = pl.ds(pl.multiple_of(n * depth, depth), depth)
+            found = dot(joint_b[...], joint_v[n], 1, 1).astype(bf16)
+            grads[:, :, lanes] = found.reshape(length, rows, depth)
+            return carry
+
+        lax.fori_loop(0, 8, to_rows, 0)
+        back.home(sends, 0)
+        for copy in rows_loads:
+            copy.wait()
+
+        def to_joint(n, carry):
+            lanes = pl.ds(pl.multiple_of(n * depth, depth), depth)
+            joint_v[n] = dot(weight_v[0:tokens, lanes], joint_b[...], 0, 0).astype(bf16)
+            return carry
+
+        lax.fori_loop(0, 8, to_joint, 0)
+        joints.hand_over(sends, 0)
+        back.home(sends, 1)
+        advance(joints, sends, 0)
+        for turn in range(2, length):
+            back.home(sends, turn)
+        advance(joints, sends, 1)
+        advance(outs, sends, length + 1)
+        advance(joints, sends, 2)
+        sends.drain()
+
+    any_spec = pl.BlockSpec(memory_space=pl.ANY)
+    vmem = pl.BlockSpec(memory_space=pltpu.VMEM)
+    shape = jax.ShapeDtypeStruct
+    return pl.pallas_call(
+        kernel,
+        name="attend_back",
+        out_shape=[
+            shape((rows, width), f32),
+            shape((depth, joint), f32),
+            shape((head_width, part), f32),
+            shape((rows, width), f32),
+            shape((1, head), f32),
+            shape((1, head), f32),
+        ],
+        in_specs=[any_spec] * 7 + [vmem] * 6,
+        out_specs=[vmem] * 6,
+        scratch_shapes=[
+            pltpu.VMEM((length, rows, width), bf16),
+            pltpu.VMEM((8, depth, joint), bf16),
+            pltpu.VMEM((head_width, width), bf16),
+            pltpu.VMEM((tokens, joint), f32),
+            pltpu.VMEM((tokens, head_width), bf16),
+            pltpu.VMEM((tokens, head_width), bf16),
+            pltpu.VMEM((tokens, joint), bf16),
+            pltpu.VMEM((head_width, width), bf16),
+            pltpu.VMEM((tokens, head), bf16),
+            pltpu.VMEM((tokens, head), bf16),
+            pltpu.VMEM((tokens, head), f32),
+            pltpu.VMEM((tokens, head), f32),
+        ]
+        + ReduceItem.scratch("all", length, rows, width)
+        + ReduceItem.scratch("z", length, rows, width, True)
+        + ReduceItem.scratch("dp", length, depth, joint, True)
+        + ReduceItem.scratch("dp", length, head_width, part, True)
+        + GatherItem.semaphores("z", length)
+        + [pltpu.SemaphoreType.DMA((4 + length,))],
+        compiler_params=pltpu.CompilerParams(
+            collective_id=collective_id, has_side_effects=True, vmem_limit_bytes=67043328
+        ),
+    )(grad_own, rows_all, joint_all, output_all, qkv_all, heads_all, part_out, seg_col, seg_row, cosine, sine, query_gain, key_gain)
 
 
 def mix(form, left, right):
@@ -1254,66 +1739,6 @@
     )
 
 
-def attn_backward_joint(
-    grad_attn, rows, seg_ids, joint_full, wo_full, query_gain, key_gain, saved
-):
-    (
-        attn_heads,
-        lse_all,
-        query_rot,
-        key_rot,
-        value_rows,
-        cosine,
-        sine_table,
-        query_hat,
-        query_factor,
-        key_hat,
-        key_factor,
-    ) = saved
-    length = rows.shape[0]
-    head_dim = query_gain.shape[0]
-    num_heads = query_hat.shape[1]
-    inv_root = 1.0 / math.sqrt(head_dim)
-    block_rows = math.gcd(length, 512)
-    grad_wo = jnp.dot(attn_heads.T, grad_attn, preferred_element_type=jnp.float32)
-    grad_heads = (
-        jnp.dot(grad_attn, wo_full.T, preferred_element_type=jnp.float32)
-        .astype(jnp.bfloat16)
-        .reshape(query_rot.shape)
-    )
-    heads_view = attn_heads.reshape(query_rot.shape)
-    row_delta = jnp.transpose(
-        jnp.sum(grad_heads.astype(jnp.float32) * heads_view.astype(jnp.float32), axis=-1), (1, 2, 0)
-    )
-    row_index = jnp.arange(length, dtype=jnp.int32)
-    scores = mix("qgrd,kgd->grqk", query_rot, key_rot) * inv_root
-    visible = (seg_ids[0:block_rows, None] == seg_ids[None, :]) & (
-        row_index[None, :] <= row_index[0:block_rows, None]
-    )
-    scores = jnp.where(visible, scores, NEG_BIG)
-    prob_f = jnp.where(visible, jnp.exp(scores - lse_all[:, :, 0:block_rows, None]), 0.0)
-    prob_rows = prob_f.astype(jnp.bfloat16)
-    grad_value = mix("grqk,qgrd->kgd", prob_rows, grad_heads)
-    grad_probs = mix("qgrd,kgd->grqk", grad_heads, value_rows)
-    grad_scores = (prob_f * (grad_probs - row_delta[:, :, 0:block_rows, None])).astype(jnp.bfloat16)
-    pieces = mix("grqk,kgd->qgrd", grad_scores, key_rot) * inv_root
-    grad_key_rot = mix("grqk,qgrd->kgd", grad_scores, query_rot) * inv_root
-    grad_query_rot = pieces.reshape(length, num_heads, head_dim)
-    grad_query, grad_qgain = head_norm_back(
-        unrotate(grad_query_rot, cosine, sine_table), query_hat, query_factor, query_gain
-    )
-    grad_key, grad_kgain = head_norm_back(
-        unrotate(grad_key_rot, cosine, sine_table), key_hat, key_factor, key_gain
-    )
-    query_b = grad_query.astype(jnp.bfloat16).reshape(length, -1)
-    key_b = grad_key.astype(jnp.bfloat16).reshape(length, -1)
-    value_b = grad_value.astype(jnp.bfloat16).reshape(length, -1)
-    joint_b = jnp.concatenate([query_b, key_b, value_b], axis=1)
-    grad_rows = jnp.dot(joint_b, joint_full.T, preferred_element_type=jnp.float32)
-    grad_joint = jnp.dot(rows.T, joint_b, preferred_element_type=jnp.float32)
-    return (grad_rows, grad_joint, grad_wo, grad_qgain, grad_kgain)
-
-
 AXES = ("dp", "tensor")
 
 
@@ -1348,27 +1773,17 @@
     normed_one = inputs32 * factor_one
     rows_one = (normed_one * gain_attn).astype(jnp.bfloat16)
     joint_weight = jnp.concatenate([query_weight, key_weight, value_weight], axis=1)
-    group_rows, full_joint, full_output = gather(
-        [
-            (rows_one, "z", False),
-            (joint_weight, "dp", False),
-            (output_weight, "dp", True),
-        ],
-        length,
-        0,
-        "gather_attention",
-    )
-    group_rows = group_rows.reshape(-1, width)
-    full_joint = full_joint.reshape(width, -1)
-    full_query = full_joint[:, :query_cols]
-    full_key = full_joint[:, query_cols : query_cols + key_cols]
-    full_value = full_joint[:, query_cols + key_cols :]
-    saved = attn_forward(
-        group_rows, seg_ids, full_query, full_key, full_value, query_gain, key_gain
-    )
-    partial_add = jnp.dot(saved[0], full_output, preferred_element_type=jnp.float32)
-    (attn_add,) = reduce_scatter(
-        [(partial_add.astype(jnp.bfloat16), "z", False, jnp.float32)], length, 1, "reduce_attention"
+    cosine, sine_table = rope_tables(seg_ids, query_gain.shape[0])
+    turns = (
+        seg_ids[:, None],
+        seg_ids[None, :],
+        jnp.concatenate([cosine, cosine], axis=1),
+        jnp.concatenate([-sine_table, sine_table], axis=1),
+        query_gain[None, :],
+        key_gain[None, :],
+    )
+    attn_add, group_rows, full_joint, full_output, all_cots, projected, attn_heads = attend(
+        rows_one, joint_weight, output_weight, cotangent, *turns, length, 0
     )
     residual = inputs32 + attn_add
     factor_two = rms_scale(residual)
@@ -1383,25 +1798,18 @@
     gates = picked / total
     named = jnp.sum(route_hot, axis=1)
     gate_table = jnp.where(named > 0.5, jnp.sum(route_hot * gates[:, :, None], axis=1), -1.0)
-    all_rows, _, partial_out, partial_rows, token_grads, grad_wg, grad_wu, grad_wd = experts(
+    all_rows, partial_out, partial_rows, token_grads, grad_wg, grad_wu, grad_wd = experts(
         rows_two,
-        cotangent,
+        all_cots,
         gate_table.T,
         gate_weight[0],
         up_weight[0],
         down_weight[0],
         length,
         capacity,
-        2,
-    )
-    back_grads = lax.all_to_all(token_grads, AXES, split_axis=0, concat_axis=0, tiled=True)
-    (grad_sum,) = reduce_scatter(
-        [(partial_rows.reshape(-1, width), "all", False, jnp.float32)], length, 3, "reduce_grads"
-    )
-    (moe_sum,) = reduce_scatter(
-        [(partial_out.reshape(-1, width), "all", False, jnp.float32)], length, 4, "reduce_outputs"
-    )
-    output = (residual + moe_sum).astype(jnp.bfloat16)
+        1,
+    )
+    back_grads = token_grads[:, 0, :]
     cot32 = cotangent.astype(jnp.float32)
     grad_gates = jnp.sum(route_hot * back_grads.T[:, None, :], axis=-1)
     grad_picked = (grad_gates - jnp.sum(gates * grad_gates, axis=1, keepdims=True)) / total
@@ -1409,39 +1817,30 @@
     grad_logits = (
         router_probs * (grad_probs - jnp.sum(grad_probs * router_probs, axis=-1, keepdims=True))
     ).astype(jnp.bfloat16)
+    grad_sum, all_logits = reduce_rows(partial_rows, grad_logits.T, length, 2)
+    grad_router = mix("btd,bet->de", all_rows, all_logits)
     grad_rows_two = grad_sum + jnp.dot(grad_logits, router.T, preferred_element_type=jnp.float32)
     grad_res_norm, grad_gain_moe = row_norm_back(grad_rows_two, normed_two, factor_two, gain_moe)
     grad_residual = cot32 + grad_res_norm
     grad_attn = grad_residual.astype(jnp.bfloat16)
-    group_grads, all_logits = gather(
-        [(grad_attn, "z", False), (grad_logits.T, "all", False)], length, 5, "gather_grads"
-    )
-    grad_router = mix("btd,bet->de", all_rows, all_logits)
-    grad_group_rows, grad_joint, grad_wo, grad_qgain, grad_kgain = attn_backward_joint(
-        group_grads.reshape(-1, width),
+    grad_rows_one, grad_joint, grad_wo, moe_sum, grad_qgain, grad_kgain = attend_back(
+        grad_attn,
         group_rows,
-        seg_ids,
         full_joint,
         full_output,
-        query_gain,
-        key_gain,
-        saved,
-    )
-    grad_rows_one, grad_joint, grad_wo = reduce_scatter(
-        [
-            (grad_group_rows.astype(jnp.bfloat16), "z", False, jnp.float32),
-            (grad_joint.astype(jnp.bfloat16), "dp", False, jnp.float32),
-            (grad_wo.astype(jnp.bfloat16), "dp", True, jnp.float32),
-        ],
+        projected,
+        attn_heads,
+        partial_out,
+        *turns,
         length,
-        6,
-        "reduce_weights",
-    )
+        3,
+    )
+    output = (residual + moe_sum).astype(jnp.bfloat16)
     grad_in_norm, grad_gain_attn = row_norm_back(grad_rows_one, normed_one, factor_one, gain_attn)
     grad_input = grad_residual + grad_in_norm
-    small = jnp.concatenate([grad_gain_attn, grad_gain_moe, grad_qgain, grad_kgain]).reshape(-1, 128)
+    small = jnp.concatenate([grad_gain_attn, grad_gain_moe, grad_qgain[0], grad_kgain[0]]).reshape(-1, 128)
     small = jnp.pad(small, ((0, -small.shape[0] % 16), (0, 0)))
-    (all_small,) = gather([(small, "all", False)], length, 7, "gather_small")
+    (all_small,) = gather([(small, "all", False)], length, 4, "gather_small")
     sums = jnp.sum(all_small, axis=0).reshape(-1)
     head_dim = query_gain.shape[0]
     return (

time: 766 us -> 639 us (0.83)
  matrix products: 53.7 us -> 11.1 us
  starting transfers between devices: 27.8 us -> 0 us
  local copies, waits for them, and re-layouts: 45.9 us -> 22 us
  Pallas kernels: 602 us -> 581 us
  other arithmetic: 31.5 us -> 19.9 us
    pallas_call x4 -> x3, Pallas kernels: 260 us -> 371 us  [the longest x1 152 us: attend_back(): pl.pallas_call(kernel, name='attend_back', out_shape=[shape((rows, width)...]
    pallas_call x3 -> x1, Pallas kernels: 126 us -> 21.9 us  [gather(): pl.pallas_call(kernel, name=name, out_shape=shapes, in_specs=[pl.BlockSpe...]
    dot_general x8 -> x0, matrix products: 30.5 us -> none  [the longest x1 6.41 us: attn_backward_joint(): jnp.dot(attn_heads.T, grad_attn, preferred_element_type=jnp.float32)]
    all_to_all x1 -> x0, starting transfers between devices: 27.8 us -> none  [gathered(): lax.all_to_all(token_grads, AXES, split_axis=0, concat_axis=0, tiled=True)]
    pallas_call x1, Pallas kernels: 215 us -> 188 us  [experts(): pl.pallas_call(kernel, name='experts', out_shape=[shape(big, bf16), shape...]
    dot_general x2 -> x0, local copies, waits for them, and re-layouts: 11.7 us -> none  [attn_forward(): jnp.dot(rows, wq_full, preferred_element_type=jnp.float32)]
    dot_general x7 -> x1, matrix products: 21.2 us -> 9.69 us  [mix(): return jnp.einsum(form, left, right, preferred_element_type=jnp.float32)]
    unnamed x147 -> x50, local copies, waits for them, and re-layouts: 17.5 us -> 16 us
  transfers between devices with their start and end apart: 1 -> 0, of which waited for: 0 -> 0; matrix products, arithmetic and copies ran while one was open for 2% -> 0% of each run, Pallas kernels for 22% -> 0%
where the time goes in v3:
time: 639 us; the launch traced here: 635 us
  Pallas kernels  581 us (91%)
  local copies, waits for them, and re-layouts  22 us (3%)
  other arithmetic  19.9 us (3%)
  matrix products  11.1 us (2%)
    pallas_call x1, Pallas kernels, experts(): pl.pallas_call(kernel, name='experts', out_shape=[shape(big, bf16), shape...  188 us
    pallas_call x1, Pallas kernels, attend_back(): pl.pallas_call(kernel, name='attend_back', out_shape=[shape((rows, width)...  152 us
    pallas_call x1, Pallas kernels, attend(): pl.pallas_call(kernel, name='attend', out_shape=[shape((rows, width), f32...  129 us
    pallas_call x1, Pallas kernels, reduce_rows(): pl.pallas_call(kernel, name='reduce_rows', out_shape=[jax.ShapeDtypeStruc...  89.5 us
    pallas_call x1, Pallas kernels, gather(): pl.pallas_call(kernel, name=name, out_shape=shapes, in_specs=[pl.BlockSpe...  21.9 us
    unnamed x50, local copies, waits for them, and re-layouts  16 us

profile of v3, /device:TPU:0, one launch (start us, length us, event | category | flops | bytes accessed | tf_op | source)
XLA Modules:
  0.0 635.3 jit_solution(10390739633960697660)
XLA Ops:
  0.6 0.0 copy-start.2
  0.7 1.3 fusion.10
  2.0 0.0 copy-start.15
  2.0 1.0 convert_reduce_fusion
  3.0 1.5 copy.38.segc
  4.5 2.0 fusion.4.rows_ref
  6.6 2.0 pad_maximum_fusion.joint_ref
  8.6 1.0 fusion.11
  9.6 1.0 pad_maximum_fusion.1
  10.6 129.2 %attend.1 = (f32[128,2048]{1,0:T(8,128)}, bf16[4,128,2048]{2,1,0:T(8,128)(2,1)}, bf16[8,256,1280]{2,1,0:T(8,128)(2,1)}, bf16[1024,2048]{1,0:T(8,128)(2,1)}, bf16...) custom-call(bf16[128,2048]{1,0:T(8,128)(2,1)} %fusion.4.rows_ref, ...), custom_call_target="tpu_custom_call" | custom-call | tf_op jit(solution)/shard_map/attend/pallas_call | solution.py:1083
  139.8 0.0 copy-done.2
  139.8 1.4 multiply_reduce_fusion.2
  141.3 0.0 copy-done.15
  141.3 0.9 copy-done
  142.2 0.0 copy-done.10
  142.2 0.2 multiply_convert_fusion.rows_ref
  142.4 0.0 copy-done.9
  142.4 0.0 copy-start.5
  142.4 0.3 fusion.16
  142.8 0.0 copy-done.12
  142.8 0.1 select_reduce_fusion
  142.9 0.6 select_bitcast_fusion.gates_ref
  143.5 0.0 copy-done.5
  143.5 188.3 %experts.1 = (bf16[32,128,2048]{2,1,0:T(8,128)(2,1)}, bf16[32,128,2048]{2,1,0:T(8,128)(2,1)}, bf16[32,128,2048]{2,1,0:T(8,128)(2,1)}, f32[32,8,128]{2,1,0:T(8,12...) custom-call(bf16[128,2048]{1,0:T(8,128)(2,1)} %copy-done.5, ...), custom_call_target="tpu_custom_call" | custom-call | tf_op jit(solution)/shard_map/experts/pallas_call | solution.py:879
  331.8 0.9 slice.36
  332.8 0.6 multiply_convert_fusion.1
  333.4 89.5 %reduce_rows.1 = (f32[128,2048]{1,0:T(8,128)}, bf16[32,32,128]{2,1,0:T(8,128)(2,1)}) custom-call(bf16[32,128,2048]{2,1,0:T(8,128)(2,1)} %get-tuple-element.38.source, bf16[32,128]{1,0:T(8,128)(2,1)} %bitcast.46), custom_call_target="tpu_custom_call" | custom-call | tf_op jit(solution)/shard_map/reduce_rows/pallas_call | solution.py:627
  423.0 0.0 copy-start.1
  423.0 0.0 copy-start.8
  423.0 0.0 copy-start.11
  423.0 0.0 copy-start.4
  423.0 9.7 %convolution_bitcast_fusion = f32[2048,32]{0,1:T(8,128)} fusion(bf16[32,32,128]{2,1,0:T(8,128)(2,1)} %get-tuple-element.54, bf16[32,128,2048]{2,1,0:T(8,128)(2,1)} %get-tuple-element.53), kind=kOutput, calls=%fused_computation.1 | convolution fusion | flops 536870912 | bytes 17301504 | tf_op jit(solution)/shard_map/btd,bet->de/dot_general | solution.py:1354
  432.7 0.0 copy-done.1
  432.7 0.0 copy-done.8
  432.7 0.0 copy-done.11
  432.7 1.1 multiply_reduce_fusion
  433.8 0.0 copy-done.14
  433.8 1.0 copy-done.3
  434.8 0.5 copy-done.16
  435.3 0.0 copy-done.4
  435.3 1.1 fusion.14.grad_ref
  436.4 152.3 %attend_back.1 = (f32[128,2048]{1,0:T(8,128)}, f32[256,1280]{1,0:T(8,128)}, f32[1024,256]{1,0:T(8,128)}, f32[128,2048]{1,0:T(8,128)}, f32[1,128]{1,0:T(1,128)}, /*index=5*/f32[1,128]{1,0:T(1,128)}) custom-call(bf16[128,2048]{1,0:T(8,128)(2,1)} %fusion.14.grad_ref, bf16[4,128,2048]{2,1,0:T(8,128)(2,1)} %get-tuple-element.41.rows_ref, ...), custom_call_target="tpu_custom_call" | custom-call | tf_op jit(solution)/shard_map/attend_back/pallas_call | solution.py:1314
  588.7 0.0 copy-start.13
  588.7 0.0 copy-start.17
  588.8 0.0 copy-start.18
  588.8 0.0 copy-start.6
  588.8 1.9 fusion.9
  590.6 0.0 copy-start.7
  590.7 4.2 fusion.8
  594.9 0.0 copy-done.13
  594.9 0.0 copy-done.17
  594.9 0.0 copy-done.18
  594.9 0.6 pad.4.refs_0_
  595.5 0.7 fusion.15
  596.3 1.1 slice.37
  597.4 21.9 %gather_small.1 = f32[32,48,128]{2,1,0:T(8,128)} custom-call(f32[48,128]{1,0:T(8,128)} %pad.4.refs_0_), custom_call_target="tpu_custom_call" | custom-call | tf_op jit(solution)/shard_map/gather_small/pallas_call | solution.py:351
  619.3 1.2 reduce_sum.169
  620.5 0.5 slice_bitcast_fusion.2
  621.0 0.6 slice_bitcast_fusion
  621.6 1.0 copy.44
  622.6 6.5 %copy.45 = f32[1,2048,768]{2,1,0:T(8,128)} copy(f32[1,2048,768]{2,1,0:T(8,128)} %bitcast.42) | data formatting | bytes 12582912
  629.1 2.8 copy.46
  631.9 0.5 slice-done.1
  632.4 2.7 copy.47
  (34 shorter events, 0.3 us)
Async XLA Ops:
  0.6 139.1 %copy-start.2 = (bf16[128,2048]{1,0:T(8,128)(2,1)S(1)}, bf16[128,2048]{1,0:T(8,128)(2,1)}, u32[]{:S(2)}) copy-start(bf16[128,2048]{1,0:T(8,128)(2,1)} %param.16) | copy-start | bytes 1572868
  1.9 140.3 %copy-start.10 = (f32[2048]{0:T(1024)S(1)}, f32[2048]{0:T(1024)}, u32[]{:S(2)}) copy-start(f32[2048]{0:T(1024)} %param.24) | copy-start | bytes 24580
  2.0 139.3 %copy-start.15 = (f32[128]{0:T(128)}, f32[128]{0:T(128)S(1)}, u32[]{:S(2)}) copy-start(f32[128]{0:T(128)S(1)} %add_rsqrt_fusion.1) | copy-start | bytes 1540
  6.6 135.8 %copy-start.9 = (bf16[2048,32]{0,1:T(8,128)(2,1)S(1)}, bf16[2048,32]{0,1:T(8,128)(2,1)}, u32[]{:S(2)}) copy-start(bf16[2048,32]{0,1:T(8,128)(2,1)} %param.27) | copy-start | bytes 393220
  8.6 134.1 %copy-start.12 = (s32[128,8]{0,1:T(8,128)S(1)}, s32[128,8]{0,1:T(8,128)}, u32[]{:S(2)}) copy-start(s32[128,8]{0,1:T(8,128)} %param.18) | copy-start | bytes 12292
  141.2 1.0 copy-start
  142.2 291.6 %copy-start.14 = (f32[128]{0:T(128)}, f32[128]{0:T(128)S(1)}, u32[]{:S(2)}) copy-start(f32[128]{0:T(128)S(1)} %add_rsqrt_fusion) | copy-start | bytes 1540
  142.4 1.1 copy-start.5
  423.0 9.7 %copy-start.1 = (f32[128,2048]{1,0:T(8,128)S(1)}, f32[128,2048]{1,0:T(8,128)}, u32[]{:S(2)}) copy-start(f32[128,2048]{1,0:T(8,128)} %copy-done) | copy-start | bytes 3145732
  423.0 9.7 %copy-start.8 = (f32[128,2048]{1,0:T(8,128)S(1)}, f32[128,2048]{1,0:T(8,128)}, u32[]{:S(2)}) copy-start(f32[128,2048]{1,0:T(8,128)} %get-tuple-element.40) | copy-start | bytes 3145732
  423.0 9.7 %copy-start.11 = (bf16[128,32]{0,1:T(8,128)(2,1)S(1)}, bf16[128,32]{0,1:T(8,128)(2,1)}, u32[]{:S(2)}) copy-start(bf16[128,32]{0,1:T(8,128)(2,1)} %multiply_convert_fusion.1) | copy-start | bytes 24580
  423.0 12.3 %copy-start.4 = (bf16[128,2048]{1,0:T(8,128)(2,1)S(1)}, bf16[128,2048]{1,0:T(8,128)(2,1)}, u32[]{:S(2)}) copy-start(bf16[128,2048]{1,0:T(8,128)(2,1)} %cots_ref.1) | copy-start | bytes 1572868
  433.8 1.0 copy-start.3
  434.7 0.5 copy-start.16
  588.7 6.2 copy-start.13
  588.7 6.2 copy-start.17
  588.8 6.1 copy-start.18
  588.8 6.8 %copy-start.6 = (f32[256,1280]{1,0:T(8,128)S(1)}, f32[256,1280]{1,0:T(8,128)}, u32[]{:S(2)}) copy-start(f32[256,1280]{1,0:T(8,128)} %get-tuple-element.49) | copy-start | bytes 3932164
  590.6 31.0 %copy-start.7 = (f32[1024,256]{1,0:T(8,128)S(1)}, f32[1024,256]{1,0:T(8,128)}, u32[]{:S(2)}) copy-start(f32[1024,256]{1,0:T(8,128)} %get-tuple-element.102) | copy-start | bytes 3145732
  597.3 31.8 %slice-start.2 = ((s8[6291456]{0:T(1024)(128)(4,1)}), s8[2097152]{0:T(1024)(128)(4,1)S(1)}, s32[]{:S(2)}) async-start(s8[6291456]{0:T(1024)(128)(4,1)} %bitcast.39), calls=%async_computation.2 | async-start | bytes 4194304
  622.6 6.5 %slice-start.3 = ((s8[6291456]{0:T(1024)(128)(4,1)}), s8[4194304]{0:T(1024)(128)(4,1)S(1)}, s32[]{:S(2)}) async-start(s8[6291456]{0:T(1024)(128)(4,1)} %bitcast.39), calls=%async_computation.3 | async-start | bytes 8388608
  622.6 9.4 %slice-start = ((s8[6291456]{0:T(1024)(128)(4,1)}), s8[4194304]{0:T(1024)(128)(4,1)S(1)}, s32[]{:S(2)}) async-start(s8[6291456]{0:T(1024)(128)(4,1)} %bitcast.36), calls=%async_computation | async-start | bytes 8388608
  629.1 3.3 slice-start.1

commit v4 on v3

--- a/solution.py
+++ b/solution.py
@@ -82,6 +82,10 @@
         return found + high * (length - 1 - 2 * found)
 
 
+def piece(rows, h):
+    return pl.ds(0, rows) if h is None else pl.ds(h * (rows // 2), rows // 2)
+
+
 def guarded(condition, action):
     if condition is None:
         action()
@@ -189,37 +193,40 @@
         ]
 
     def pass_on(self, sends, lane, kind, column, offset, turn, h, source=None, condition=lambda: None):
+        at = 0 if h is None else h
+
         def views():
             z = self.z + offset
             view = self.slot(column, z, h)
             return (
                 view if source is None else source(h),
                 view,
-                self.send.at[lane, turn, h],
-                self.recv.at[self.index(column, z), h],
+                self.send.at[lane, turn, at],
+                self.recv.at[self.index(column, z), at],
             )
 
         sends.start(kind, views, condition)
 
     def arrived(self, column, z, h):
         view = self.slot(column, z, h)
-        pltpu.make_async_copy(view, view, self.recv.at[self.index(column, z), h]).wait()
+        at = 0 if h is None else h
+        pltpu.make_async_copy(view, view, self.recv.at[self.index(column, z), at]).wait()
+
+    def local_copy(self):
+        return pltpu.make_async_copy(
+            self.own(None), self.slot(self.place.dp, self.z, None), self.local.at[0]
+        )
 
     def begin(self, sends):
         place = self.place
-        for h in range(2):
-            own = self.own
-            if self.over_z:
-                self.pass_on(sends, 0, "up", place.dp, 0, 0, h, own)
-                self.pass_on(sends, 1, "down", place.dp, 0, 0, h, own)
-            if self.over_dp:
-                self.pass_on(sends, 2, "x", place.dp, 0, 0, h, own)
-                self.pass_on(sends, 3, "y", place.dp, 0, 0, h, own)
-                self.pass_on(sends, 4, "core", place.dp, 0, 0, h, own)
-        for h in range(2):
-            pltpu.make_async_copy(
-                self.own(h), self.slot(place.dp, self.z, h), self.local.at[h]
-            ).start()
+        if self.over_z:
+            self.pass_on(sends, 0, "up", place.dp, 0, 0, None, self.own)
+            self.pass_on(sends, 1, "down", place.dp, 0, 0, None, self.own)
+        if self.over_dp:
+            self.pass_on(sends, 2, "x", place.dp, 0, 0, None, self.own)
+            self.pass_on(sends, 3, "y", place.dp, 0, 0, None, self.own)
+            self.pass_on(sends, 4, "core", place.dp, 0, 0, None, self.own)
+        self.local_copy().start()
 
     def along_z(self, sends, distance):
         if not self.over_z or distance >= self.length:
@@ -228,18 +235,16 @@
         for turn, offset, condition, onward in self.turns(distance):
 
             def step(turn=turn, offset=offset, condition=condition, onward=onward):
-                for h in range(2):
-                    self.arrived(place.dp, self.z + offset, h)
-                    if distance < self.length - 1:
-                        self.pass_on(
-                            sends, 0 if onward == "up" else 1, onward, place.dp, offset, turn, h,
-                            condition=condition,
-                        )
-                    if self.over_dp:
-                        for lane, kind in ((2, "x"), (3, "y"), (4, "core")):
-                            self.pass_on(
-                                sends, lane, kind, place.dp, offset, turn, h, condition=condition
-                            )
+                self.arrived(place.dp, self.z + offset, None)
+                lanes = []
+                if distance < self.length - 1:
+                    lanes.append((0 if onward == "up" else 1, onward))
+                if self.over_dp:
+                    lanes += [(2, "x"), (3, "y"), (4, "core")]
+                for lane, kind in lanes:
+                    self.pass_on(
+                        sends, lane, kind, place.dp, offset, turn, None, condition=condition
+                    )
 
             guarded(condition(), step)
 
@@ -250,15 +255,12 @@
         for turn, offset, condition, _ in self.turns(distance):
 
             def step(turn=turn, offset=offset, condition=condition):
-                for h in range(2):
-                    self.arrived(x, self.z + offset, h)
-                    if h == 0:
-                        self.pass_on(sends, 5, "y", x, offset, turn, h, condition=condition)
-                    self.pass_on(sends, 7, "core", x, offset, turn, h, condition=condition)
-                    self.arrived(y, self.z + offset, h)
-                    if h == 1:
-                        self.pass_on(sends, 6, "x", y, offset, turn, h, condition=condition)
-                    self.pass_on(sends, 8, "core", y, offset, turn, h, condition=condition)
+                self.arrived(x, self.z + offset, None)
+                self.pass_on(sends, 5, "y", x, offset, turn, 0, condition=condition)
+                self.pass_on(sends, 7, "core", x, offset, turn, None, condition=condition)
+                self.arrived(y, self.z + offset, None)
+                self.pass_on(sends, 6, "x", y, offset, turn, 1, condition=condition)
+                self.pass_on(sends, 8, "core", y, offset, turn, None, condition=condition)
 
             guarded(condition(), step)
 
@@ -276,14 +278,11 @@
             guarded(condition(), step)
 
     def settled(self):
-        for h in range(2):
-            pltpu.make_async_copy(
-                self.own(h), self.slot(self.place.dp, self.z, h), self.local.at[h]
-            ).wait()
+        self.local_copy().wait()
 
     def from_core(self, z):
-        for column in self.place.columns:
-            for h in range(2):
+        for number, column in enumerate(self.place.columns):
+            for h in (0, 1) if number == 3 else (None,):
                 self.arrived(column + self.place.to_core, z, h)
 
     def finish(self):
@@ -291,72 +290,6 @@
         if self.over_dp:
             for z in range(self.length):
                 self.from_core(z)
-
-
-def run_gather(place, items):
-    meet(place, any(i.over_z for i in items), any(i.over_dp for i in items))
-    sends = Sends(place)
-    for item in items:
-        item.begin(sends)
-    for step in range(place.length + 2):
-        for item in items:
-            item.along_z(sends, step + 1)
-        for item in items:
-            item.across(sends, step)
-        for item in items:
-            item.diagonal(sends, step - 1)
-    for item in items:
-        item.finish()
-    sends.drain()
-
-
-def gather(specs, length, collective_id, name):
-    modes = [mode for _, mode, _ in specs]
-    shapes, sems = [], []
-    for array, mode, by_columns in specs:
-        blocks = {"all": 8 * length, "dp": 8, "z": length}[mode]
-        if by_columns:
-            shape = (array.shape[0], blocks * array.shape[1])
-        else:
-            shape = (blocks,) + array.shape
-        shapes.append(jax.ShapeDtypeStruct(shape, array.dtype))
-        sems += GatherItem.semaphores(mode, length)
-    count = len(specs)
-
-    def kernel(*refs):
-        place = Place(length)
-        items = []
-        for number, (array, mode, by_columns) in enumerate(specs):
-            source, target = refs[number], refs[count + number]
-            recv, send, local = refs[2 * count + 3 * number : 2 * count + 3 * number + 3]
-            half = array.shape[0] // 2
-            width = array.shape[1]
-            item = GatherItem(mode, place, None, None, recv, send, local)
-
-            def own(h, source=source, half=half):
-                return source.at[pl.ds(h * half, half)]
-
-            def slot(column, z, h, target=target, half=half, width=width, item=item, by=by_columns):
-                block = item.index(column, z)
-                if by:
-                    return target.at[
-                        pl.ds(h * half, half), pl.ds(pl.multiple_of(block * width, width), width)
-                    ]
-                return target.at[block, pl.ds(h * half, half)]
-
-            item.own, item.slot = own, slot
-            items.append(item)
-        run_gather(place, items)
-
-    return pl.pallas_call(
-        kernel,
-        name=name,
-        out_shape=shapes,
-        in_specs=[pl.BlockSpec(memory_space=pl.ANY)] * count,
-        out_specs=[pl.BlockSpec(memory_space=pl.ANY)] * count,
-        scratch_shapes=sems,
-        compiler_params=pltpu.CompilerParams(collective_id=collective_id, has_side_effects=True),
-    )(*[array for array, _, _ in specs])
 
 
 class ReduceItem:
@@ -373,15 +306,14 @@
         t = length if mode != "dp" else 1
         columns = 4 if mode != "z" else 1
         dp = mode != "z"
-        half = (rows // 2, width)
         small = (8, 128)
         return [
-            pltpu.VMEM(small if in_place else (columns, t, 2) + half, jnp.bfloat16),
-            pltpu.VMEM(((columns, t, 2) + half) if dp else small, jnp.bfloat16),
-            pltpu.VMEM(((2, t) + half) if dp else small, jnp.bfloat16),
-            pltpu.VMEM(((2, t, 2) + half) if dp else small, jnp.bfloat16),
-            pltpu.VMEM(((t + 1, 2) + half) if mode != "dp" else small, jnp.bfloat16),
-            pltpu.SemaphoreType.DMA((columns, t, 2)),
+            pltpu.VMEM(small if in_place else (columns, t, rows, width), jnp.bfloat16),
+            pltpu.VMEM((columns, t, rows, width) if dp else small, jnp.bfloat16),
+            pltpu.VMEM((2, t, rows // 2, width) if dp else small, jnp.bfloat16),
+            pltpu.VMEM((2, t, rows, width) if dp else small, jnp.bfloat16),
+            pltpu.VMEM((t + 1, rows, width) if mode != "dp" else small, jnp.bfloat16),
+            pltpu.SemaphoreType.DMA((columns, t)),
             pltpu.SemaphoreType.DMA((10, t, 2)),
             pltpu.SemaphoreType.DMA((9, t + 1, 2)),
         ]
@@ -389,7 +321,7 @@
     def z_of(self, turn):
         return self.place.target(turn) if self.over_z else 0
 
-    def got(self, ref, lane, turn, h):
+    def got(self, ref, lane, turn, h=0):
         pltpu.make_async_copy(ref, ref, self.recv.at[lane, turn, h]).wait()
 
     computed = False
@@ -398,13 +330,7 @@
     def partial(self, column, turn, h):
         if self.in_place:
             return self.block(self.place.columns[column], self.z_of(turn), h)
-        return self.acc.at[column, turn, h]
-
-    def loaded(self, column, turn, h):
-        if self.computed or self.in_place:
-            return
-        ref = self.acc.at[column, turn, h]
-        pltpu.make_async_copy(ref, ref, self.load.at[column, turn, h]).wait()
+        return self.acc.at[column, turn, piece(self.acc.shape[2], h)]
 
     def add(self, target, refs, out=None):
         rows = target.shape[0]
@@ -428,51 +354,55 @@
             @pl.when((place.z == 0) | (place.z == self.length - 1))
             def _():
                 def clear(i, carry):
-                    self.from_z[i // 2, i % 2] = jnp.zeros(self.from_z.shape[2:], jnp.bfloat16)
+                    self.from_z[i] = jnp.zeros(self.from_z.shape[1:], jnp.bfloat16)
                     return carry
 
-                lax.fori_loop(0, 2 * (self.length + 1), clear, 0)
+                lax.fori_loop(0, self.length + 1, clear, 0)
 
     def load_all(self):
         place = self.place
         for turn in range(self.length):
             for column in (3, 1, 2, 0) if self.over_dp else (0,):
-                for h in range(2):
-                    pltpu.make_async_copy(
-                        self.block(place.columns[column], self.z_of(turn), h),
-                        self.acc.at[column, turn, h],
-                        self.load.at[column, turn, h],
-                    ).start()
+                pltpu.make_async_copy(
+                    self.block(place.columns[column], self.z_of(turn), None),
+                    self.acc.at[column, turn],
+                    self.load.at[column, turn],
+                ).start()
 
     def hand_over(self, sends, turn):
         if not self.over_dp or turn >= self.length:
             return
         place = self.place
         for column in (3, 1, 2, 0):
-            for h in range(2):
-                sends.start(
-                    "core",
-                    lambda column=column, h=h: (
-                        self.block(place.columns[column] + place.to_core, self.z_of(turn), h),
-                        self.from_core.at[column, turn, h],
-                        self.send.at[column, turn, h],
-                        self.recv.at[column, turn, h],
-                    ),
-                )
+            sends.start(
+                "core",
+                lambda column=column: (
+                    self.block(place.columns[column] + place.to_core, self.z_of(turn), None),
+                    self.from_core.at[column, turn],
+                    self.send.at[column, turn, 0],
+                    self.recv.at[column, turn, 0],
+                ),
+            )
+
+    def ready(self, column, turn):
+        if not (self.computed or self.in_place):
+            ref = self.acc.at[column, turn]
+            pltpu.make_async_copy(ref, ref, self.load.at[column, turn]).wait()
+        if self.over_dp:
+            self.got(self.from_core.at[column, turn], column, turn)
 
     def settle(self, column, turn, h, extra=(), out=None):
-        self.loaded(column, turn, h)
         refs = list(extra)
         if self.over_dp:
-            ref = self.from_core.at[column, turn, h]
-            self.got(ref, column, turn, h)
-            refs.append(ref)
+            rows = self.from_core.shape[2]
+            refs.append(self.from_core.at[column, turn, piece(rows, h)])
         if refs or out is not None:
             self.add(self.partial(column, turn, h), refs, out)
 
     def corners(self, sends, turn):
         if not self.over_dp or not 0 <= turn < self.length:
             return
+        self.ready(3, turn)
         for h, kind in ((0, "y"), (1, "x")):
             self.settle(3, turn, h)
             sends.start(
@@ -488,6 +418,7 @@
     def straight(self, sends, turn, second):
         if not self.over_dp or not 0 <= turn < self.length:
             return
+        rows = self.from_xy.shape[2]
         for column, kind in ((1, "x"), (2, "y")):
             h = (column - 1) if second else (2 - column)
             extra = ()
@@ -495,12 +426,14 @@
                 ref = self.corner.at[h, turn]
                 self.got(ref, 4, turn, h)
                 extra = (ref,)
+            else:
+                self.ready(column, turn)
             self.settle(column, turn, h, extra)
             sends.start(
                 kind,
                 lambda column=column, h=h: (
                     self.partial(column, turn, h),
-                    self.from_xy.at[column - 1, turn, h],
+                    self.from_xy.at[column - 1, turn, piece(rows, h)],
                     self.send.at[4 + column, turn, h],
                     self.recv.at[4 + column, turn, h],
                 ),
@@ -512,56 +445,61 @@
         place = self.place
         last = turn == self.length - 1
         z = self.z_of(turn)
-        for h in range(2):
-            extra = []
-            if self.over_dp:
-                for lane in (0, 1):
-                    ref = self.from_xy.at[lane, turn, h]
-                    self.got(ref, 5 + lane, turn, h)
-                    extra.append(ref)
-            if self.over_z:
-                slot = self.from_z.at[z, h]
-
-                def got_slot(h=h):
-                    self.got(self.from_z.at[z, h], 7, z, h)
-
-                def got_other(h=h):
-                    self.got(self.from_z.at[self.length, h], 7, self.length, h)
-
-                if last:
-                    guarded(place.has_down, got_slot)
-                    guarded(place.has_up, got_other)
-                    extra += [slot, self.from_z.at[self.length, h]]
-                else:
-                    guarded((z > place.z) & place.has_down, got_slot)
-                    guarded((z < place.z) & place.has_up, got_slot)
-                    extra.append(slot)
-            self.settle(
-                0, turn, h, extra, self.out(h) if last else None
-            )
-            if self.over_z and not last:
-
-                def going_up(h=h):
-                    return (
-                        self.partial(0, turn, h),
-                        self.from_z.at[z, h],
-                        self.send.at[7, turn, h],
-                        self.recv.at[7, z, h],
-                    )
-
-                def going_down(h=h):
-                    arrives = (z - place.z + 1 + self.length) // self.length
-                    goal = z + arrives * (self.length - z)
-                    return (
-                        self.partial(0, turn, h),
-                        self.from_z.at[goal, h],
-                        self.send.at[7, turn, h],
-                        self.recv.at[7, goal, h],
-                    )
-
-                above, below = z > place.z, z < place.z
-                pl.when(above)(lambda: sends.start("up", going_up, lambda: above))
-                pl.when(below)(lambda: sends.start("down", going_down, lambda: below))
+        extra = []
+        self.ready(0, turn)
+        if self.over_dp:
+            for lane in (0, 1):
+                rows = self.from_xy.shape[2]
+                for h in range(2):
+                    self.got(self.from_xy.at[lane, turn, piece(rows, h)], 5 + lane, turn, h)
+                extra.append(self.from_xy.at[lane, turn])
+        if self.over_z:
+
+            def got_slot():
+                self.got(self.from_z.at[z], 7, z)
+
+            def got_other():
+                self.got(self.from_z.at[self.length], 7, self.length)
+
+            extra.append(self.from_z.at[z])
+            if last:
+                guarded(place.has_down, got_slot)
+                guarded(place.has_up, got_other)
+                extra.append(self.from_z.at[self.length])
+            else:
+                guarded((z > place.z) & place.has_down, got_slot)
+                guarded((z < place.z) & place.has_up, got_slot)
+        self.settle(0, turn, None, extra, self.out(None) if last else None)
+        if self.over_z and not last:
+
+            def going_up():
+                goal = self.z_of(turn)
+                return (
+                    self.partial(0, turn, None),
+                    self.from_z.at[goal],
+                    self.send.at[7, turn, 0],
+                    self.recv.at[7, goal, 0],
+                )
+
+            def going_down():
+                there = self.z_of(turn)
+                arrives = (there - place.z + 1 + self.length) // self.length
+                goal = there + arrives * (self.length - there)
+                return (
+                    self.partial(0, turn, None),
+                    self.from_z.at[goal],
+                    self.send.at[7, turn, 0],
+                    self.recv.at[7, goal, 0],
+                )
+
+            def above():
+                return self.z_of(turn) > place.z
+
+            def below():
+                return self.z_of(turn) < place.z
+
+            pl.when(above())(lambda: sends.start("up", going_up, above))
+            pl.when(below())(lambda: sends.start("down", going_down, below))
 
 
 def advance(item, sends, step):
@@ -572,73 +510,176 @@
     item.home(sends, step - 2 if item.over_dp else step)
 
 
-def run_reduce(place, items, gathers=()):
-    for item in items:
-        item.begin()
-    meet(place, any(i.over_z for i in items), any(i.over_dp for i in items))
-    sends = Sends(place)
-    for item in gathers:
-        item.begin(sends)
-    for item in items:
-        item.load_all()
-    for turn in range(2):
-        for item in items:
-            item.hand_over(sends, turn)
-    longest = max(item.length for item in items)
-    for step in range(longest + 2):
-        for item in items:
-            item.corners(sends, step)
-        for item in items:
-            item.straight(sends, step, False)
-        for item in items:
-            item.hand_over(sends, step + 2)
-        for item in items:
-            item.straight(sends, step - 1, True)
-        for item in items:
-            item.home(sends, step - 2 if item.over_dp else step)
-        for item in gathers:
-            item.along_z(sends, step + 1)
-            item.across(sends, step)
-            item.diagonal(sends, step - 1)
-    for item in gathers:
-        item.finish()
-    sends.drain()
-
-
-def reduce_rows(partials, small, length, collective_id):
+def reduce_rows(partials, small, picked, gated, hid, dgate, dup, length, collective_id):
     devices, rows, width = partials.shape
+    slots, hidden = dup.shape
     half, low = rows // 2, small.shape[0] // 2
-
-    def kernel(source, small_ref, target, small_all, *rest):
+    tile, narrow = width // 4, hidden // 3
+    f32, bf16 = jnp.float32, jnp.bfloat16
+
+    def kernel(
+        source, small_ref, picked_ref, gated_ref, hid_ref, dgate_ref, dup_ref,
+        target, small_all, out_g, out_u, out_d,
+        hid_v, dgate_v, dup_v, picked_v, gated_v, tile_g, tile_u, tile_d, load_sem, tile_sem, store_sem,
+        *rest,
+    ):
         place = Place(length)
         item = ReduceItem(
             "all",
             place,
-            lambda c, z, h: source.at[c * length + z, pl.ds(h * half, half)],
+            lambda c, z, h: source.at[c * length + z, piece(2 * half, h)],
             rest[:8],
-            lambda h: target.at[pl.ds(h * half, half)],
+            lambda h: target.at[piece(2 * half, h)],
         )
         beside = GatherItem("all", place, None, None, *rest[8:])
-        beside.own = lambda h: small_ref.at[pl.ds(h * low, low)]
-        beside.slot = lambda c, z, h: small_all.at[c * length + z, pl.ds(h * low, low)]
-        run_reduce(place, [item], [beside])
+        beside.own = lambda h: small_ref.at[piece(2 * low, h)]
+        beside.slot = lambda c, z, h: small_all.at[c * length + z, piece(2 * low, h)]
+        item.begin()
+        meet(place, True, True)
+        sends = Sends(place)
+        beside.begin(sends)
+        item.load_all()
+        item.hand_over(sends, 0)
+        item.hand_over(sends, 1)
+        resident = [
+            pltpu.make_async_copy(left, right, load_sem.at[n])
+            for n, (left, right) in enumerate(
+                ((hid_ref, hid_v), (dgate_ref, dgate_v), (dup_ref, dup_v))
+            )
+        ]
+        for copy in resident:
+            copy.start()
+
+        def lanes_of(n):
+            return pl.ds(pl.multiple_of(n * tile, tile), tile)
+
+        def tiles(n, slot):
+            return [
+                pltpu.make_async_copy(picked_ref.at[:, lanes_of(n)], picked_v.at[slot], tile_sem.at[slot, 0]),
+                pltpu.make_async_copy(gated_ref.at[:, lanes_of(n)], gated_v.at[slot], tile_sem.at[slot, 1]),
+            ]
+
+        def stores(n, slot):
+            return [
+                pltpu.make_async_copy(tile_g.at[slot], out_g.at[lanes_of(n)], store_sem.at[slot, 0]),
+                pltpu.make_async_copy(tile_u.at[slot], out_u.at[lanes_of(n)], store_sem.at[slot, 1]),
+                pltpu.make_async_copy(tile_d.at[slot], out_d.at[:, lanes_of(n)], store_sem.at[slot, 2]),
+            ]
+
+        for copy in tiles(0, 0):
+            copy.start()
+
+        def narrow_of(m):
+            return pl.ds(pl.multiple_of(m * narrow, narrow), narrow)
+
+        def turn_of(i, carry):
+            for step in range(length + 2):
+
+                @pl.when(i == 2 * step)
+                def _(step=step):
+                    item.corners(sends, step)
+                    item.straight(sends, step, False)
+                    item.hand_over(sends, step + 2)
+                    beside.along_z(sends, step + 1)
+                    beside.across(sends, step)
+
+                @pl.when(i == 2 * step + 1)
+                def _(step=step):
+                    item.straight(sends, step - 1, True)
+                    item.home(sends, step - 2)
+                    beside.diagonal(sends, step)
+
+            n, kind = i // 3, i % 3
+            slot = n % 2
+
+            @pl.when(i == 0)
+            def _():
+                for copy in resident:
+                    copy.wait()
+
+            @pl.when((kind == 0) & (n < 4))
+            def _():
+                for copy in tiles(n, slot):
+                    copy.wait()
+
+                @pl.when(n < 3)
+                def _():
+                    for copy in tiles(n + 1, 1 - slot):
+                        copy.start()
+
+                @pl.when(n >= 2)
+                def _():
+                    for copy in stores(n, slot):
+                        copy.wait()
+
+                def body(m, carry):
+                    tile_g[slot, :, narrow_of(m)] = dot(picked_v[slot], dgate_v[:, narrow_of(m)], 0, 0)
+                    return carry
+
+                lax.fori_loop(0, 3, body, 0)
+                stores(n, slot)[0].start()
+
+            @pl.when((kind == 1) & (n < 4))
+            def _():
+                def body(m, carry):
+                    tile_u[slot, :, narrow_of(m)] = dot(picked_v[slot], dup_v[:, narrow_of(m)], 0, 0)
+                    return carry
+
+                lax.fori_loop(0, 3, body, 0)
+                stores(n, slot)[1].start()
+
+            @pl.when((kind == 2) & (n < 4))
+            def _():
+                def body(m, carry):
+                    tile_d[slot, narrow_of(m), :] = dot(hid_v[:, narrow_of(m)], gated_v[slot], 0, 0)
+                    return carry
+
+                lax.fori_loop(0, 3, body, 0)
+                stores(n, slot)[2].start()
+
+            return carry
+
+        lax.fori_loop(0, max(12, 2 * (length + 2)), turn_of, 0)
+        beside.finish()
+        for slot in range(2):
+            for copy in stores(slot, slot):
+                copy.wait()
+        sends.drain()
 
     any_spec = pl.BlockSpec(memory_space=pl.ANY)
+    shape = jax.ShapeDtypeStruct
+    sems = pltpu.SemaphoreType.DMA
     return pl.pallas_call(
         kernel,
         name="reduce_rows",
         out_shape=[
-            jax.ShapeDtypeStruct((rows, width), jnp.float32),
-            jax.ShapeDtypeStruct((devices,) + small.shape, small.dtype),
+            shape((rows, width), f32),
+            shape((devices,) + small.shape, small.dtype),
+            shape((width, hidden), f32),
+            shape((width, hidden), f32),
+            shape((hidden, width), f32),
         ],
-        in_specs=[any_spec, any_spec],
-        out_specs=[pl.BlockSpec(memory_space=pltpu.VMEM), any_spec],
-        scratch_shapes=ReduceItem.scratch("all", length, rows, width)
+        in_specs=[any_spec] * 7,
+        out_specs=[pl.BlockSpec(memory_space=pltpu.VMEM)] + [any_spec] * 4,
+        scratch_shapes=[
+            pltpu.VMEM((slots, hidden), bf16),
+            pltpu.VMEM((slots, hidden), bf16),
+            pltpu.VMEM((slots, hidden), bf16),
+            pltpu.VMEM((2, slots, tile), bf16),
+            pltpu.VMEM((2, slots, tile), bf16),
+            pltpu.VMEM((2, tile, hidden), f32),
+            pltpu.VMEM((2, tile, hidden), f32),
+            pltpu.VMEM((2, hidden, tile), f32),
+            sems((3,)),
+            sems((2, 2)),
+            sems((2, 3)),
+        ]
+        + ReduceItem.scratch("all", length, rows, width)
         + GatherItem.semaphores("all", length),
         compiler_params=pltpu.CompilerParams(
-            collective_id=collective_id, has_side_effects=True, vmem_limit_bytes=56 << 20
+            collective_id=collective_id, has_side_effects=True, vmem_limit_bytes=67043328
         ),
-    )(partials, small)
+    )(partials, small, picked, gated, hid, dgate, dup)
 
 
 def dot(left, right, left_dim=1, right_dim=0):
@@ -657,32 +698,57 @@
     f32, bf16 = jnp.float32, jnp.bfloat16
 
     def kernel(
-        rows_ref, all_cots, gates_ref, wg, wu, wd,
-        all_rows, part_out, part_grad, token_in, out_wg, out_wu, out_wd,
-        table, row_buf, cot_buf, picked, cotan, gated, hid, dgate, dup, scaled, back,
-        chosen, slot_gate, slot_sum, acc_g, acc_u, acc_d, stage_out, stage_grad, token_out,
-        recv_r, send_r, local_r, recv_t, send_t, local_t,
-        load_sem, store_sem, final_sem, token_sem,
+        rows_ref, all_cots, gates_ref, wg_ref, wu_ref, wd_ref,
+        all_rows, part_out, part_grad, token_in, picked_all, gated_all, hid_all, dgate_all, dup_all,
+        wg, wu, wd, chosen_all, gates_all, rank_v, table, row_buf, cot_buf, picked, cotan, gated, hid, dgate, dup, scaled, back,
+        chosen, slot_gate, slot_sum, stage_out, stage_grad, token_out,
+        recv_r, send_r, local_r,
+        load_sem, store_sem, save_sem, token_sem, gate_sem, weight_sem,
     ):
         place = Place(length)
         expert = place.dp * length + place.z
 
         def item_of(source, target, sems, half):
             item = GatherItem("all", place, None, None, *sems)
-            item.own = lambda h: source.at[pl.ds(h * half, half)]
+            item.own = lambda h: source.at[piece(2 * half, h)]
             item.slot = lambda column, z, h: target.at[
-                column * length + z, pl.ds(h * half, half)
+                column * length + z, piece(2 * half, h)
             ]
             return item
 
         big = [
             item_of(rows_ref, all_rows, (recv_r, send_r, local_r), rows // 2),
         ]
-        items = [item_of(gates_ref, table, (recv_t, send_t, local_t), gates_ref.shape[0] // 2)] + big
+        items = big
         meet_all(place)
         sends = Sends(place)
+
+        def gate_send(n):
+            device, there = other_device(place, n + 1)
+            return pltpu.make_async_remote_copy(
+                src_ref=gates_ref.at[there],
+                dst_ref=table.at[expert],
+                send_sem=gate_sem.at[0],
+                recv_sem=gate_sem.at[1],
+                device_id=device,
+                device_id_type=MESH,
+            )
+
+        def send_gates(n, carry):
+            gate_send(n).start()
+            return carry
+
+        lax.fori_loop(0, devices - 1, send_gates, 0)
+        pltpu.make_async_copy(gates_ref.at[expert], table.at[expert], gate_sem.at[1]).start()
         for item in items:
             item.begin(sends)
+
+        weights = [
+            pltpu.make_async_copy(source, target, weight_sem.at[n])
+            for n, (source, target) in enumerate(((wg_ref, wg), (wu_ref, wu), (wd_ref, wd)))
+        ]
+        for copy in weights:
+            copy.start()
 
         def along(distance):
             for item in items:
@@ -696,20 +762,24 @@
             for item in items:
                 item.diagonal(sends, distance)
 
-        def clear(i, carry):
-            at = pl.ds(pl.multiple_of(i * 64, 64), 64)
-            acc_g[at, :] = jnp.zeros((64, hidden), f32)
-            acc_u[at, :] = jnp.zeros((64, hidden), f32)
+        along(1)
+        pltpu.make_async_copy(table, table, gate_sem.at[1]).wait()
+        order = lax.broadcasted_iota(jnp.int32, (rows, rows), 0)
+        upto = (order <= lax.broadcasted_iota(jnp.int32, (rows, rows), 1)).astype(f32).astype(bf16)
+        slots = lax.broadcasted_iota(jnp.int32, (capacity, rows), 0).astype(f32)
+        lines = table[:, 0, :]
+        rank_v[...] = dot((lines >= 0.0).astype(f32).astype(bf16), upto) - 1.0
+
+        def choose(block, carry):
+            line = table[block, 0:1, :]
+            ranks = rank_v[pl.ds(block, 1), :]
+            pick = jnp.where((line >= 0.0) & (ranks == slots), 1.0, 0.0)
+            gate = jnp.sum(pick * line, axis=1, keepdims=True)
+            chosen_all[block] = pick.astype(bf16)
+            gates_all[block] = jnp.broadcast_to(gate, (capacity, 128))
             return carry
 
-        def clear_down(i, carry):
-            at = pl.ds(pl.multiple_of(i * 64, 64), 64)
-            acc_d[at, :] = jnp.zeros((64, width), f32)
-            return carry
-
-        lax.fori_loop(0, width // 64, clear, 0)
-        lax.fori_loop(0, hidden // 64, clear_down, 0)
-        along(1)
+        lax.fori_loop(0, devices, choose, 0, unroll=4)
         across(0)
         for item in items:
             item.settled()
@@ -731,56 +801,90 @@
                 pltpu.make_async_copy(stage_grad.at[slot, j], part_grad.at[block], store_sem.at[slot, 1, j]),
             ]
 
-        order = lax.broadcasted_iota(jnp.int32, (rows, rows), 0)
-        upto = (order <= lax.broadcasted_iota(jnp.int32, (rows, rows), 1)).astype(f32).astype(bf16)
-        slots = lax.broadcasted_iota(jnp.int32, (capacity, rows), 0).astype(f32)
+        def saved(i):
+            first = [
+                pltpu.make_async_copy(picked, picked_all.at[i], save_sem.at[0]),
+                pltpu.make_async_copy(gated, gated_all.at[i], save_sem.at[1]),
+            ]
+            second = [
+                pltpu.make_async_copy(hid, hid_all.at[i], save_sem.at[2]),
+                pltpu.make_async_copy(dgate, dgate_all.at[i], save_sem.at[3]),
+                pltpu.make_async_copy(dup, dup_all.at[i], save_sem.at[4]),
+            ]
+            return first, second
+
+        def start_loads(step, side):
+            for j in range(4):
+                for copy in load(j, side, place.nearest(step), side):
+                    copy.start()
+
+        corner(0)
+        for item in items:
+            item.from_core(place.nearest(0))
+        start_loads(0, 0)
+        start_loads(0, 1)
+        for copy in weights:
+            copy.wait()
 
         def unit(i, carry):
             turn, side = i // 2, i % 2
             z = place.nearest(turn)
 
-            for step in range(length):
-
-                @pl.when(i == 2 * step)
+            @pl.when(i == 1)
+            def _():
+                along(2)
+                across(1)
+
+            for step in range(1, length):
+
+                @pl.when(i == max(2, 2 * step - 1))
                 def _(step=step):
+                    corner(step)
                     along(step + 2)
-                    corner(step)
                     across(step + 1)
                     for item in items:
                         item.from_core(place.nearest(step))
-                    for other in range(2):
-                        for j in range(4):
-                            for copy in load(j, other, place.nearest(step), other):
-                                copy.start()
-
-            @pl.when(i >= 2)
+                    start_loads(step, 0)
+                    if step == 1:
+                        start_loads(step, 1)
+
+            @pl.when(i >= 1)
             def _():
-                for j in range(4):
-                    for copy in store(j, side, z, side):
-                        copy.wait()
+                for copy in saved(i)[0]:
+                    copy.wait()
 
             for j in range(4):
                 for copy in load(j, side, z, side):
                     copy.wait()
+            for j in range(4):
                 block = block_of(j, side, z)
-                line = table[block, pl.ds(expert, 1), :]
-                named = line >= 0.0
-                ranks = dot(named.astype(f32).astype(bf16), upto) - 1.0
-                pick = jnp.where(named & (ranks == slots), 1.0, 0.0)
-                gate = jnp.sum(pick * line, axis=1, keepdims=True)
-                chosen[j] = pick.astype(bf16)
-                at = pl.ds(j * capacity, capacity)
-                slot_gate[at, :] = jnp.broadcast_to(gate, (capacity, 128))
-
-                def select(n, carry, j=j, at=at):
-                    lanes = pl.ds(pl.multiple_of(n * tile, tile), tile)
+                chosen[j] = chosen_all[block]
+                slot_gate[pl.ds(j * capacity, capacity), :] = gates_all[block]
+
+            def select(n, carry):
+                lanes = pl.ds(pl.multiple_of(n * tile, tile), tile)
+                for j in range(4):
+                    at = pl.ds(j * capacity, capacity)
                     picked[at, lanes] = dot(chosen[j], row_buf[side, j, :, lanes]).astype(bf16)
                     cot = dot(chosen[j], cot_buf[side, j, :, lanes])
                     cotan[at, lanes] = cot.astype(bf16)
                     gated[at, lanes] = (slot_gate[at, 0:1] * cot).astype(bf16)
-                    return carry
-
-                lax.fori_loop(0, width // tile, select, 0)
+                return carry
+
+            lax.fori_loop(0, width // tile, select, 0)
+
+            for copy in saved(i)[0]:
+                copy.start()
+            for step in range(2, length):
+
+                @pl.when(i == 2 * step - 1)
+                def _(step=step):
+                    start_loads(step, 1)
+
+            @pl.when(i >= 1)
+            def _():
+                for copy in saved(i)[1]:
+                    copy.wait()
 
             def middle(n, carry):
                 lanes = pl.ds(pl.multiple_of(n * narrow, narrow), narrow)
@@ -794,7 +898,15 @@
                 return carry
 
             lax.fori_loop(0, hidden // narrow, middle, 0)
+            for copy in saved(i)[1]:
+                copy.start()
             slot_sum[...] = jnp.zeros(slot_sum.shape, f32)
+
+            @pl.when(i >= 2)
+            def _():
+                for j in range(4):
+                    for copy in store(j, side, z, side):
+                        copy.wait()
 
             def outward(n, carry):
                 lanes = pl.ds(pl.multiple_of(n * tile, tile), tile)
@@ -818,30 +930,13 @@
             for j in range(4):
                 for copy in store(j, side, z, side):
                     copy.start()
-                at = pl.ds(j * capacity, capacity)
-                total = jnp.sum(slot_sum[at, :], axis=1, keepdims=True)
-                sums = jnp.sum(chosen[j].astype(f32) * total, axis=0, keepdims=True)
-                token_out[block_of(j, side, z)] = jnp.broadcast_to(sums, (8, rows))
-
-            def weights(n, carry):
-                lanes = pl.ds(pl.multiple_of(n * tile, tile), tile)
-                acc_g[lanes, :] += dot(picked[:, lanes], dgate[...], 0, 0)
-                acc_u[lanes, :] += dot(picked[:, lanes], dup[...], 0, 0)
-                acc_d[:, lanes] += dot(hid[...], gated[:, lanes], 0, 0)
-                return carry
-
-            lax.fori_loop(0, width // tile, weights, 0)
+            total = jnp.sum(slot_sum[...], axis=1, keepdims=True).reshape(4, capacity, 1)
+            sums = jnp.sum(chosen[...].astype(f32) * total, axis=1)
+            for j in range(4):
+                token_out[block_of(j, side, z)] = jnp.broadcast_to(sums[j : j + 1], (8, rows))
             return carry
 
         lax.fori_loop(0, 2 * length, unit, 0)
-        finals = [
-            pltpu.make_async_copy(source, target, final_sem.at[n])
-            for n, (source, target) in enumerate(
-                ((acc_g, out_wg), (acc_u, out_wu), (acc_d, out_wd))
-            )
-        ]
-        for copy in finals:
-            copy.start()
 
         def token_send(n):
             device, there = other_device(place, n + 1)
@@ -864,12 +959,14 @@
             for j in range(4):
                 for copy in store(j, side, 0, side):
                     copy.wait()
-        for copy in finals:
-            copy.wait()
+        for copies in saved(0):
+            for copy in copies:
+                copy.wait()
         sends.drain()
         pltpu.make_async_copy(token_out, token_in, token_sem.at[1]).wait()
         sent = token_out.at[pl.ds(0, devices - 1)]
         pltpu.make_async_copy(sent, sent, token_sem.at[0]).wait()
+        pltpu.make_async_copy(sent, sent, gate_sem.at[0]).wait()
 
     any_spec = pl.BlockSpec(memory_space=pl.ANY)
     vmem = pl.BlockSpec(memory_space=pltpu.VMEM)
@@ -882,12 +979,20 @@
         out_shape=[
             shape(big, bf16), shape(big, bf16), shape(big, bf16),
             shape((devices, 8, rows), f32),
-            shape((width, hidden), f32), shape((width, hidden), f32), shape((hidden, width), f32),
+            shape((2 * length, count, width), bf16), shape((2 * length, count, width), bf16),
+            shape((2 * length, count, hidden), bf16), shape((2 * length, count, hidden), bf16),
+            shape((2 * length, count, hidden), bf16),
         ],
-        in_specs=[any_spec] * 3 + [vmem] * 3,
-        out_specs=[any_spec] * 3 + [vmem] + [any_spec] * 3,
+        in_specs=[any_spec] * 6,
+        out_specs=[any_spec] * 3 + [vmem] + [any_spec] * 5,
         scratch_shapes=[
-            pltpu.VMEM((devices,) + gates_own.shape, f32),
+            pltpu.VMEM((width, hidden), bf16),
+            pltpu.VMEM((width, hidden), bf16),
+            pltpu.VMEM((hidden, width), bf16),
+            pltpu.VMEM((devices, capacity, rows), bf16),
+            pltpu.VMEM((devices, capacity, 128), f32),
+            pltpu.VMEM((devices, rows), f32),
+            pltpu.VMEM((devices, 8, rows), f32),
             pltpu.VMEM((2, 4, rows, width), bf16),
             pltpu.VMEM((2, 4, rows, width), bf16),
             pltpu.VMEM((count, width), bf16),
@@ -901,15 +1006,12 @@
             pltpu.VMEM((4, capacity, rows), bf16),
             pltpu.VMEM((count, 128), f32),
             pltpu.VMEM((count, 128), f32),
-            pltpu.VMEM((width, hidden), f32),
-            pltpu.VMEM((width, hidden), f32),
-            pltpu.VMEM((hidden, width), f32),
             pltpu.VMEM((2, 4, rows, width), bf16),
             pltpu.VMEM((2, 4, rows, width), bf16),
             pltpu.VMEM((devices, 8, rows), f32),
         ]
-        + GatherItem.semaphores("all", length) * 2
-        + [sems((2, 2, 4)), sems((2, 2, 4)), sems((3,)), sems((2,))],
+        + GatherItem.semaphores("all", length)
+        + [sems((2, 2, 4)), sems((2, 2, 4)), sems((5,)), sems((2,)), sems((2,)), sems((3,))],
         compiler_params=pltpu.CompilerParams(
             collective_id=collective_id, has_side_effects=True, vmem_limit_bytes=63 << 20
         ),
@@ -958,23 +1060,23 @@
 
         def item_of(mode, source, half, slot, sems):
             item = GatherItem(mode, place, None, None, *sems)
-            item.own = lambda h: source.at[pl.ds(h * half, half)]
+            item.own = lambda h: source.at[piece(2 * half, h)]
             item.slot = slot
             return item
 
         half, deep, tall = rows // 2, depth // 2, head_width // 2
         own_rows = item_of(
-            "z", rows_ref, half, lambda c, z, h: rows_v.at[z, pl.ds(h * half, half)], (g0, g1, g2)
+            "z", rows_ref, half, lambda c, z, h: rows_v.at[z, piece(2 * half, h)], (g0, g1, g2)
         )
         own_joint = item_of(
-            "dp", joint_ref, deep, lambda c, z, h: joint_v.at[c, pl.ds(h * deep, deep)], (j0, j1, j2)
+            "dp", joint_ref, deep, lambda c, z, h: joint_v.at[c, piece(2 * deep, h)], (j0, j1, j2)
         )
         own_weight = item_of(
             "dp",
             output_ref,
             tall,
             lambda c, z, h: weight_v.at[
-                pl.ds(h * tall, tall), pl.ds(pl.multiple_of(c * part, part), part)
+                piece(2 * tall, h), pl.ds(pl.multiple_of(c * part, part), part)
             ],
             (w0, w1, w2),
         )
@@ -982,12 +1084,12 @@
             "all",
             cots_ref,
             half,
-            lambda c, z, h: out_cots.at[c * length + z, pl.ds(h * half, half)],
+            lambda c, z, h: out_cots.at[c * length + z, piece(2 * half, h)],
             (c0, c1, c2),
         )
         total = ReduceItem(
             "z", place, None, (r0, r1, r2, r3, r4, r5, r6, r7),
-            lambda h: out_add.at[pl.ds(h * half, half)],
+            lambda h: out_add.at[piece(2 * half, h)],
         )
         total.computed = True
         total.begin()
@@ -1060,8 +1162,7 @@
                 lanes = pl.ds(pl.multiple_of(n * tile, tile), tile)
                 left = att[pl.ds(pl.multiple_of(z * rows, rows), rows), :]
                 found = dot(left, weight_v[:, lanes]).astype(bf16)
-                for h in range(2):
-                    total.acc[0, turn, h, :, lanes] = found[h * half : (h + 1) * half, :]
+                total.acc[0, turn, :, lanes] = found
                 return carry
 
             lax.fori_loop(0, width // tile, body, 0)
@@ -1141,38 +1242,38 @@
         outs = ReduceItem(
             "all",
             place,
-            lambda c, z, h: part_ref.at[c * length + z, pl.ds(h * half, half)],
+            lambda c, z, h: part_ref.at[c * length + z, piece(2 * half, h)],
             o_bufs,
-            lambda h: out_moe.at[pl.ds(h * half, half)],
+            lambda h: out_moe.at[piece(2 * half, h)],
         )
         back = ReduceItem(
             "z",
             place,
-            lambda c, z, h: grads.at[z, pl.ds(h * half, half)],
+            lambda c, z, h: grads.at[z, piece(2 * half, h)],
             z_bufs,
-            lambda h: out_rows.at[pl.ds(h * half, half)],
+            lambda h: out_rows.at[piece(2 * half, h)],
         )
         joints = ReduceItem(
             "dp",
             place,
-            lambda c, z, h: joint_v.at[c, pl.ds(h * deep, deep)],
+            lambda c, z, h: joint_v.at[c, piece(2 * deep, h)],
             j_bufs,
-            lambda h: out_joint.at[pl.ds(h * deep, deep)],
+            lambda h: out_joint.at[piece(2 * deep, h)],
         )
         weights = ReduceItem(
             "dp",
             place,
             lambda c, z, h: part_w.at[
-                pl.ds(h * tall, tall), pl.ds(pl.multiple_of(c * part, part), part)
+                piece(2 * tall, h), pl.ds(pl.multiple_of(c * part, part), part)
             ],
             w_bufs,
-            lambda h: out_weight.at[pl.ds(h * tall, tall)],
+            lambda h: out_weight.at[piece(2 * tall, h)],
         )
         for item in (back, joints, weights):
             item.in_place = True
         gathers = GatherItem("z", place, None, None, *gather_sems)
-        gathers.own = lambda h: grad_ref.at[pl.ds(h * half, half)]
-        gathers.slot = lambda c, z, h: grads.at[z, pl.ds(h * half, half)]
+        gathers.own = lambda h: grad_ref.at[piece(2 * half, h)]
+        gathers.slot = lambda c, z, h: grads.at[z, piece(2 * half, h)]
 
         outs.begin()
         back.begin()
@@ -1350,6 +1451,53 @@
     )(grad_own, rows_all, joint_all, output_all, qkv_all, heads_all, part_out, seg_col, seg_row, cosine, sine, query_gain, key_gain)
 
 
+def share_sum(values, length, collective_id):
+    devices = 8 * length
+    rows, width = values.shape
+
+    def kernel(own, target, land, sem):
+        place = Place(length)
+        me = place.dp * length + place.z
+        meet_all(place)
+
+        def send(n, carry):
+            device, _ = other_device(place, n + 1)
+            pltpu.make_async_remote_copy(
+                src_ref=own,
+                dst_ref=land.at[me],
+                send_sem=sem.at[0],
+                recv_sem=sem.at[1],
+                device_id=device,
+                device_id_type=MESH,
+            ).start()
+            return carry
+
+        lax.fori_loop(0, devices - 1, send, 0)
+        pltpu.make_async_copy(own, land.at[me], sem.at[1]).start()
+        pltpu.make_async_copy(land, land, sem.at[1]).wait()
+        sent = land.at[pl.ds(0, devices - 1)]
+        pltpu.make_async_copy(sent, sent, sem.at[0]).wait()
+
+        def add(n, total):
+            return total + land[n]
+
+        target[...] = lax.fori_loop(1, devices, add, land[0])
+
+    vmem = pl.BlockSpec(memory_space=pltpu.VMEM)
+    return pl.pallas_call(
+        kernel,
+        name="share_sum",
+        out_shape=jax.ShapeDtypeStruct((rows, width), values.dtype),
+        in_specs=[vmem],
+        out_specs=vmem,
+        scratch_shapes=[
+            pltpu.VMEM((devices, rows, width), values.dtype),
+            pltpu.SemaphoreType.DMA((2,)),
+        ],
+        compiler_params=pltpu.CompilerParams(collective_id=collective_id, has_side_effects=True),
+    )(values)
+
+
 def mix(form, left, right):
     return jnp.einsum(form, left, right, preferred_element_type=jnp.float32)
 
@@ -1798,10 +1946,10 @@
     gates = picked / total
     named = jnp.sum(route_hot, axis=1)
     gate_table = jnp.where(named > 0.5, jnp.sum(route_hot * gates[:, :, None], axis=1), -1.0)
-    all_rows, partial_out, partial_rows, token_grads, grad_wg, grad_wu, grad_wd = experts(
+    all_rows, partial_out, partial_rows, token_grads, *units = experts(
         rows_two,
         all_cots,
-        gate_table.T,
+        jnp.broadcast_to(gate_table.T[:, None, :], (expert_count, 8, rows_dev)),
         gate_weight[0],
         up_weight[0],
         down_weight[0],
@@ -1817,7 +1965,13 @@
     grad_logits = (
         router_probs * (grad_probs - jnp.sum(grad_probs * router_probs, axis=-1, keepdims=True))
     ).astype(jnp.bfloat16)
-    grad_sum, all_logits = reduce_rows(partial_rows, grad_logits.T, length, 2)
+    grad_sum, all_logits, grad_wg, grad_wu, grad_wd = reduce_rows(
+        partial_rows,
+        grad_logits.T,
+        *[unit.reshape(-1, unit.shape[-1]) for unit in units],
+        length,
+        2,
+    )
     grad_router = mix("btd,bet->de", all_rows, all_logits)
     grad_rows_two = grad_sum + jnp.dot(grad_logits, router.T, preferred_element_type=jnp.float32)
     grad_res_norm, grad_gain_moe = row_norm_back(grad_rows_two, normed_two, factor_two, gain_moe)
@@ -1839,9 +1993,8 @@
     grad_in_norm, grad_gain_attn = row_norm_back(grad_rows_one, normed_one, factor_one, gain_attn)
     grad_input = grad_residual + grad_in_norm
     small = jnp.concatenate([grad_gain_attn, grad_gain_moe, grad_qgain[0], grad_kgain[0]]).reshape(-1, 128)
-    small = jnp.pad(small, ((0, -small.shape[0] % 16), (0, 0)))
-    (all_small,) = gather([(small, "all", False)], length, 4, "gather_small")
-    sums = jnp.sum(all_small, axis=0).reshape(-1)
+    small = jnp.pad(small, ((0, -small.shape[0] % 8), (0, 0)))
+    sums = share_sum(small, length, 4).reshape(-1)
     head_dim = query_gain.shape[0]
     return (
         output,

time: 639 us -> 601 us (0.941)
  Pallas kernels: 581 us -> 546 us
    pallas_call x1, Pallas kernels: 188 us -> 152 us  [experts(): pl.pallas_call(kernel, name='experts', out_shape=[shape(big, bf16), shape...]
    unnamed x50 -> x54, local copies, waits for them, and re-layouts: 16 us -> 14.9 us
where the time goes in v4:
time: 601 us
  Pallas kernels  546 us (91%)
  local copies, waits for them, and re-layouts  23 us (4%)
  other arithmetic  19.3 us (3%)
  matrix products  12 us (2%)
    pallas_call x1, Pallas kernels, experts(): pl.pallas_call(kernel, name='experts', out_shape=[shape(big, bf16), shape...  152 us
    pallas_call x1, Pallas kernels, attend_back(): pl.pallas_call(kernel, name='attend_back', out_shape=[shape((rows, width)...  147 us
    pallas_call x1, Pallas kernels, attend(): pl.pallas_call(kernel, name='attend', out_shape=[shape((rows, width), f32...  131 us
    pallas_call x1, Pallas kernels, reduce_rows(): pl.pallas_call(kernel, name='reduce_rows', out_shape=[shape((rows, width)...  94.5 us
    pallas_call x1, Pallas kernels, share_sum(): pl.pallas_call(kernel, name='share_sum', out_shape=jax.ShapeDtypeStruct((...  21.9 us
    unnamed x54, local copies, waits for them, and re-layouts  14.9 us

profile of v4, /device:TPU:0, one launch (start us, length us, event | category | flops | bytes accessed | tf_op | source)
XLA Modules:
  0.0 600.9 jit_solution(15886656179503332280)
XLA Ops:
  0.6 0.0 copy-start.2
  0.7 1.3 fusion.10
  2.0 0.0 copy-start.17
  2.0 1.0 convert_reduce_fusion
  3.0 1.5 copy.38.segc
  4.5 0.0 copy-done.17
  4.5 2.0 fusion.4.rows_ref
  6.6 2.0 pad_maximum_fusion.joint_ref
  8.6 1.0 fusion.11
  9.6 1.0 pad_maximum_fusion.1
  10.6 130.7 %attend.1 = (f32[128,2048]{1,0:T(8,128)}, bf16[4,128,2048]{2,1,0:T(8,128)(2,1)}, bf16[8,256,1280]{2,1,0:T(8,128)(2,1)}, bf16[1024,2048]{1,0:T(8,128)(2,1)}, bf16...) custom-call(bf16[128,2048]{1,0:T(8,128)(2,1)} %fusion.4.rows_ref, ...), custom_call_target="tpu_custom_call" | custom-call | tf_op jit(solution)/shard_map/attend/pallas_call | solution.py:1184
  141.4 0.0 copy-done.2
  141.4 1.4 multiply_reduce_fusion.2
  142.8 1.0 copy-done
  143.8 0.5 copy-done.15
  144.3 0.0 copy-done.10
  144.3 0.2 multiply_convert_fusion.rows_ref
  144.5 0.0 copy-done.8
  144.5 0.0 copy-start.4
  144.5 0.3 fusion.16
  144.8 0.0 copy-done.13
  144.8 0.1 select_reduce_fusion
  144.9 0.7 broadcast_in_dim.19.gates_ref
  145.6 0.0 copy-done.4
  145.6 151.7 %experts.1 = (bf16[32,128,2048]{2,1,0:T(8,128)(2,1)}, bf16[32,128,2048]{2,1,0:T(8,128)(2,1)}, bf16[32,128,2048]{2,1,0:T(8,128)(2,1)}, f32[32,8,128]{2,1,0:T(8,12...) custom-call(bf16[128,2048]{1,0:T(8,128)(2,1)} %copy-done.4, ...), custom_call_target="tpu_custom_call" | custom-call | tf_op jit(solution)/shard_map/experts/pallas_call | solution.py:976
  297.3 0.9 slice.36
  298.4 0.6 multiply_convert_fusion.1
  299.0 94.5 %reduce_rows.1 = (f32[128,2048]{1,0:T(8,128)}, bf16[32,32,128]{2,1,0:T(8,128)(2,1)}, f32[2048,768]{1,0:T(8,128)}, f32[2048,768]{1,0:T(8,128)}, f32[768,2048]{1,0:T(8,128)}) custom-call(bf16[32,128,2048]{2,1,0:T(8,128)(2,1)} %get-tuple-element.43.source, bf16[32,128]{1,0:T(8,128)(2,1)} %bitcast.56, bf16[2048,2048]{1,0:T(8,128)(2,1)} %bitcast.41, ...), custom_call_target="tpu_custom_call" | custom-call | tf_op jit(solution)/shard_map/reduce_rows/pallas_call | solution.py:652
  393.5 0.0 copy-start.1
  393.5 0.0 copy-start.7
  393.5 0.0 copy-start.9
  393.5 0.0 copy-start.11
  393.5 0.0 copy-start.12
  393.6 0.0 copy-start.16
  393.6 0.0 copy-start.3
  393.6 9.7 %convolution_bitcast_fusion = f32[2048,32]{0,1:T(8,128)} fusion(bf16[32,32,128]{2,1,0:T(8,128)(2,1)} %get-tuple-element.64, bf16[32,128,2048]{2,1,0:T(8,128)(2,1)} %get-tuple-element.63), kind=kOutput, calls=%fused_computation.1 | convolution fusion | flops 536870912 | bytes 17301504 | tf_op jit(solution)/shard_map/btd,bet->de/dot_general | solution.py:1502
  403.3 0.0 copy-done.1
  403.3 0.0 copy-done.7
  403.3 0.0 copy-done.9
  403.3 0.0 copy-done.11
  403.3 0.0 copy-done.12
  403.3 0.0 copy-done.16
  403.3 2.0 multiply_reduce_fusion
  405.4 0.5 copy-done.18
  405.9 0.0 copy-done.3
  405.9 2.4 fusion.14.grad_ref
  408.2 146.8 %attend_back.1 = (f32[128,2048]{1,0:T(8,128)}, f32[256,1280]{1,0:T(8,128)}, f32[1024,256]{1,0:T(8,128)}, f32[128,2048]{1,0:T(8,128)}, f32[1,128]{1,0:T(1,128)}, /*index=5*/f32[1,128]{1,0:T(1,128)}) custom-call(bf16[128,2048]{1,0:T(8,128)(2,1)} %fusion.14.grad_ref, bf16[4,128,2048]{2,1,0:T(8,128)(2,1)} %get-tuple-element.51.rows_ref, ...), custom_call_target="tpu_custom_call" | custom-call | tf_op jit(solution)/shard_map/attend_back/pallas_call | solution.py:1415
  555.0 0.0 copy-start.14
  555.0 1.9 fusion.9
  557.0 4.2 fusion.8
  561.1 0.0 copy-done.14
  561.1 0.0 copy-done.20
  561.2 0.6 pad.4.own
  561.8 21.9 %share_sum.1 = f32[40,128]{1,0:T(8,128)} custom-call(f32[40,128]{1,0:T(8,128)} %pad.4.own), custom_call_target="tpu_custom_call" | custom-call | tf_op jit(solution)/shard_map/share_sum/pallas_call | solution.py:1487
  583.7 1.3 slice_bitcast_fusion.2
  584.9 1.3 slice_bitcast_fusion
  586.2 0.7 fusion.15
  587.0 1.1 slice.37
  588.1 1.0 copy.44
  589.1 6.1 %copy.45 = f32[1,2048,768]{2,1,0:T(8,128)} copy(f32[1,2048,768]{2,1,0:T(8,128)} %bitcast.49) | data formatting | bytes 12582912
  595.1 0.0 slice-done.3
  595.1 2.8 copy.46
  598.0 0.3 slice-done.1
  598.2 2.7 copy.47
  (38 shorter events, 0.3 us)
Async XLA Ops:
  0.6 140.7 %copy-start.2 = (bf16[128,2048]{1,0:T(8,128)(2,1)S(1)}, bf16[128,2048]{1,0:T(8,128)(2,1)}, u32[]{:S(2)}) copy-start(bf16[128,2048]{1,0:T(8,128)(2,1)} %param.16) | copy-start | bytes 1572868
  1.9 142.4 %copy-start.10 = (f32[2048]{0:T(1024)S(1)}, f32[2048]{0:T(1024)}, u32[]{:S(2)}) copy-start(f32[2048]{0:T(1024)} %param.24) | copy-start | bytes 24580
  2.0 2.6 copy-start.17
  6.6 137.9 %copy-start.8 = (bf16[2048,32]{0,1:T(8,128)(2,1)S(1)}, bf16[2048,32]{0,1:T(8,128)(2,1)}, u32[]{:S(2)}) copy-start(bf16[2048,32]{0,1:T(8,128)(2,1)} %param.27) | copy-start | bytes 393220
  8.6 136.2 %copy-start.13 = (s32[128,8]{0,1:T(8,128)S(1)}, s32[128,8]{0,1:T(8,128)}, u32[]{:S(2)}) copy-start(s32[128,8]{0,1:T(8,128)} %param.18) | copy-start | bytes 12292
  142.8 1.0 copy-start
  143.8 0.5 copy-start.15
  144.5 1.1 copy-start.4
  393.5 9.8 %copy-start.1 = (f32[128,2048]{1,0:T(8,128)S(1)}, f32[128,2048]{1,0:T(8,128)}, u32[]{:S(2)}) copy-start(f32[128,2048]{1,0:T(8,128)} %copy-done) | copy-start | bytes 3145732
  393.5 9.8 %copy-start.7 = (f32[128,2048]{1,0:T(8,128)S(1)}, f32[128,2048]{1,0:T(8,128)}, u32[]{:S(2)}) copy-start(f32[128,2048]{1,0:T(8,128)} %get-tuple-element.50) | copy-start | bytes 3145732
  393.5 9.8 %copy-start.9 = (bf16[2048,32]{0,1:T(8,128)(2,1)S(1)}, bf16[2048,32]{0,1:T(8,128)(2,1)}, u32[]{:S(2)}) copy-start(bf16[2048,32]{0,1:T(8,128)(2,1)} %param.27) | copy-start | bytes 393220
  393.5 9.7 %copy-start.11 = (f32[2048]{0:T(1024)S(1)}, f32[2048]{0:T(1024)}, u32[]{:S(2)}) copy-start(f32[2048]{0:T(1024)} %param.24) | copy-start | bytes 24580
  393.5 9.7 %copy-start.12 = (bf16[128,32]{0,1:T(8,128)(2,1)S(1)}, bf16[128,32]{0,1:T(8,128)(2,1)}, u32[]{:S(2)}) copy-start(bf16[128,32]{0,1:T(8,128)(2,1)} %multiply_convert_fusion.1) | copy-start | bytes 24580
  393.6 9.7 %copy-start.16 = (f32[128]{0:T(128)S(1)}, f32[128]{0:T(128)}, u32[]{:S(2)}) copy-start(f32[128]{0:T(128)} %copy-done.15) | copy-start | bytes 1540
  393.6 12.3 %copy-start.3 = (bf16[128,2048]{1,0:T(8,128)(2,1)S(1)}, bf16[128,2048]{1,0:T(8,128)(2,1)}, u32[]{:S(2)}) copy-start(bf16[128,2048]{1,0:T(8,128)(2,1)} %cots_ref.1) | copy-start | bytes 1572868
  405.3 0.5 copy-start.18
  555.0 6.1 %copy-start.14 = (f32[2048]{0:T(1024)S(1)}, f32[2048]{0:T(1024)}, u32[]{:S(2)}) copy-start(f32[2048]{0:T(1024)} %get-tuple-element.68) | copy-start | bytes 24580
  555.0 6.1 %copy-start.19 = (f32[1,128]{1,0:T(1,128)S(1)}, f32[1,128]{1,0:T(1,128)}, u32[]{:S(2)}) copy-start(f32[1,128]{1,0:T(1,128)} %get-tuple-element.61) | copy-start | bytes 1540
  555.0 6.1 %copy-start.20 = (f32[1,128]{1,0:T(1,128)S(1)}, f32[1,128]{1,0:T(1,128)}, u32[]{:S(2)}) copy-start(f32[1,128]{1,0:T(1,128)} %get-tuple-element.62) | copy-start | bytes 1540
  555.0 31.2 %copy-start.5 = (f32[256,1280]{1,0:T(8,128)S(1)}, f32[256,1280]{1,0:T(8,128)}, u32[]{:S(2)}) copy-start(f32[256,1280]{1,0:T(8,128)} %get-tuple-element.59) | copy-start | bytes 3932164
  555.0 33.0 %copy-start.6 = (f32[1024,256]{1,0:T(8,128)S(1)}, f32[1024,256]{1,0:T(8,128)}, u32[]{:S(2)}) copy-start(f32[1024,256]{1,0:T(8,128)} %get-tuple-element.112) | copy-start | bytes 3145732
  587.0 8.1 %slice-start.2 = ((s8[6291456]{0:T(1024)(128)(4,1)}), s8[4194304]{0:T(1024)(128)(4,1)S(1)}, s32[]{:S(2)}) async-start(s8[6291456]{0:T(1024)(128)(4,1)} %bitcast.46), calls=%async_computation.2 | async-start | bytes 8388608
  589.1 6.1 %slice-start.3 = ((s8[6291456]{0:T(1024)(128)(4,1)}), s8[2097152]{0:T(1024)(128)(4,1)S(1)}, s32[]{:S(2)}) async-start(s8[6291456]{0:T(1024)(128)(4,1)} %bitcast.46), calls=%async_computation.3 | async-start | bytes 4194304
  589.1 8.9 %slice-start = ((s8[6291456]{0:T(1024)(128)(4,1)}), s8[4194304]{0:T(1024)(128)(4,1)S(1)}, s32[]{:S(2)}) async-start(s8[6291456]{0:T(1024)(128)(4,1)} %bitcast.43), calls=%async_computation | async-start | bytes 8388608
  595.1 3.1 slice-start.1

commit v5 on v4

--- a/solution.py
+++ b/solution.py
@@ -510,7 +510,7 @@
     item.home(sends, step - 2 if item.over_dp else step)
 
 
-def reduce_rows(partials, small, picked, gated, hid, dgate, dup, length, collective_id):
+def reduce_rows(partials, small, all_rows, picked, gated, hid, dgate, dup, length, collective_id):
     devices, rows, width = partials.shape
     slots, hidden = dup.shape
     half, low = rows // 2, small.shape[0] // 2
@@ -518,9 +518,9 @@
     f32, bf16 = jnp.float32, jnp.bfloat16
 
     def kernel(
-        source, small_ref, picked_ref, gated_ref, hid_ref, dgate_ref, dup_ref,
-        target, small_all, out_g, out_u, out_d,
-        hid_v, dgate_v, dup_v, picked_v, gated_v, tile_g, tile_u, tile_d, load_sem, tile_sem, store_sem,
+        source, small_ref, all_ref, picked_ref, gated_ref, hid_ref, dgate_ref, dup_ref,
+        target, product, out_g, out_u, out_d,
+        small_all, rows_v, rows_sem, hid_v, dgate_v, dup_v, picked_v, gated_v, tile_g, tile_u, tile_d, load_sem, tile_sem, store_sem,
         *rest,
     ):
         place = Place(length)
@@ -569,6 +569,14 @@
         for copy in tiles(0, 0):
             copy.start()
 
+        def rows_load(group, part):
+            return pltpu.make_async_copy(
+                all_ref.at[pl.ds(group * length, length)], rows_v.at[part], rows_sem.at[part]
+            )
+
+        for part in range(2):
+            rows_load(part, part).start()
+
         def narrow_of(m):
             return pl.ds(pl.multiple_of(m * narrow, narrow), narrow)
 
@@ -580,14 +588,46 @@
                     item.corners(sends, step)
                     item.straight(sends, step, False)
                     item.hand_over(sends, step + 2)
-                    beside.along_z(sends, step + 1)
-                    beside.across(sends, step)
 
                 @pl.when(i == 2 * step + 1)
                 def _(step=step):
                     item.straight(sends, step - 1, True)
                     item.home(sends, step - 2)
-                    beside.diagonal(sends, step)
+
+            for step in range(length + 2):
+
+                @pl.when(i == step)
+                def _(step=step):
+                    beside.along_z(sends, step + 1)
+                    beside.across(sends, step)
+                    beside.diagonal(sends, step - 1)
+
+            @pl.when(i == length + 2)
+            def _():
+                beside.finish()
+                product[...] = jnp.zeros(product.shape, f32)
+
+            @pl.when((i >= length + 2) & (i < length + 6))
+            def _():
+                for part in range(2):
+                    group = 2 * (i - length - 2) + part
+                    rows_load(group, part).wait()
+                    marks = [
+                        small_all[group * length + z] for z in range(length)
+                    ]
+                    left = jnp.concatenate(marks, axis=1)
+
+                    def body(m, carry, part=part, left=left):
+                        lanes = pl.ds(pl.multiple_of(m * tile, tile), tile)
+                        right = rows_v[part, :, :, lanes].reshape(length * rows, tile)
+                        product[:, lanes] += dot(left, right)
+                        return carry
+
+                    lax.fori_loop(0, 4, body, 0)
+
+                    @pl.when(group + 2 < 8)
+                    def _(part=part, group=group):
+                        rows_load(group + 2, part).start()
 
             n, kind = i // 3, i % 3
             slot = n % 2
@@ -639,8 +679,7 @@
 
             return carry
 
-        lax.fori_loop(0, max(12, 2 * (length + 2)), turn_of, 0)
-        beside.finish()
+        lax.fori_loop(0, max(12, 2 * (length + 2), length + 6), turn_of, 0)
         for slot in range(2):
             for copy in stores(slot, slot):
                 copy.wait()
@@ -654,14 +693,17 @@
         name="reduce_rows",
         out_shape=[
             shape((rows, width), f32),
-            shape((devices,) + small.shape, small.dtype),
+            shape((small.shape[0], width), f32),
             shape((width, hidden), f32),
             shape((width, hidden), f32),
             shape((hidden, width), f32),
         ],
-        in_specs=[any_spec] * 7,
-        out_specs=[pl.BlockSpec(memory_space=pltpu.VMEM)] + [any_spec] * 4,
+        in_specs=[any_spec] * 8,
+        out_specs=[pl.BlockSpec(memory_space=pltpu.VMEM)] * 2 + [any_spec] * 3,
         scratch_shapes=[
+            pltpu.VMEM((devices,) + small.shape, small.dtype),
+            pltpu.VMEM((2, length, rows, width), bf16),
+            sems((2,)),
             pltpu.VMEM((slots, hidden), bf16),
             pltpu.VMEM((slots, hidden), bf16),
             pltpu.VMEM((slots, hidden), bf16),
@@ -679,7 +721,7 @@
         compiler_params=pltpu.CompilerParams(
             collective_id=collective_id, has_side_effects=True, vmem_limit_bytes=67043328
         ),
-    )(partials, small, picked, gated, hid, dgate, dup)
+    )(partials, small, all_rows, picked, gated, hid, dgate, dup)
 
 
 def dot(left, right, left_dim=1, right_dim=0):
@@ -762,6 +804,7 @@
             for item in items:
                 item.diagonal(sends, distance)
 
+        across(0)
         along(1)
         pltpu.make_async_copy(table, table, gate_sem.at[1]).wait()
         order = lax.broadcasted_iota(jnp.int32, (rows, rows), 0)
@@ -780,7 +823,6 @@
             return carry
 
         lax.fori_loop(0, devices, choose, 0, unroll=4)
-        across(0)
         for item in items:
             item.settled()
 
@@ -1103,10 +1145,10 @@
         own_weight.across(sends, 0)
         own_joint.diagonal(sends, 0)
         own_rows.along_z(sends, 2)
+        cots.begin(sends)
         own_weight.diagonal(sends, 0)
         for distance in range(3, length):
             own_rows.along_z(sends, distance)
-        cots.begin(sends)
         own_joint.finish()
         own_rows.finish()
 
@@ -1148,8 +1190,8 @@
             return carry
 
         lax.fori_loop(0, heads // 2, one_head, 0)
+        cots.across(sends, 0)
         cots.along_z(sends, 1)
-        cots.across(sends, 0)
         lax.fori_loop(heads // 2, heads, one_head, 0)
         saves[4].start()
         own_weight.finish()
@@ -1170,9 +1212,9 @@
         for turn in range(length):
             outward(turn)
             total.home(sends, turn)
-            cots.along_z(sends, turn + 2)
             cots.diagonal(sends, turn)
             cots.across(sends, turn + 1)
+            cots.along_z(sends, turn + 2)
         cots.finish()
         for copy in saves:
             copy.wait()
@@ -1452,36 +1494,43 @@
 
 
 def share_sum(values, length, collective_id):
-    devices = 8 * length
     rows, width = values.shape
-
-    def kernel(own, target, land, sem):
+    jumps = []
+    while 2 ** len(jumps) < length:
+        jumps.append(2 ** len(jumps))
+    stages = 3 + len(jumps)
+
+    def kernel(own, target, sums, land, send_sem, recv_sem):
         place = Place(length)
-        me = place.dp * length + place.z
-        meet_all(place)
-
-        def send(n, carry):
-            device, _ = other_device(place, n + 1)
-            pltpu.make_async_remote_copy(
-                src_ref=own,
-                dst_ref=land.at[me],
-                send_sem=sem.at[0],
-                recv_sem=sem.at[1],
+        z = place.z
+        partners = [(place.core, z), (place.x, z), (place.y, z)] + [
+            (place.dp, z + jump - 2 * jump * ((z // jump) % 2)) for jump in jumps
+        ]
+        barrier = pltpu.get_barrier_semaphore()
+        for device in partners:
+            pl.semaphore_signal(barrier, 1, device_id=device, device_id_type=MESH)
+        pl.semaphore_wait(barrier, stages)
+        sums[0] = own[...]
+        copies = []
+        for stage, device in enumerate(partners):
+            copy = pltpu.make_async_remote_copy(
+                src_ref=sums.at[stage],
+                dst_ref=land.at[stage],
+                send_sem=send_sem.at[stage],
+                recv_sem=recv_sem.at[stage],
                 device_id=device,
                 device_id_type=MESH,
-            ).start()
-            return carry
-
-        lax.fori_loop(0, devices - 1, send, 0)
-        pltpu.make_async_copy(own, land.at[me], sem.at[1]).start()
-        pltpu.make_async_copy(land, land, sem.at[1]).wait()
-        sent = land.at[pl.ds(0, devices - 1)]
-        pltpu.make_async_copy(sent, sent, sem.at[0]).wait()
-
-        def add(n, total):
-            return total + land[n]
-
-        target[...] = lax.fori_loop(1, devices, add, land[0])
+            )
+            copy.start()
+            copies.append(copy)
+            copy.wait_recv()
+            total = sums[stage] + land[stage]
+            if stage + 1 < stages:
+                sums[stage + 1] = total
+            else:
+                target[...] = total
+        for copy in copies:
+            copy.wait_send()
 
     vmem = pl.BlockSpec(memory_space=pltpu.VMEM)
     return pl.pallas_call(
@@ -1491,8 +1540,10 @@
         in_specs=[vmem],
         out_specs=vmem,
         scratch_shapes=[
-            pltpu.VMEM((devices, rows, width), values.dtype),
-            pltpu.SemaphoreType.DMA((2,)),
+            pltpu.VMEM((stages, rows, width), values.dtype),
+            pltpu.VMEM((stages, rows, width), values.dtype),
+            pltpu.SemaphoreType.DMA((stages,)),
+            pltpu.SemaphoreType.DMA((stages,)),
         ],
         compiler_params=pltpu.CompilerParams(collective_id=collective_id, has_side_effects=True),
     )(values)
@@ -1965,14 +2016,14 @@
     grad_logits = (
         router_probs * (grad_probs - jnp.sum(grad_probs * router_probs, axis=-1, keepdims=True))
     ).astype(jnp.bfloat16)
-    grad_sum, all_logits, grad_wg, grad_wu, grad_wd = reduce_rows(
+    grad_sum, grad_router, grad_wg, grad_wu, grad_wd = reduce_rows(
         partial_rows,
         grad_logits.T,
+        all_rows,
         *[unit.reshape(-1, unit.shape[-1]) for unit in units],
         length,
         2,
     )
-    grad_router = mix("btd,bet->de", all_rows, all_logits)
     grad_rows_two = grad_sum + jnp.dot(grad_logits, router.T, preferred_element_type=jnp.float32)
     grad_res_norm, grad_gain_moe = row_norm_back(grad_rows_two, normed_two, factor_two, gain_moe)
     grad_residual = cot32 + grad_res_norm
@@ -2007,7 +2058,7 @@
         sums[width : 2 * width],
         sums[2 * width : 2 * width + head_dim],
         sums[2 * width + head_dim : 2 * width + 2 * head_dim],
-        grad_router,
+        grad_router.T,
         grad_wg[None],
         grad_wu[None],
         grad_wd[None],

time: 601 us -> 571 us (0.950)
  Pallas kernels: 546 us -> 523 us
  matrix products: 12 us -> 3.16 us
    pallas_call x1, Pallas kernels: 152 us -> 134 us  [experts(): pl.pallas_call(kernel, name='experts', out_shape=[shape(big, bf16), shape...]
    dot_general x1 -> x0, matrix products: 9.69 us -> none  [mix(): return jnp.einsum(form, left, right, preferred_element_type=jnp.float32)]
    pallas_call x1, Pallas kernels: 21.9 us -> 15.8 us  [share_sum(): pl.pallas_call(kernel, name='share_sum', out_shape=jax.ShapeDtypeStruct((...]
    unnamed x54 -> x53, local copies, waits for them, and re-layouts: 14.9 us -> 16.6 us
where the time goes in v5:
time: 571 us; the launch traced here: 570 us
  Pallas kernels  523 us (92%)
  local copies, waits for them, and re-layouts  24.7 us (4%)
  other arithmetic  18 us (3%)
    pallas_call x1, Pallas kernels, attend_back(): pl.pallas_call(kernel, name='attend_back', out_shape=[shape((rows, width)...  147 us
    pallas_call x1, Pallas kernels, experts(): pl.pallas_call(kernel, name='experts', out_shape=[shape(big, bf16), shape...  134 us
    pallas_call x1, Pallas kernels, attend(): pl.pallas_call(kernel, name='attend', out_shape=[shape((rows, width), f32...  129 us
    pallas_call x1, Pallas kernels, reduce_rows(): pl.pallas_call(kernel, name='reduce_rows', out_shape=[shape((rows, width)...  97.6 us
    unnamed x53, local copies, waits for them, and re-layouts  16.6 us
    pallas_call x1, Pallas kernels, share_sum(): pl.pallas_call(kernel, name='share_sum', out_shape=jax.ShapeDtypeStruct((...  15.8 us

profile of v5, /device:TPU:0, one launch (start us, length us, event | category | flops | bytes accessed | tf_op | source)
XLA Modules:
  0.0 570.2 jit_solution(8361489530444909565)
XLA Ops:
  0.6 1.2 fusion.10
  1.9 1.0 convert_reduce_fusion
  2.9 1.5 copy.38.segc
  4.5 2.0 fusion.4.rows_ref
  6.5 2.1 pad_maximum_fusion.joint_ref
  8.5 1.0 fusion.11
  9.5 1.0 pad_maximum_fusion.1
  10.5 128.5 %attend.1 = (f32[128,2048]{1,0:T(8,128)}, bf16[4,128,2048]{2,1,0:T(8,128)(2,1)}, bf16[8,256,1280]{2,1,0:T(8,128)(2,1)}, bf16[1024,2048]{1,0:T(8,128)(2,1)}, bf16...) custom-call(bf16[128,2048]{1,0:T(8,128)(2,1)} %fusion.4.rows_ref, ...), custom_call_target="tpu_custom_call" | custom-call | tf_op jit(solution)/shard_map/attend/pallas_call | solution.py:1226
  139.1 0.0 copy-done.16
  139.1 0.0 copy-start.12
  139.1 0.0 copy-done.2
  139.1 1.4 multiply_reduce_fusion.2
  140.6 1.0 copy-done
  141.5 0.5 copy-done.14
  142.0 0.0 copy-done.10
  142.0 0.2 multiply_convert_fusion.rows_ref
  142.2 0.0 copy-done.8
  142.2 0.0 copy-start.5
  142.2 0.3 fusion.16
  142.6 0.0 copy-done.12
  142.6 0.1 select_reduce_fusion
  142.7 0.7 broadcast_in_dim.19.gates_ref
  143.3 0.0 copy-done.5
  143.3 134.4 %experts.1 = (bf16[32,128,2048]{2,1,0:T(8,128)(2,1)}, bf16[32,128,2048]{2,1,0:T(8,128)(2,1)}, bf16[32,128,2048]{2,1,0:T(8,128)(2,1)}, f32[32,8,128]{2,1,0:T(8,12...) custom-call(bf16[128,2048]{1,0:T(8,128)(2,1)} %copy-done.5, ...), custom_call_target="tpu_custom_call" | custom-call | tf_op jit(solution)/shard_map/experts/pallas_call | solution.py:1018
  277.8 0.9 slice.36
  278.8 0.6 multiply_convert_fusion.1
  279.4 97.6 %reduce_rows.1 = (f32[128,2048]{1,0:T(8,128)}, f32[32,2048]{1,0:T(8,128)}, f32[2048,768]{1,0:T(8,128)}, f32[2048,768]{1,0:T(8,128)}, f32[768,2048]{1,0:T(8,128)}) custom-call(bf16[32,128,2048]{2,1,0:T(8,128)(2,1)} %get-tuple-element.43.source, bf16[32,128]{1,0:T(8,128)(2,1)} %bitcast.54, bf16[32,128,2048]{2,1,0:T(8,128)(2,1)} %get-tuple-element.45.all_ref, ...), custom_call_target="tpu_custom_call" | custom-call | tf_op jit(solution)/shard_map/reduce_rows/pallas_call | solution.py:691
  377.1 0.0 copy-start.1
  377.1 0.0 copy-start.4
  377.1 0.0 copy-start.11
  377.1 0.0 copy-start.15
  377.2 2.9 multiply_reduce_fusion
  380.0 1.0 copy-done.3
  381.0 0.5 copy-done.17
  381.5 0.0 copy-done.1
  381.5 0.0 copy-done.4
  381.5 0.0 copy-done.11
  381.5 0.0 copy-done.15
  381.5 1.1 fusion.14.grad_ref
  382.6 147.0 %attend_back.1 = (f32[128,2048]{1,0:T(8,128)}, f32[256,1280]{1,0:T(8,128)}, f32[1024,256]{1,0:T(8,128)}, f32[128,2048]{1,0:T(8,128)}, f32[1,128]{1,0:T(1,128)}, /*index=5*/f32[1,128]{1,0:T(1,128)}) custom-call(bf16[128,2048]{1,0:T(8,128)(2,1)} %fusion.14.grad_ref, bf16[4,128,2048]{2,1,0:T(8,128)(2,1)} %get-tuple-element.52.rows_ref, ...), custom_call_target="tpu_custom_call" | custom-call | tf_op jit(solution)/shard_map/attend_back/pallas_call | solution.py:1457
  529.7 1.8 fusion.9
  531.4 0.0 copy-start.13
  531.5 0.0 copy-start.18
  531.5 0.0 copy-start.19
  531.5 0.0 copy-start.6
  531.5 0.0 copy-start.7
  531.5 4.3 fusion.8
  535.8 0.0 copy-done.13
  535.8 0.0 copy-done.18
  535.8 0.6 pad.4.own
  536.4 15.8 %share_sum.1 = f32[40,128]{1,0:T(8,128)} custom-call(f32[40,128]{1,0:T(8,128)} %pad.4.own), custom_call_target="tpu_custom_call" | custom-call | tf_op jit(solution)/shard_map/share_sum/pallas_call | solution.py:1536
  552.3 1.3 slice_bitcast_fusion.2
  553.5 1.3 slice_bitcast_fusion
  554.9 0.7 fusion.15
  555.6 1.1 slice.37
  556.7 0.0 copy-done.7
  556.7 1.0 copy.45
  557.7 0.0 copy-done.9
  557.7 0.7 copy.46
  558.4 6.1 %copy.47 = f32[1,2048,768]{2,1,0:T(8,128)} copy(f32[1,2048,768]{2,1,0:T(8,128)} %bitcast.46) | data formatting | bytes 12582912
  564.4 0.0 slice-done.3
  564.4 2.8 copy.48
  567.3 0.3 slice-done.1
  567.5 2.7 copy.49
  (36 shorter events, 0.3 us)
Async XLA Ops:
  1.9 137.2 %copy-start.16 = (f32[128]{0:T(128)}, f32[128]{0:T(128)S(1)}, u32[]{:S(2)}) copy-start(f32[128]{0:T(128)S(1)} %add_rsqrt_fusion.1) | copy-start | bytes 1540
  6.5 132.6 %copy-start.2 = (bf16[128,2048]{1,0:T(8,128)(2,1)S(1)}, bf16[128,2048]{1,0:T(8,128)(2,1)}, u32[]{:S(2)}) copy-start(bf16[128,2048]{1,0:T(8,128)(2,1)} %param.16) | copy-start | bytes 1572868
  10.5 131.5 %copy-start.10 = (f32[2048]{0:T(1024)S(1)}, f32[2048]{0:T(1024)}, u32[]{:S(2)}) copy-start(f32[2048]{0:T(1024)} %param.24) | copy-start | bytes 24580
  10.5 131.7 %copy-start.8 = (bf16[2048,32]{0,1:T(8,128)(2,1)S(1)}, bf16[2048,32]{0,1:T(8,128)(2,1)}, u32[]{:S(2)}) copy-start(bf16[2048,32]{0,1:T(8,128)(2,1)} %param.27) | copy-start | bytes 393220
  139.1 3.5 copy-start.12
  140.5 1.0 copy-start
  141.5 0.5 copy-start.14
  142.2 1.1 copy-start.5
  377.1 4.4 copy-start.1
  377.1 4.4 copy-start.4
  377.1 4.4 copy-start.11
  377.1 4.4 copy-start.15
  380.0 1.0 copy-start.3
  381.0 0.5 copy-start.17
  531.4 4.3 copy-start.13
  531.5 4.3 copy-start.18
  531.5 4.3 copy-start.19
  531.5 23.4 %copy-start.6 = (f32[256,1280]{1,0:T(8,128)S(1)}, f32[256,1280]{1,0:T(8,128)}, u32[]{:S(2)}) copy-start(f32[256,1280]{1,0:T(8,128)} %get-tuple-element.60) | copy-start | bytes 3932164
  531.5 25.2 %copy-start.7 = (f32[1024,256]{1,0:T(8,128)S(1)}, f32[1024,256]{1,0:T(8,128)}, u32[]{:S(2)}) copy-start(f32[1024,256]{1,0:T(8,128)} %get-tuple-element.112) | copy-start | bytes 3145732
  535.8 21.9 %copy-start.9 = (f32[32,2048]{1,0:T(8,128)S(1)}, f32[32,2048]{1,0:T(8,128)}, u32[]{:S(2)}) copy-start(f32[32,2048]{1,0:T(8,128)} %get-tuple-element.64) | copy-start | bytes 786436
  555.6 8.9 %slice-start.2 = ((s8[6291456]{0:T(1024)(128)(4,1)}), s8[4194304]{0:T(1024)(128)(4,1)S(1)}, s32[]{:S(2)}) async-start(s8[6291456]{0:T(1024)(128)(4,1)} %bitcast.43), calls=%async_computation.2 | async-start | bytes 8388608
  558.4 6.1 %slice-start.3 = ((s8[6291456]{0:T(1024)(128)(4,1)}), s8[2097152]{0:T(1024)(128)(4,1)S(1)}, s32[]{:S(2)}) async-start(s8[6291456]{0:T(1024)(128)(4,1)} %bitcast.43), calls=%async_computation.3 | async-start | bytes 4194304
  558.4 8.9 %slice-start = ((s8[6291456]{0:T(1024)(128)(4,1)}), s8[4194304]{0:T(1024)(128)(4,1)S(1)}, s32[]{:S(2)}) async-start(s8[6291456]{0:T(1024)(128)(4,1)} %bitcast.40), calls=%async_computation | async-start | bytes 8388608
  564.4 3.1 slice-start.1

commit v6 on v5

--- a/solution.py
+++ b/solution.py
@@ -580,6 +580,51 @@
         def narrow_of(m):
             return pl.ds(pl.multiple_of(m * narrow, narrow), narrow)
 
+        def chunk(c, carry):
+            n, kind = c // 3, c % 3
+            slot = n % 2
+
+            @pl.when((kind == 0) & (n < 4))
+            def _():
+                for copy in tiles(n, slot):
+                    copy.wait()
+
+                @pl.when(n < 3)
+                def _():
+                    for copy in tiles(n + 1, 1 - slot):
+                        copy.start()
+
+                @pl.when(n >= 2)
+                def _():
+                    for copy in stores(n, slot):
+                        copy.wait()
+
+                def body(m, carry):
+                    tile_g[slot, :, narrow_of(m)] = dot(picked_v[slot], dgate_v[:, narrow_of(m)], 0, 0)
+                    return carry
+
+                lax.fori_loop(0, 3, body, 0)
+                stores(n, slot)[0].start()
+
+            @pl.when((kind == 1) & (n < 4))
+            def _():
+                def body(m, carry):
+                    tile_u[slot, :, narrow_of(m)] = dot(picked_v[slot], dup_v[:, narrow_of(m)], 0, 0)
+                    return carry
+
+                lax.fori_loop(0, 3, body, 0)
+                stores(n, slot)[1].start()
+
+            @pl.when((kind == 2) & (n < 4))
+            def _():
+                def body(m, carry):
+                    tile_d[slot, narrow_of(m), :] = dot(hid_v[:, narrow_of(m)], gated_v[slot], 0, 0)
+                    return carry
+
+                lax.fori_loop(0, 3, body, 0)
+                stores(n, slot)[2].start()
+            return carry
+
         def turn_of(i, carry):
             for step in range(length + 2):
 
@@ -629,53 +674,14 @@
                     def _(part=part, group=group):
                         rows_load(group + 2, part).start()
 
-            n, kind = i // 3, i % 3
-            slot = n % 2
-
             @pl.when(i == 0)
             def _():
                 for copy in resident:
                     copy.wait()
 
-            @pl.when((kind == 0) & (n < 4))
+            @pl.when(i < 6)
             def _():
-                for copy in tiles(n, slot):
-                    copy.wait()
-
-                @pl.when(n < 3)
-                def _():
-                    for copy in tiles(n + 1, 1 - slot):
-                        copy.start()
-
-                @pl.when(n >= 2)
-                def _():
-                    for copy in stores(n, slot):
-                        copy.wait()
-
-                def body(m, carry):
-                    tile_g[slot, :, narrow_of(m)] = dot(picked_v[slot], dgate_v[:, narrow_of(m)], 0, 0)
-                    return carry
-
-                lax.fori_loop(0, 3, body, 0)
-                stores(n, slot)[0].start()
-
-            @pl.when((kind == 1) & (n < 4))
-            def _():
-                def body(m, carry):
-                    tile_u[slot, :, narrow_of(m)] = dot(picked_v[slot], dup_v[:, narrow_of(m)], 0, 0)
-                    return carry
-
-                lax.fori_loop(0, 3, body, 0)
-                stores(n, slot)[1].start()
-
-            @pl.when((kind == 2) & (n < 4))
-            def _():
-                def body(m, carry):
-                    tile_d[slot, narrow_of(m), :] = dot(hid_v[:, narrow_of(m)], gated_v[slot], 0, 0)
-                    return carry
-
-                lax.fori_loop(0, 3, body, 0)
-                stores(n, slot)[2].start()
+                lax.fori_loop(0, 2, lambda part, carry: chunk(2 * i + part, carry), 0)
 
             return carry
 
@@ -1420,8 +1426,6 @@
         out_kgain[...] = gain_part
         joint_b[:, head_width : head_width + head] = found.astype(bf16)
         joint_b[:, head_width + head : head_width + 2 * head] = dvalue[...].astype(bf16)
-        advance(outs, sends, length)
-        advance(weights, sends, 2)
         loads[3].wait()
 
         def to_rows(n, carry):
@@ -1442,12 +1446,15 @@
 
         lax.fori_loop(0, 8, to_joint, 0)
         joints.hand_over(sends, 0)
+        advance(outs, sends, length)
+        advance(joints, sends, 0)
         back.home(sends, 1)
-        advance(joints, sends, 0)
-        for turn in range(2, length):
+        advance(weights, sends, 2)
+        for turn in range(2, length - 1):
             back.home(sends, turn)
         advance(joints, sends, 1)
         advance(outs, sends, length + 1)
+        back.home(sends, length - 1)
         advance(joints, sends, 2)
         sends.drain()
 

time: 571 us -> 550 us (0.963)
  Pallas kernels: 523 us -> 503 us
    pallas_call x1, Pallas kernels: 147 us -> 128 us  [attend_back(): pl.pallas_call(kernel, name='attend_back', out_shape=[shape((rows, width)...]
where the time goes in v6:
time: 550 us
  Pallas kernels  503 us (91%)
  local copies, waits for them, and re-layouts  24.7 us (4%)
  other arithmetic  18 us (3%)
    pallas_call x1, Pallas kernels, experts(): pl.pallas_call(kernel, name='experts', out_shape=[shape(big, bf16), shape...  134 us
    pallas_call x1, Pallas kernels, attend(): pl.pallas_call(kernel, name='attend', out_shape=[shape((rows, width), f32...  129 us
    pallas_call x1, Pallas kernels, attend_back(): pl.pallas_call(kernel, name='attend_back', out_shape=[shape((rows, width)...  128 us
    pallas_call x1, Pallas kernels, reduce_rows(): pl.pallas_call(kernel, name='reduce_rows', out_shape=[shape((rows, width)...  98.7 us
    unnamed x53, local copies, waits for them, and re-layouts  16.6 us
    pallas_call x1, Pallas kernels, share_sum(): pl.pallas_call(kernel, name='share_sum', out_shape=jax.ShapeDtypeStruct((...  13.7 us

profile of v6, /device:TPU:0, one launch (start us, length us, event | category | flops | bytes accessed | tf_op | source)
XLA Modules:
  0.0 549.9 jit_solution(14605990446803245181)
XLA Ops:
  0.6 1.2 fusion.10
  1.9 1.0 convert_reduce_fusion
  2.9 1.5 copy.38.segc
  4.5 2.0 fusion.4.rows_ref
  6.5 2.1 pad_maximum_fusion.joint_ref
  8.5 1.0 fusion.11
  9.5 1.0 pad_maximum_fusion.1
  10.5 128.5 %attend.1 = (f32[128,2048]{1,0:T(8,128)}, bf16[4,128,2048]{2,1,0:T(8,128)(2,1)}, bf16[8,256,1280]{2,1,0:T(8,128)(2,1)}, bf16[1024,2048]{1,0:T(8,128)(2,1)}, bf16...) custom-call(bf16[128,2048]{1,0:T(8,128)(2,1)} %fusion.4.rows_ref, ...), custom_call_target="tpu_custom_call" | custom-call | tf_op jit(solution)/shard_map/attend/pallas_call | solution.py:1232
  139.1 0.0 copy-done.16
  139.1 0.0 copy-start.12
  139.1 0.0 copy-done.2
  139.1 1.4 multiply_reduce_fusion.2
  140.6 1.0 copy-done
  141.5 0.5 copy-done.14
  142.0 0.0 copy-done.10
  142.0 0.2 multiply_convert_fusion.rows_ref
  142.2 0.0 copy-done.8
  142.2 0.0 copy-start.5
  142.2 0.3 fusion.16
  142.6 0.0 copy-done.12
  142.6 0.1 select_reduce_fusion
  142.7 0.7 broadcast_in_dim.19.gates_ref
  143.3 0.0 copy-done.5
  143.3 134.4 %experts.1 = (bf16[32,128,2048]{2,1,0:T(8,128)(2,1)}, bf16[32,128,2048]{2,1,0:T(8,128)(2,1)}, bf16[32,128,2048]{2,1,0:T(8,128)(2,1)}, f32[32,8,128]{2,1,0:T(8,12...) custom-call(bf16[128,2048]{1,0:T(8,128)(2,1)} %copy-done.5, ...), custom_call_target="tpu_custom_call" | custom-call | tf_op jit(solution)/shard_map/experts/pallas_call | solution.py:1024
  277.8 0.9 slice.36
  278.8 0.6 multiply_convert_fusion.1
  279.4 98.7 %reduce_rows.1 = (f32[128,2048]{1,0:T(8,128)}, f32[32,2048]{1,0:T(8,128)}, f32[2048,768]{1,0:T(8,128)}, f32[2048,768]{1,0:T(8,128)}, f32[768,2048]{1,0:T(8,128)}) custom-call(bf16[32,128,2048]{2,1,0:T(8,128)(2,1)} %get-tuple-element.43.source, bf16[32,128]{1,0:T(8,128)(2,1)} %bitcast.54, bf16[32,128,2048]{2,1,0:T(8,128)(2,1)} %get-tuple-element.45.all_ref, ...), custom_call_target="tpu_custom_call" | custom-call | tf_op jit(solution)/shard_map/reduce_rows/pallas_call | solution.py:697
  378.2 0.0 copy-start.1
  378.2 0.0 copy-start.4
  378.2 0.0 copy-start.11
  378.2 0.0 copy-start.15
  378.2 2.9 multiply_reduce_fusion
  381.1 1.0 copy-done.3
  382.1 0.5 copy-done.17
  382.6 0.0 copy-done.1
  382.6 0.0 copy-done.4
  382.6 0.0 copy-done.11
  382.6 0.0 copy-done.15
  382.6 1.1 fusion.14.grad_ref
  383.7 127.7 %attend_back.1 = (f32[128,2048]{1,0:T(8,128)}, f32[256,1280]{1,0:T(8,128)}, f32[1024,256]{1,0:T(8,128)}, f32[128,2048]{1,0:T(8,128)}, f32[1,128]{1,0:T(1,128)}, /*index=5*/f32[1,128]{1,0:T(1,128)}) custom-call(bf16[128,2048]{1,0:T(8,128)(2,1)} %fusion.14.grad_ref, bf16[4,128,2048]{2,1,0:T(8,128)(2,1)} %get-tuple-element.52.rows_ref, ...), custom_call_target="tpu_custom_call" | custom-call | tf_op jit(solution)/shard_map/attend_back/pallas_call | solution.py:1464
  511.4 1.8 fusion.9
  513.2 0.0 copy-start.13
  513.2 0.0 copy-start.18
  513.2 0.0 copy-start.19
  513.2 0.0 copy-start.6
  513.2 0.0 copy-start.7
  513.2 4.3 fusion.8
  517.5 0.0 copy-done.13
  517.5 0.0 copy-done.18
  517.6 0.6 pad.4.own
  518.2 13.7 %share_sum.1 = f32[40,128]{1,0:T(8,128)} custom-call(f32[40,128]{1,0:T(8,128)} %pad.4.own), custom_call_target="tpu_custom_call" | custom-call | tf_op jit(solution)/shard_map/share_sum/pallas_call | solution.py:1543
  531.9 1.3 slice_bitcast_fusion.2
  533.2 1.3 slice_bitcast_fusion
  534.5 0.7 fusion.15
  535.2 1.1 slice.37
  536.3 0.0 copy-done.7
  536.3 1.0 copy.45
  537.3 0.0 copy-done.9
  537.3 0.7 copy.46
  538.0 6.1 %copy.47 = f32[1,2048,768]{2,1,0:T(8,128)} copy(f32[1,2048,768]{2,1,0:T(8,128)} %bitcast.46) | data formatting | bytes 12582912
  544.1 0.0 slice-done.3
  544.1 2.8 copy.48
  546.9 0.3 slice-done.1
  547.2 2.7 copy.49
  (36 shorter events, 0.3 us)
Async XLA Ops:
  1.9 137.2 %copy-start.16 = (f32[128]{0:T(128)}, f32[128]{0:T(128)S(1)}, u32[]{:S(2)}) copy-start(f32[128]{0:T(128)S(1)} %add_rsqrt_fusion.1) | copy-start | bytes 1540
  6.5 132.6 %copy-start.2 = (bf16[128,2048]{1,0:T(8,128)(2,1)S(1)}, bf16[128,2048]{1,0:T(8,128)(2,1)}, u32[]{:S(2)}) copy-start(bf16[128,2048]{1,0:T(8,128)(2,1)} %param.16) | copy-start | bytes 1572868
  10.5 131.5 %copy-start.10 = (f32[2048]{0:T(1024)S(1)}, f32[2048]{0:T(1024)}, u32[]{:S(2)}) copy-start(f32[2048]{0:T(1024)} %param.24) | copy-start | bytes 24580
  10.5 131.7 %copy-start.8 = (bf16[2048,32]{0,1:T(8,128)(2,1)S(1)}, bf16[2048,32]{0,1:T(8,128)(2,1)}, u32[]{:S(2)}) copy-start(bf16[2048,32]{0,1:T(8,128)(2,1)} %param.27) | copy-start | bytes 393220
  139.1 3.5 copy-start.12
  140.5 1.0 copy-start
  141.5 0.5 copy-start.14
  142.2 1.1 copy-start.5
  378.2 4.4 copy-start.1
  378.2 4.4 copy-start.4
  378.2 4.4 copy-start.11
  378.2 4.4 copy-start.15
  381.1 1.0 copy-start.3
  382.1 0.5 copy-start.17
  513.2 4.3 copy-start.13
  513.2 4.3 copy-start.18
  513.2 4.3 copy-start.19
  513.2 21.3 %copy-start.6 = (f32[256,1280]{1,0:T(8,128)S(1)}, f32[256,1280]{1,0:T(8,128)}, u32[]{:S(2)}) copy-start(f32[256,1280]{1,0:T(8,128)} %get-tuple-element.60) | copy-start | bytes 3932164
  513.2 23.1 %copy-start.7 = (f32[1024,256]{1,0:T(8,128)S(1)}, f32[1024,256]{1,0:T(8,128)}, u32[]{:S(2)}) copy-start(f32[1024,256]{1,0:T(8,128)} %get-tuple-element.112) | copy-start | bytes 3145732
  517.5 19.8 %copy-start.9 = (f32[32,2048]{1,0:T(8,128)S(1)}, f32[32,2048]{1,0:T(8,128)}, u32[]{:S(2)}) copy-start(f32[32,2048]{1,0:T(8,128)} %get-tuple-element.64) | copy-start | bytes 786436
  535.2 8.9 %slice-start.2 = ((s8[6291456]{0:T(1024)(128)(4,1)}), s8[4194304]{0:T(1024)(128)(4,1)S(1)}, s32[]{:S(2)}) async-start(s8[6291456]{0:T(1024)(128)(4,1)} %bitcast.43), calls=%async_computation.2 | async-start | bytes 8388608
  538.0 6.1 %slice-start.3 = ((s8[6291456]{0:T(1024)(128)(4,1)}), s8[2097152]{0:T(1024)(128)(4,1)S(1)}, s32[]{:S(2)}) async-start(s8[6291456]{0:T(1024)(128)(4,1)} %bitcast.43), calls=%async_computation.3 | async-start | bytes 4194304
  538.0 8.9 %slice-start = ((s8[6291456]{0:T(1024)(128)(4,1)}), s8[4194304]{0:T(1024)(128)(4,1)S(1)}, s32[]{:S(2)}) async-start(s8[6291456]{0:T(1024)(128)(4,1)} %bitcast.40), calls=%async_computation | async-start | bytes 8388608
  544.1 3.1 slice-start.1

commit v7 on v6

--- a/solution.py
+++ b/solution.py
@@ -1085,7 +1085,14 @@
     return (seg_col[start:stop, :] == seg_row[:, 0:reach]) & (key <= query)
 
 
-def attend(rows_own, joint_own, output_own, cots_own, seg_col, seg_row, cosine, sine, query_gain, key_gain, length, collective_id):
+def fill_turns(seg_row, cos_half, sin_half, seg_col, cosine, sine):
+    spread = jnp.broadcast_to(seg_row[...].astype(jnp.float32), (128, seg_row.shape[1]))
+    seg_col[...] = spread.T[:, 0:1].astype(jnp.int32)
+    cosine[...] = jnp.concatenate([cos_half[...], cos_half[...]], axis=1)
+    sine[...] = jnp.concatenate([-sin_half[...], sin_half[...]], axis=1)
+
+
+def attend(rows_own, joint_own, output_own, cots_own, segments, cosine, sine, query_gain, key_gain, length, collective_id):
     rows, width = rows_own.shape
     depth, joint = joint_own.shape
     head_width, part = output_own.shape
@@ -1098,8 +1105,9 @@
     f32, bf16 = jnp.float32, jnp.bfloat16
 
     def kernel(
-        rows_ref, joint_ref, output_ref, cots_ref, segc, segr, cos_ref, sin_ref, qgain, kgain,
+        rows_ref, joint_ref, output_ref, cots_ref, segr, cos_half, sin_half, qgain, kgain,
         out_add, out_rows, out_joint, out_weight, out_cots, out_qkv, out_heads,
+        segc, cos_ref, sin_ref,
         rows_v, joint_v, weight_v, qkv, att, key_v, value_v,
         r0, r1, r2, r3, r4, r5, r6, r7,
         g0, g1, g2, j0, j1, j2, w0, w1, w2, c0, c1, c2, save_sem,
@@ -1146,6 +1154,7 @@
         own_joint.begin(sends)
         own_rows.begin(sends)
         own_weight.begin(sends)
+        fill_turns(segr, cos_half, sin_half, segc, cos_ref, sin_ref)
         own_joint.across(sends, 0)
         own_rows.along_z(sends, 1)
         own_weight.across(sends, 0)
@@ -1240,9 +1249,12 @@
             shape((8 * length, rows, width), bf16),
             shape((tokens, joint), f32),
             shape((tokens, head_width), bf16),
+            shape((tokens, 1), jnp.int32),
+            shape((tokens, head), f32),
+            shape((tokens, head), f32),
         ],
-        in_specs=[any_spec] * 4 + [vmem] * 6,
-        out_specs=[vmem] + [any_spec] * 6,
+        in_specs=[any_spec] * 4 + [vmem] * 5,
+        out_specs=[vmem] + [any_spec] * 6 + [vmem] * 3,
         scratch_shapes=[
             pltpu.VMEM((length, rows, width), bf16),
             pltpu.VMEM((8, depth, joint), bf16),
@@ -1260,7 +1272,7 @@
         compiler_params=pltpu.CompilerParams(
             collective_id=collective_id, has_side_effects=True, vmem_limit_bytes=56 << 20
         ),
-    )(rows_own, joint_own, output_own, cots_own, seg_col, seg_row, cosine, sine, query_gain, key_gain)
+    )(rows_own, joint_own, output_own, cots_own, segments, cosine, sine, query_gain, key_gain)
 
 
 def attend_back(grad_own, rows_all, joint_all, output_all, qkv_all, heads_all, part_out, seg_col, seg_row, cosine, sine, query_gain, key_gain, length, collective_id):
@@ -1502,42 +1514,44 @@
 
 def share_sum(values, length, collective_id):
     rows, width = values.shape
-    jumps = []
-    while 2 ** len(jumps) < length:
-        jumps.append(2 ** len(jumps))
-    stages = 3 + len(jumps)
-
-    def kernel(own, target, sums, land, send_sem, recv_sem):
+
+    def kernel(own, target, middle, group, line, send_sem, recv_sem):
         place = Place(length)
-        z = place.z
-        partners = [(place.core, z), (place.x, z), (place.y, z)] + [
-            (place.dp, z + jump - 2 * jump * ((z // jump) % 2)) for jump in jumps
-        ]
+
+        def dp_peer(n):
+            return lax.rem(place.dp + n, 8), place.z
+
+        def z_peer(n):
+            return place.dp, lax.rem(place.z + n, length)
+
+        peers = [dp_peer(n) for n in range(1, 8)] + [z_peer(n) for n in range(1, length)]
         barrier = pltpu.get_barrier_semaphore()
-        for device in partners:
+        for device in peers:
             pl.semaphore_signal(barrier, 1, device_id=device, device_id_type=MESH)
-        pl.semaphore_wait(barrier, stages)
-        sums[0] = own[...]
-        copies = []
-        for stage, device in enumerate(partners):
-            copy = pltpu.make_async_remote_copy(
-                src_ref=sums.at[stage],
-                dst_ref=land.at[stage],
-                send_sem=send_sem.at[stage],
-                recv_sem=recv_sem.at[stage],
-                device_id=device,
-                device_id_type=MESH,
-            )
-            copy.start()
-            copies.append(copy)
-            copy.wait_recv()
-            total = sums[stage] + land[stage]
-            if stage + 1 < stages:
-                sums[stage + 1] = total
-            else:
-                target[...] = total
-        for copy in copies:
-            copy.wait_send()
+        pl.semaphore_wait(barrier, len(peers))
+
+        def exchange(source, land, mine, devices, at):
+            for device in devices:
+                pltpu.make_async_remote_copy(
+                    src_ref=source,
+                    dst_ref=land.at[mine],
+                    send_sem=send_sem.at[at],
+                    recv_sem=recv_sem.at[at],
+                    device_id=device,
+                    device_id_type=MESH,
+                ).start()
+            pltpu.make_async_copy(source, land.at[mine], recv_sem.at[at]).start()
+            pltpu.make_async_copy(land, land, recv_sem.at[at]).wait()
+            total = land[0]
+            for n in range(1, land.shape[0]):
+                total = total + land[n]
+            return total
+
+        middle[...] = exchange(own, group, place.dp, peers[:7], 0)
+        target[...] = exchange(middle, line, place.z, peers[7:], 1)
+        for at, land in ((0, group), (1, line)):
+            sent = land.at[pl.ds(0, land.shape[0] - 1)]
+            pltpu.make_async_copy(sent, sent, send_sem.at[at]).wait()
 
     vmem = pl.BlockSpec(memory_space=pltpu.VMEM)
     return pl.pallas_call(
@@ -1547,10 +1561,11 @@
         in_specs=[vmem],
         out_specs=vmem,
         scratch_shapes=[
-            pltpu.VMEM((stages, rows, width), values.dtype),
-            pltpu.VMEM((stages, rows, width), values.dtype),
-            pltpu.SemaphoreType.DMA((stages,)),
-            pltpu.SemaphoreType.DMA((stages,)),
+            pltpu.VMEM((rows, width), values.dtype),
+            pltpu.VMEM((8, rows, width), values.dtype),
+            pltpu.VMEM((length, rows, width), values.dtype),
+            pltpu.SemaphoreType.DMA((2,)),
+            pltpu.SemaphoreType.DMA((2,)),
         ],
         compiler_params=pltpu.CompilerParams(collective_id=collective_id, has_side_effects=True),
     )(values)
@@ -1981,14 +1996,13 @@
     joint_weight = jnp.concatenate([query_weight, key_weight, value_weight], axis=1)
     cosine, sine_table = rope_tables(seg_ids, query_gain.shape[0])
     turns = (
-        seg_ids[:, None],
         seg_ids[None, :],
-        jnp.concatenate([cosine, cosine], axis=1),
-        jnp.concatenate([-sine_table, sine_table], axis=1),
+        cosine,
+        sine_table,
         query_gain[None, :],
         key_gain[None, :],
     )
-    attn_add, group_rows, full_joint, full_output, all_cots, projected, attn_heads = attend(
+    attn_add, group_rows, full_joint, full_output, all_cots, projected, attn_heads, *laid = attend(
         rows_one, joint_weight, output_weight, cotangent, *turns, length, 0
     )
     residual = inputs32 + attn_add
@@ -2043,7 +2057,10 @@
         projected,
         attn_heads,
         partial_out,
-        *turns,
+        laid[0],
+        turns[0],
+        *laid[1:],
+        *turns[3:],
         length,
         3,
     )

time: 550 us -> 545 us (level)
  no operation moved by 1% of the time
where the time goes in v7:
time: 545 us
  Pallas kernels  500 us (92%)
  local copies, waits for them, and re-layouts  23.2 us (4%)
  other arithmetic  17.8 us (3%)
    pallas_call x1, Pallas kernels, experts(): pl.pallas_call(kernel, name='experts', out_shape=[shape(big, bf16), shape...  134 us
    pallas_call x1, Pallas kernels, attend(): pl.pallas_call(kernel, name='attend', out_shape=[shape((rows, width), f32...  129 us
    pallas_call x1, Pallas kernels, attend_back(): pl.pallas_call(kernel, name='attend_back', out_shape=[shape((rows, width)...  128 us
    pallas_call x1, Pallas kernels, reduce_rows(): pl.pallas_call(kernel, name='reduce_rows', out_shape=[shape((rows, width)...  98.8 us
    unnamed x53, local copies, waits for them, and re-layouts  16.6 us

profile of v7, /device:TPU:0, one launch (start us, length us, event | category | flops | bytes accessed | tf_op | source)
XLA Modules:
  0.0 544.8 jit_solution(5546390925368199720)
XLA Ops:
  0.6 0.0 copy-start.2
  0.7 1.3 fusion.10
  2.0 1.0 convert_reduce_fusion
  3.0 1.8 multiply_sine_fusion
  4.8 2.0 fusion.4.rows_ref
  6.8 0.0 copy-done.16
  6.8 2.0 pad_maximum_fusion.joint_ref
  8.9 128.7 %attend.1 = (f32[128,2048]{1,0:T(8,128)}, bf16[4,128,2048]{2,1,0:T(8,128)(2,1)}, bf16[8,256,1280]{2,1,0:T(8,128)(2,1)}, bf16[1024,2048]{1,0:T(8,128)(2,1)}, bf16...) custom-call(bf16[128,2048]{1,0:T(8,128)(2,1)} %fusion.4.rows_ref, ...), custom_call_target="tpu_custom_call" | custom-call | tf_op jit(solution)/shard_map/attend/pallas_call | solution.py:1241
  137.6 0.0 copy-start.12
  137.6 0.0 copy-done.2
  137.6 1.4 multiply_reduce_fusion.2
  139.0 1.0 copy-done
  140.0 0.5 copy-done.14
  140.5 0.0 copy-done.10
  140.5 0.2 multiply_convert_fusion.rows_ref
  140.7 0.0 copy-done.8
  140.7 0.0 copy-start.4
  140.7 0.3 fusion.15
  141.0 0.0 copy-done.12
  141.1 0.1 select_reduce_fusion
  141.2 0.7 broadcast_in_dim.19.gates_ref
  141.8 0.0 copy-done.4
  141.8 134.4 %experts.1 = (bf16[32,128,2048]{2,1,0:T(8,128)(2,1)}, bf16[32,128,2048]{2,1,0:T(8,128)(2,1)}, bf16[32,128,2048]{2,1,0:T(8,128)(2,1)}, f32[32,8,128]{2,1,0:T(8,12...) custom-call(bf16[128,2048]{1,0:T(8,128)(2,1)} %copy-done.4, ...), custom_call_target="tpu_custom_call" | custom-call | tf_op jit(solution)/shard_map/experts/pallas_call | solution.py:1024
  276.3 0.9 slice.36
  277.3 0.6 multiply_convert_fusion.1
  277.9 98.8 %reduce_rows.1 = (f32[128,2048]{1,0:T(8,128)}, f32[32,2048]{1,0:T(8,128)}, f32[2048,768]{1,0:T(8,128)}, f32[2048,768]{1,0:T(8,128)}, f32[768,2048]{1,0:T(8,128)}) custom-call(bf16[32,128,2048]{2,1,0:T(8,128)(2,1)} %get-tuple-element.46.source, bf16[32,128]{1,0:T(8,128)(2,1)} %bitcast.53, bf16[32,128,2048]{2,1,0:T(8,128)(2,1)} %get-tuple-element.48.all_ref, ...), custom_call_target="tpu_custom_call" | custom-call | tf_op jit(solution)/shard_map/reduce_rows/pallas_call | solution.py:697
  376.7 0.0 copy-start.1
  376.7 0.0 copy-start.5
  376.7 0.0 copy-start.11
  376.7 0.0 copy-start.15
  376.7 2.9 multiply_reduce_fusion
  379.6 1.0 copy-done.3
  380.6 0.5 copy-done.17
  381.1 0.0 copy-done.1
  381.1 0.0 copy-done.5
  381.1 0.0 copy-done.11
  381.1 0.0 copy-done.15
  381.1 1.1 fusion.13.grad_ref
  382.2 127.5 %attend_back.1 = (f32[128,2048]{1,0:T(8,128)}, f32[256,1280]{1,0:T(8,128)}, f32[1024,256]{1,0:T(8,128)}, f32[128,2048]{1,0:T(8,128)}, f32[1,128]{1,0:T(1,128)}, /*index=5*/f32[1,128]{1,0:T(1,128)}) custom-call(bf16[128,2048]{1,0:T(8,128)(2,1)} %fusion.13.grad_ref, bf16[4,128,2048]{2,1,0:T(8,128)(2,1)} %get-tuple-element.55.rows_ref, ...), custom_call_target="tpu_custom_call" | custom-call | tf_op jit(solution)/shard_map/attend_back/pallas_call | solution.py:1476
  509.8 1.8 fusion.9
  511.5 0.0 copy-start.13
  511.6 0.0 copy-start.18
  511.6 0.0 copy-start.19
  511.6 0.0 copy-start.6
  511.6 0.0 copy-start.7
  511.6 4.3 fusion.8
  515.9 0.0 copy-done.13
  515.9 0.0 copy-done.18
  515.9 0.0 copy-done.19
  515.9 0.6 pad.4.own
  516.5 10.3 %share_sum.1 = f32[40,128]{1,0:T(8,128)} custom-call(f32[40,128]{1,0:T(8,128)} %pad.4.own), custom_call_target="tpu_custom_call" | custom-call | tf_op jit(solution)/shard_map/share_sum/pallas_call | solution.py:1557
  526.8 1.3 slice_bitcast_fusion.2
  528.1 1.3 slice_bitcast_fusion
  529.4 0.0 copy-done.6
  529.4 0.7 fusion.14
  530.1 1.1 slice.37
  531.2 0.0 copy-done.7
  531.2 1.0 copy.38
  532.2 0.7 copy.39
  532.9 6.1 %copy.40 = f32[1,2048,768]{2,1,0:T(8,128)} copy(f32[1,2048,768]{2,1,0:T(8,128)} %bitcast.45) | data formatting | bytes 12582912
  539.0 0.0 slice-done.2
  539.0 2.8 copy.41
  541.8 0.3 slice-done.1
  542.1 2.7 copy.42
  (34 shorter events, 0.3 us)
Async XLA Ops:
  0.6 136.9 %copy-start.2 = (bf16[128,2048]{1,0:T(8,128)(2,1)S(1)}, bf16[128,2048]{1,0:T(8,128)(2,1)}, u32[]{:S(2)}) copy-start(bf16[128,2048]{1,0:T(8,128)(2,1)} %param.16) | copy-start | bytes 1572868
  2.0 4.9 copy-start.16
  6.8 133.7 %copy-start.10 = (f32[2048]{0:T(1024)S(1)}, f32[2048]{0:T(1024)}, u32[]{:S(2)}) copy-start(f32[2048]{0:T(1024)} %param.24) | copy-start | bytes 24580
  8.9 131.8 %copy-start.8 = (bf16[2048,32]{0,1:T(8,128)(2,1)S(1)}, bf16[2048,32]{0,1:T(8,128)(2,1)}, u32[]{:S(2)}) copy-start(bf16[2048,32]{0,1:T(8,128)(2,1)} %param.27) | copy-start | bytes 393220
  137.6 3.5 copy-start.12
  139.0 1.0 copy-start
  140.0 0.5 copy-start.14
  140.7 1.1 copy-start.4
  376.7 4.4 copy-start.1
  376.7 4.4 copy-start.5
  376.7 4.4 copy-start.11
  376.7 4.4 copy-start.15
  379.6 1.0 copy-start.3
  380.6 0.5 copy-start.17
  511.5 4.3 copy-start.13
  511.6 4.3 copy-start.18
  511.6 4.3 copy-start.19
  511.6 17.8 %copy-start.6 = (f32[256,1280]{1,0:T(8,128)S(1)}, f32[256,1280]{1,0:T(8,128)}, u32[]{:S(2)}) copy-start(f32[256,1280]{1,0:T(8,128)} %get-tuple-element.66) | copy-start | bytes 3932164
  511.6 19.6 %copy-start.7 = (f32[1024,256]{1,0:T(8,128)S(1)}, f32[1024,256]{1,0:T(8,128)}, u32[]{:S(2)}) copy-start(f32[1024,256]{1,0:T(8,128)} %get-tuple-element.115) | copy-start | bytes 3145732
  515.9 16.3 %copy-start.9 = (f32[32,2048]{1,0:T(8,128)S(1)}, f32[32,2048]{1,0:T(8,128)}, u32[]{:S(2)}) copy-start(f32[32,2048]{1,0:T(8,128)} %get-tuple-element.70) | copy-start | bytes 786436
  530.1 8.9 %slice-start.2 = ((s8[6291456]{0:T(1024)(128)(4,1)}), s8[4194304]{0:T(1024)(128)(4,1)S(1)}, s32[]{:S(2)}) async-start(s8[6291456]{0:T(1024)(128)(4,1)} %bitcast.42), calls=%async_computation.2 | async-start | bytes 8388608
  532.9 6.1 %slice-start.3 = ((s8[6291456]{0:T(1024)(128)(4,1)}), s8[2097152]{0:T(1024)(128)(4,1)S(1)}, s32[]{:S(2)}) async-start(s8[6291456]{0:T(1024)(128)(4,1)} %bitcast.42), calls=%async_computation.3 | async-start | bytes 4194304
  532.9 8.9 %slice-start = ((s8[6291456]{0:T(1024)(128)(4,1)}), s8[4194304]{0:T(1024)(128)(4,1)S(1)}, s32[]{:S(2)}) async-start(s8[6291456]{0:T(1024)(128)(4,1)} %bitcast.39), calls=%async_computation | async-start | bytes 8388608
  539.0 3.1 slice-start.1

commit v8 on v7

--- a/solution.py
+++ b/solution.py
@@ -538,8 +538,8 @@
         meet(place, True, True)
         sends = Sends(place)
         beside.begin(sends)
+        item.hand_over(sends, 0)
         item.load_all()
-        item.hand_over(sends, 0)
         item.hand_over(sends, 1)
         resident = [
             pltpu.make_async_copy(left, right, load_sem.at[n])
@@ -1340,8 +1340,8 @@
         meet(place, True, True)
         first, sends = Sends(place), Sends(place)
         gathers.begin(first)
+        outs.hand_over(sends, 0)
         outs.load_all()
-        outs.hand_over(sends, 0)
         outs.hand_over(sends, 1)
         loads = [
             pltpu.make_async_copy(source, target, load_sem.at[n])

time: 545 us -> 545 us (level)
  no operation moved by 1% of the time
where the time goes in v8:
time: 545 us
  Pallas kernels  500 us (92%)
  local copies, waits for them, and re-layouts  23.2 us (4%)
  other arithmetic  17.8 us (3%)
    pallas_call x1, Pallas kernels, experts(): pl.pallas_call(kernel, name='experts', out_shape=[shape(big, bf16), shape...  134 us
    pallas_call x1, Pallas kernels, attend(): pl.pallas_call(kernel, name='attend', out_shape=[shape((rows, width), f32...  129 us
    pallas_call x1, Pallas kernels, attend_back(): pl.pallas_call(kernel, name='attend_back', out_shape=[shape((rows, width)...  127 us
    pallas_call x1, Pallas kernels, reduce_rows(): pl.pallas_call(kernel, name='reduce_rows', out_shape=[shape((rows, width)...  98.8 us
    unnamed x53, local copies, waits for them, and re-layouts  16.6 us

profile of v8, /device:TPU:0, one launch (start us, length us, event | category | flops | bytes accessed | tf_op | source)
XLA Modules:
  0.0 544.7 jit_solution(6246128803902226510)
XLA Ops:
  0.6 0.0 copy-start.2
  0.7 1.3 fusion.10
  2.0 1.0 convert_reduce_fusion
  3.0 1.8 multiply_sine_fusion
  4.8 2.0 fusion.4.rows_ref
  6.8 0.0 copy-done.16
  6.8 2.0 pad_maximum_fusion.joint_ref
  8.9 128.7 %attend.1 = (f32[128,2048]{1,0:T(8,128)}, bf16[4,128,2048]{2,1,0:T(8,128)(2,1)}, bf16[8,256,1280]{2,1,0:T(8,128)(2,1)}, bf16[1024,2048]{1,0:T(8,128)(2,1)}, bf16...) custom-call(bf16[128,2048]{1,0:T(8,128)(2,1)} %fusion.4.rows_ref, ...), custom_call_target="tpu_custom_call" | custom-call | tf_op jit(solution)/shard_map/attend/pallas_call | solution.py:1241
  137.6 0.0 copy-start.12
  137.6 0.0 copy-done.2
  137.6 1.4 multiply_reduce_fusion.2
  139.0 1.0 copy-done
  140.0 0.5 copy-done.14
  140.5 0.0 copy-done.10
  140.5 0.2 multiply_convert_fusion.rows_ref
  140.7 0.0 copy-done.8
  140.7 0.0 copy-start.4
  140.7 0.3 fusion.15
  141.0 0.0 copy-done.12
  141.1 0.1 select_reduce_fusion
  141.2 0.7 broadcast_in_dim.19.gates_ref
  141.8 0.0 copy-done.4
  141.8 134.4 %experts.1 = (bf16[32,128,2048]{2,1,0:T(8,128)(2,1)}, bf16[32,128,2048]{2,1,0:T(8,128)(2,1)}, bf16[32,128,2048]{2,1,0:T(8,128)(2,1)}, f32[32,8,128]{2,1,0:T(8,12...) custom-call(bf16[128,2048]{1,0:T(8,128)(2,1)} %copy-done.4, ...), custom_call_target="tpu_custom_call" | custom-call | tf_op jit(solution)/shard_map/experts/pallas_call | solution.py:1024
  276.3 0.9 slice.36
  277.3 0.6 multiply_convert_fusion.1
  277.9 98.8 %reduce_rows.1 = (f32[128,2048]{1,0:T(8,128)}, f32[32,2048]{1,0:T(8,128)}, f32[2048,768]{1,0:T(8,128)}, f32[2048,768]{1,0:T(8,128)}, f32[768,2048]{1,0:T(8,128)}) custom-call(bf16[32,128,2048]{2,1,0:T(8,128)(2,1)} %get-tuple-element.46.source, bf16[32,128]{1,0:T(8,128)(2,1)} %bitcast.53, bf16[32,128,2048]{2,1,0:T(8,128)(2,1)} %get-tuple-element.48.all_ref, ...), custom_call_target="tpu_custom_call" | custom-call | tf_op jit(solution)/shard_map/reduce_rows/pallas_call | solution.py:697
  376.7 0.0 copy-start.1
  376.7 0.0 copy-start.5
  376.8 0.0 copy-start.11
  376.8 0.0 copy-start.15
  376.8 2.9 multiply_reduce_fusion
  379.6 1.0 copy-done.3
  380.6 0.5 copy-done.17
  381.1 0.0 copy-done.1
  381.1 0.0 copy-done.5
  381.1 0.0 copy-done.11
  381.1 0.0 copy-done.15
  381.1 1.1 fusion.13.grad_ref
  382.3 127.4 %attend_back.1 = (f32[128,2048]{1,0:T(8,128)}, f32[256,1280]{1,0:T(8,128)}, f32[1024,256]{1,0:T(8,128)}, f32[128,2048]{1,0:T(8,128)}, f32[1,128]{1,0:T(1,128)}, /*index=5*/f32[1,128]{1,0:T(1,128)}) custom-call(bf16[128,2048]{1,0:T(8,128)(2,1)} %fusion.13.grad_ref, bf16[4,128,2048]{2,1,0:T(8,128)(2,1)} %get-tuple-element.55.rows_ref, ...), custom_call_target="tpu_custom_call" | custom-call | tf_op jit(solution)/shard_map/attend_back/pallas_call | solution.py:1476
  509.7 1.8 fusion.9
  511.4 0.0 copy-start.13
  511.5 0.0 copy-start.18
  511.5 0.0 copy-start.19
  511.5 0.0 copy-start.6
  511.5 0.0 copy-start.7
  511.5 4.3 fusion.8
  515.8 0.0 copy-done.13
  515.8 0.0 copy-done.18
  515.8 0.0 copy-done.19
  515.8 0.6 pad.4.own
  516.4 10.2 %share_sum.1 = f32[40,128]{1,0:T(8,128)} custom-call(f32[40,128]{1,0:T(8,128)} %pad.4.own), custom_call_target="tpu_custom_call" | custom-call | tf_op jit(solution)/shard_map/share_sum/pallas_call | solution.py:1557
  526.7 1.3 slice_bitcast_fusion.2
  528.0 1.3 slice_bitcast_fusion
  529.3 0.0 copy-done.6
  529.3 0.7 fusion.14
  530.0 1.1 slice.37
  531.1 0.0 copy-done.7
  531.1 1.0 copy.38
  532.1 0.7 copy.39
  532.8 6.1 %copy.40 = f32[1,2048,768]{2,1,0:T(8,128)} copy(f32[1,2048,768]{2,1,0:T(8,128)} %bitcast.45) | data formatting | bytes 12582912
  538.8 0.0 slice-done.2
  538.9 2.8 copy.41
  541.7 0.3 slice-done.1
  542.0 2.7 copy.42
  (34 shorter events, 0.3 us)
Async XLA Ops:
  0.6 136.9 %copy-start.2 = (bf16[128,2048]{1,0:T(8,128)(2,1)S(1)}, bf16[128,2048]{1,0:T(8,128)(2,1)}, u32[]{:S(2)}) copy-start(bf16[128,2048]{1,0:T(8,128)(2,1)} %param.16) | copy-start | bytes 1572868
  2.0 4.9 copy-start.16
  6.8 133.7 %copy-start.10 = (f32[2048]{0:T(1024)S(1)}, f32[2048]{0:T(1024)}, u32[]{:S(2)}) copy-start(f32[2048]{0:T(1024)} %param.24) | copy-start | bytes 24580
  8.9 131.8 %copy-start.8 = (bf16[2048,32]{0,1:T(8,128)(2,1)S(1)}, bf16[2048,32]{0,1:T(8,128)(2,1)}, u32[]{:S(2)}) copy-start(bf16[2048,32]{0,1:T(8,128)(2,1)} %param.27) | copy-start | bytes 393220
  137.6 3.5 copy-start.12
  139.0 1.0 copy-start
  140.0 0.5 copy-start.14
  140.7 1.1 copy-start.4
  376.7 4.4 copy-start.1
  376.7 4.4 copy-start.5
  376.8 4.4 copy-start.11
  376.8 4.4 copy-start.15
  379.6 1.0 copy-start.3
  380.6 0.5 copy-start.17
  511.4 4.3 copy-start.13
  511.5 4.3 copy-start.18
  511.5 4.3 copy-start.19
  511.5 17.8 %copy-start.6 = (f32[256,1280]{1,0:T(8,128)S(1)}, f32[256,1280]{1,0:T(8,128)}, u32[]{:S(2)}) copy-start(f32[256,1280]{1,0:T(8,128)} %get-tuple-element.66) | copy-start | bytes 3932164
  511.5 19.6 %copy-start.7 = (f32[1024,256]{1,0:T(8,128)S(1)}, f32[1024,256]{1,0:T(8,128)}, u32[]{:S(2)}) copy-start(f32[1024,256]{1,0:T(8,128)} %get-tuple-element.115) | copy-start | bytes 3145732
  515.8 16.3 %copy-start.9 = (f32[32,2048]{1,0:T(8,128)S(1)}, f32[32,2048]{1,0:T(8,128)}, u32[]{:S(2)}) copy-start(f32[32,2048]{1,0:T(8,128)} %get-tuple-element.70) | copy-start | bytes 786436
  530.0 8.9 %slice-start.2 = ((s8[6291456]{0:T(1024)(128)(4,1)}), s8[4194304]{0:T(1024)(128)(4,1)S(1)}, s32[]{:S(2)}) async-start(s8[6291456]{0:T(1024)(128)(4,1)} %bitcast.42), calls=%async_computation.2 | async-start | bytes 8388608
  532.8 6.1 %slice-start.3 = ((s8[6291456]{0:T(1024)(128)(4,1)}), s8[2097152]{0:T(1024)(128)(4,1)S(1)}, s32[]{:S(2)}) async-start(s8[6291456]{0:T(1024)(128)(4,1)} %bitcast.42), calls=%async_computation.3 | async-start | bytes 4194304
  532.8 8.9 %slice-start = ((s8[6291456]{0:T(1024)(128)(4,1)}), s8[4194304]{0:T(1024)(128)(4,1)S(1)}, s32[]{:S(2)}) async-start(s8[6291456]{0:T(1024)(128)(4,1)} %bitcast.39), calls=%async_computation | async-start | bytes 8388608
  538.8 3.1 slice-start.1
